TPU v7x, 32 devices: a whole 2x2x4 slice. The times are simulated.
32 devices in a mesh: parts: 2 (over y), pix: 4 (over z), par: 4 (over x, core).
Axes of the slice: x: 2, y: 2, z: 4, core: 2. Of those that a mesh axis runs over, the one named last changes fastest.
Arguments:
- green_matrix: bfloat16 [4608, 16384], P('pix', 'par'), may hold values from -0.046875 to 0.046875
- observed: bfloat16 [64, 4608], P('parts', 'pix'), parts along dimension 0, may hold values from -1000 to 1000
Outputs:
- solution: float32 [64, 16384], P('parts', 'par'), parts along dimension 0
- residual: float32 [64, 4608], P('parts', 'pix'), parts along dimension 0
There are 2 independent parts, one for each index of `parts`. A program takes and returns all parts, laid end to end along the dimension named above; an argument that names none is the same for every part. Nothing has to cross between parts.
All inputs are finite; a program needn't handle non-finite values.
Results may differ from a plain program's by a relative error of at most 0.0038.
Values may be sent and summed in bfloat16 or wider, within the bound.
No kernel may reach another device: no remote copies, remote signals or barrier semaphores. Data moves between devices by JAX's collectives and lax.ppermute only.
A program may use at most 64 MiB of HBM per device.

v0:
```python
import jax
import jax.numpy as jnp
from jax import lax
from jax.sharding import PartitionSpec as P

GRID = 128
ITERS = 5


def padded_2(block, sides, width):
    for axis, dim in sides:
        count = lax.axis_size(axis)
        forward = [(i, i + 1) for i in range(count - 1)]
        backward = [(target, source) for source, target in forward]
        low = lax.ppermute(
            lax.slice_in_dim(block, block.shape[dim] - width, None, axis=dim), axis, forward
        )
        high = lax.ppermute(lax.slice_in_dim(block, 0, width, axis=dim), axis, backward)
        block = jnp.concatenate([low, block, high], axis=dim)
    return block


def smooth(values):
    set_count = values.shape[0]
    grid_rows = values.shape[1] // GRID
    tiles = values.reshape(set_count, grid_rows, GRID)
    padded = padded_2(tiles, (("par", 1),), 1)
    padded = jnp.pad(padded, ((0, 0), (0, 0), (1, 1)))
    beside_all = (
        padded[:, 2:, 1:-1] + padded[:, :-2, 1:-1] + padded[:, 1:-1, 2:] + padded[:, 1:-1, :-2]
    )
    return (0.25 * (4.0 * tiles - beside_all)).reshape(set_count, grid_rows * GRID)


def forward(rounded, green_matrix):
    partial_value = lax.dot_general(
        rounded, green_matrix, (((1,), (1,)), ((), ())), preferred_element_type=jnp.float32
    )
    return lax.psum(partial_value, "par")


def curvatures(image, smoothed):
    local_image = jnp.sum(image * image, axis=1)
    local_smooth = jnp.sum(smoothed * smoothed, axis=1)
    image_sq = lax.psum(local_image, "pix")
    smooth_sq = lax.psum(local_smooth, "par")
    return image_sq + smooth_sq


def backward_sum(rounded, green_matrix):
    return lax.psum(jnp.dot(rounded, green_matrix, preferred_element_type=jnp.float32), "pix")


def column_squares(gradient):
    return lax.psum(jnp.sum(gradient * gradient, axis=1), "par")


def on_device(green_matrix, observed):
    set_count = observed.shape[0]
    tile_cells = green_matrix.shape[1]
    residual = observed.astype(jnp.float32)
    gradient = backward_sum(observed, green_matrix)
    grad_sq = column_squares(gradient)
    direction = gradient
    solution = jnp.zeros((set_count, tile_cells), jnp.float32)
    smooth_res = jnp.zeros((set_count, tile_cells), jnp.float32)
    for sweep in range(ITERS):
        rounded = direction.astype(jnp.bfloat16)
        image = forward(rounded, green_matrix)
        smoothed = smooth(lax.optimization_barrier(rounded).astype(jnp.float32))
        step_len = (grad_sq / curvatures(image, smoothed))[:, None]
        solution = solution + step_len * direction
        residual = residual - step_len * image
        smooth_res = smooth_res - step_len * smoothed
        if sweep + 1 < ITERS:
            gradient = backward_sum(residual.astype(jnp.bfloat16), green_matrix) + smooth(
                smooth_res
            )
            fresh_sq = column_squares(gradient)
            direction = gradient + (fresh_sq / grad_sq)[:, None] * direction
            grad_sq = fresh_sq
    return (solution, residual)


def solution(mesh):
    return jax.shard_map(
        on_device,
        mesh=mesh,
        in_specs=(P("pix", "par"), P("parts", "pix")),
        out_specs=(P("parts", "par"), P("parts", "pix")),
        check_vma=False,
    )
```

profile of v0, /device:TPU:0, one launch (start us, length us, event | category | flops | bytes accessed | tf_op | source)
XLA Modules:
  0.0 557.3 jit_solution(6629463593647099205)
XLA Ops:
  13.5 41.3 %all-reduce.21.cloned.1.call-done = f32[32,4096]{1,0:T(8,128)} async-done(((f32[32,4096]{1,0:T(8,128)}), f32[32,4096]{1,0:T(8,128)}) %all-reduce.21.cloned.1.call-update) | async-done | bytes 524304 | tf_op jit(solution)/shard_map/psum | solution.py:51
  59.0 7.2 %fusion.54 = f32[32,1152]{1,0:T(8,128)} fusion(bf16[32,4096]{1,0:T(8,128)(2,1)S(1)} %get-tuple-element.45, bf16[1152,4096]{1,0:T(8,128)(2,1)} %param.2), kind=kOutput, calls=%fused_computation.151 | convolution fusion | flops 301989888 | bytes 9846784 | tf_op jit(solution)/shard_map/dot_general | solution.py:36
  67.5 8.5 %all-reduce.9 = (f32[32]{0:T(128)S(1)}, f32[32]{0:T(128)S(1)}) all-reduce(f32[32]{0:T(128)S(1)} %get-tuple-element.44, f32[32]{0:T(128)S(1)} %get-tuple-element.24), channel_id=1, replica_groups=mesh['parts'=2,'pix'=4,'par'=4] {'par'}, use_global_device_ids=true, to_apply=%region_2.0 | all-reduce | flops 64 | bytes 512 | tf_op jit(solution)/shard_map/psum | solution.py:55
  75.9 24.4 %all-reduce.23.cloned.1.call-done = f32[32,1152]{1,0:T(8,128)} async-done(((f32[32,1152]{1,0:T(8,128)}), f32[32,1152]{1,0:T(8,128)}) %all-reduce.23.cloned.1.call-update) | async-done | bytes 147472 | tf_op jit(solution)/shard_map/psum | solution.py:39
  101.3 11.7 %psum.178 = f32[32]{0:T(128)S(1)} all-reduce(f32[32]{0:T(128)S(1)} %multiply_reduce_fusion.13), channel_id=1, replica_groups=mesh['parts'=2,'pix'=4,'par'=4] {'pix'}, use_global_device_ids=true, to_apply=%region_5.6 | all-reduce | flops 32 | bytes 256 | tf_op jit(solution)/shard_map/psum | solution.py:45
  126.5 29.6 %all-reduce.25.cloned.1.call-done = f32[32,4096]{1,0:T(8,128)} async-done(((f32[32,4096]{1,0:T(8,128)}), f32[32,4096]{1,0:T(8,128)}) %all-reduce.25.cloned.1.call-update) | async-done | bytes 524304 | tf_op jit(solution)/shard_map/psum | solution.py:51
  166.9 7.2 %fusion.55 = f32[32,1152]{1,0:T(8,128)} fusion(bf16[32,4096]{1,0:T(8,128)(2,1)S(1)} %get-tuple-element.20, bf16[1152,4096]{1,0:T(8,128)(2,1)} %param.2), kind=kOutput, calls=%fused_computation.152 | convolution fusion | flops 301989888 | bytes 9846784 | tf_op jit(solution)/shard_map/dot_general | solution.py:36
  175.4 8.4 %psum.184 = f32[32]{0:T(128)S(1)} all-reduce(f32[32]{0:T(128)S(1)} %get-tuple-element.18), channel_id=1, replica_groups=mesh['parts'=2,'pix'=4,'par'=4] {'par'}, use_global_device_ids=true, to_apply=%region_15.16 | all-reduce | flops 32 | bytes 256 | tf_op jit(solution)/shard_map/psum | solution.py:46
  183.8 24.2 %all-reduce.27.cloned.1.call-done = f32[32,1152]{1,0:T(8,128)} async-done(((f32[32,1152]{1,0:T(8,128)}), f32[32,1152]{1,0:T(8,128)}) %all-reduce.27.cloned.1.call-update) | async-done | bytes 147472 | tf_op jit(solution)/shard_map/psum | solution.py:39
  209.0 11.7 %psum.183 = f32[32]{0:T(128)S(1)} all-reduce(f32[32]{0:T(128)S(1)} %multiply_reduce_fusion.12), channel_id=1, replica_groups=mesh['parts'=2,'pix'=4,'par'=4] {'pix'}, use_global_device_ids=true, to_apply=%region_13.14 | all-reduce | flops 32 | bytes 256 | tf_op jit(solution)/shard_map/psum | solution.py:45
  235.0 29.6 %all-reduce.29.cloned.1.call-done = f32[32,4096]{1,0:T(8,128)} async-done(((f32[32,4096]{1,0:T(8,128)}), f32[32,4096]{1,0:T(8,128)}) %all-reduce.29.cloned.1.call-update) | async-done | bytes 524304 | tf_op jit(solution)/shard_map/psum | solution.py:51
  275.4 7.2 %fusion.56 = f32[32,1152]{1,0:T(8,128)} fusion(bf16[32,4096]{1,0:T(8,128)(2,1)S(1)} %get-tuple-element.14, bf16[1152,4096]{1,0:T(8,128)(2,1)} %param.2), kind=kOutput, calls=%fused_computation.153 | convolution fusion | flops 301989888 | bytes 9846784 | tf_op jit(solution)/shard_map/dot_general | solution.py:36
  283.9 8.3 %psum.189 = f32[32]{0:T(128)S(1)} all-reduce(f32[32]{0:T(128)S(1)} %get-tuple-element.12), channel_id=1, replica_groups=mesh['parts'=2,'pix'=4,'par'=4] {'par'}, use_global_device_ids=true, to_apply=%region_23.24 | all-reduce | flops 32 | bytes 256 | tf_op jit(solution)/shard_map/psum | solution.py:46
  292.1 24.4 %all-reduce.31.cloned.1.call-done = f32[32,1152]{1,0:T(8,128)} async-done(((f32[32,1152]{1,0:T(8,128)}), f32[32,1152]{1,0:T(8,128)}) %all-reduce.31.cloned.1.call-update) | async-done | bytes 147472 | tf_op jit(solution)/shard_map/psum | solution.py:39
  317.5 11.7 %psum.188 = f32[32]{0:T(128)S(1)} all-reduce(f32[32]{0:T(128)S(1)} %multiply_reduce_fusion.11), channel_id=1, replica_groups=mesh['parts'=2,'pix'=4,'par'=4] {'pix'}, use_global_device_ids=true, to_apply=%region_21.22 | all-reduce | flops 32 | bytes 256 | tf_op jit(solution)/shard_map/psum | solution.py:45
  342.7 29.6 %all-reduce.33.cloned.1.call-done = f32[32,4096]{1,0:T(8,128)} async-done(((f32[32,4096]{1,0:T(8,128)}), f32[32,4096]{1,0:T(8,128)}) %all-reduce.33.cloned.1.call-update) | async-done | bytes 524304 | tf_op jit(solution)/shard_map/psum | solution.py:51
  393.4 8.3 %psum.194 = f32[32]{0:T(128)S(1)} all-reduce(f32[32]{0:T(128)S(1)} %get-tuple-element.6), channel_id=1, replica_groups=mesh['parts'=2,'pix'=4,'par'=4] {'par'}, use_global_device_ids=true, to_apply=%region_31.32 | all-reduce | flops 32 | bytes 256 | tf_op jit(solution)/shard_map/psum | solution.py:46
  401.7 23.6 %all-reduce.35.cloned.1.call-done = f32[32,1152]{1,0:T(8,128)} async-done(((f32[32,1152]{1,0:T(8,128)}), f32[32,1152]{1,0:T(8,128)}) %all-reduce.35.cloned.1.call-update) | async-done | bytes 147472 | tf_op jit(solution)/shard_map/psum | solution.py:39
  426.4 11.7 %psum.193 = f32[32]{0:T(128)S(1)} all-reduce(f32[32]{0:T(128)S(1)} %multiply_reduce_fusion.10), channel_id=1, replica_groups=mesh['parts'=2,'pix'=4,'par'=4] {'pix'}, use_global_device_ids=true, to_apply=%region_29.30 | all-reduce | flops 32 | bytes 256 | tf_op jit(solution)/shard_map/psum | solution.py:45
  453.1 29.6 %all-reduce.37.cloned.1.call-done = f32[32,4096]{1,0:T(8,128)} async-done(((f32[32,4096]{1,0:T(8,128)}), f32[32,4096]{1,0:T(8,128)}) %all-reduce.37.cloned.1.call-update) | async-done | bytes 524304 | tf_op jit(solution)/shard_map/psum | solution.py:51
  493.5 7.2 %fusion.58 = f32[32,1152]{1,0:T(8,128)} fusion(bf16[32,4096]{1,0:T(8,128)(2,1)S(1)} %fusion.26, bf16[1152,4096]{1,0:T(8,128)(2,1)} %param.2), kind=kOutput, calls=%fused_computation.155 | convolution fusion | flops 301989888 | bytes 9846784 | tf_op jit(solution)/shard_map/dot_general | solution.py:36
  501.9 8.3 %psum.199 = f32[32]{0:T(128)S(1)} all-reduce(f32[32]{0:T(128)S(1)} %fusion.4), channel_id=1, replica_groups=mesh['parts'=2,'pix'=4,'par'=4] {'par'}, use_global_device_ids=true, to_apply=%region_39.40 | all-reduce | flops 32 | bytes 256 | tf_op jit(solution)/shard_map/psum | solution.py:46
  510.2 24.4 %all-reduce.39.cloned.1.call-done = f32[32,1152]{1,0:T(8,128)} async-done(((f32[32,1152]{1,0:T(8,128)}), f32[32,1152]{1,0:T(8,128)}) %all-reduce.39.cloned.1.call-update) | async-done | bytes 147472 | tf_op jit(solution)/shard_map/psum | solution.py:39
  535.6 11.7 %psum.198 = f32[32]{0:T(128)S(1)} all-reduce(f32[32]{0:T(128)S(1)} %multiply_reduce_fusion.9), channel_id=1, replica_groups=mesh['parts'=2,'pix'=4,'par'=4] {'pix'}, use_global_device_ids=true, to_apply=%region_37.38 | all-reduce | flops 32 | bytes 256 | tf_op jit(solution)/shard_map/psum | solution.py:45
  (156 shorter events, 132.7 us)
Async XLA Ops:
  7.2 47.7 %all-reduce.21.cloned.1.call-start = ((), (), s32[]{:S(2)}) async-start(), calls=%async_computation | async-start | bytes 1048576 | tf_op jit(solution)/shard_map/psum | solution.py:51
  13.5 86.8 %all-reduce.23.cloned.1.call-start = ((), (), s32[]{:S(2)}) async-start(), calls=%async_computation.1 | async-start | bytes 294912 | tf_op jit(solution)/shard_map/psum | solution.py:39
  56.4 9.9 %collective-permute-start.1 = (f32[32,1,128]{2,1,0:T(1,128)S(1)}, f32[32,1,128]{2,1,0:T(1,128)S(1)}, u32[]{:S(2)}, u32[]{:S(2)}) collective-permute-start(f32[32,1,128]{2,1,0:T(1,128)S(1)} %get-tuple-element.42), channel_id=1, source_target_pairs={{0,1},{1,2},{2,3},{4,5},{5,6},{6,7},{8,9},{9,10},{10,11},{12,13},{... | collective-permute-start | bytes 49160 | tf_op jit(solution)/shard_map/ppermute | solution.py:15
  57.7 8.6 %collective-permute-start = (f32[32,1,128]{2,1,0:T(1,128)S(1)}, f32[32,1,128]{2,1,0:T(1,128)S(1)}, u32[]{:S(2)}, u32[]{:S(2)}) collective-permute-start(f32[32,1,128]{2,1,0:T(1,128)S(1)} %get-tuple-element.43), channel_id=1, source_target_pairs={{1,0},{2,1},{3,2},{5,4},{6,5},{7,6},{9,8},{10,9},{11,10},{13,12},{... | collective-permute-start | bytes 49160 | tf_op jit(solution)/shard_map/ppermute | solution.py:18
  66.3 89.8 %all-reduce.25.cloned.1.call-start = ((), (), s32[]{:S(2)}) async-start(), calls=%async_computation.2 | async-start | bytes 1048576 | tf_op jit(solution)/shard_map/psum | solution.py:51
  119.4 88.6 %all-reduce.27.cloned.1.call-start = ((), (), s32[]{:S(2)}) async-start(), calls=%async_computation.3 | async-start | bytes 294912 | tf_op jit(solution)/shard_map/psum | solution.py:39
  120.9 4.6 collective-permute-start.2
  163.8 10.4 %collective-permute-start.5 = (f32[32,1,128]{2,1,0:T(1,128)S(1)}, f32[32,1,128]{2,1,0:T(1,128)S(1)}, u32[]{:S(2)}, u32[]{:S(2)}) collective-permute-start(f32[32,1,128]{2,1,0:T(1,128)S(1)} %get-tuple-element.38), channel_id=1, source_target_pairs={{0,1},{1,2},{2,3},{4,5},{5,6},{6,7},{8,9},{9,10},{10,11},{12,13},{... | collective-permute-start | bytes 49160 | tf_op jit(solution)/shard_map/ppermute | solution.py:15
  165.6 8.6 %collective-permute-start.4 = (f32[32,1,128]{2,1,0:T(1,128)S(1)}, f32[32,1,128]{2,1,0:T(1,128)S(1)}, u32[]{:S(2)}, u32[]{:S(2)}) collective-permute-start(f32[32,1,128]{2,1,0:T(1,128)S(1)} %get-tuple-element.39), channel_id=1, source_target_pairs={{1,0},{2,1},{3,2},{5,4},{6,5},{7,6},{9,8},{10,9},{11,10},{13,12},{... | collective-permute-start | bytes 49160 | tf_op jit(solution)/shard_map/ppermute | solution.py:18
  174.2 90.4 %all-reduce.29.cloned.1.call-start = ((), (), s32[]{:S(2)}) async-start(), calls=%async_computation.4 | async-start | bytes 1048576 | tf_op jit(solution)/shard_map/psum | solution.py:51
  228.0 88.5 %all-reduce.31.cloned.1.call-start = ((), (), s32[]{:S(2)}) async-start(), calls=%async_computation.5 | async-start | bytes 294912 | tf_op jit(solution)/shard_map/psum | solution.py:39
  229.5 4.6 collective-permute-start.6
  272.4 10.4 %collective-permute-start.9 = (f32[32,1,128]{2,1,0:T(1,128)S(1)}, f32[32,1,128]{2,1,0:T(1,128)S(1)}, u32[]{:S(2)}, u32[]{:S(2)}) collective-permute-start(f32[32,1,128]{2,1,0:T(1,128)S(1)} %get-tuple-element.34), channel_id=1, source_target_pairs={{0,1},{1,2},{2,3},{4,5},{5,6},{6,7},{8,9},{9,10},{10,11},{12,13},{... | collective-permute-start | bytes 49160 | tf_op jit(solution)/shard_map/ppermute | solution.py:15
  274.1 8.6 %collective-permute-start.8 = (f32[32,1,128]{2,1,0:T(1,128)S(1)}, f32[32,1,128]{2,1,0:T(1,128)S(1)}, u32[]{:S(2)}, u32[]{:S(2)}) collective-permute-start(f32[32,1,128]{2,1,0:T(1,128)S(1)} %get-tuple-element.35), channel_id=1, source_target_pairs={{1,0},{2,1},{3,2},{5,4},{6,5},{7,6},{9,8},{10,9},{11,10},{13,12},{... | collective-permute-start | bytes 49160 | tf_op jit(solution)/shard_map/ppermute | solution.py:18
  282.7 89.6 %all-reduce.33.cloned.1.call-start = ((), (), s32[]{:S(2)}) async-start(), calls=%async_computation.6 | async-start | bytes 1048576 | tf_op jit(solution)/shard_map/psum | solution.py:51
  335.6 89.7 %all-reduce.35.cloned.1.call-start = ((), (), s32[]{:S(2)}) async-start(), calls=%async_computation.7 | async-start | bytes 294912 | tf_op jit(solution)/shard_map/psum | solution.py:39
  337.1 4.6 collective-permute-start.10
  381.0 10.6 %collective-permute-start.13 = (f32[32,1,128]{2,1,0:T(1,128)S(1)}, f32[32,1,128]{2,1,0:T(1,128)S(1)}, u32[]{:S(2)}, u32[]{:S(2)}) collective-permute-start(f32[32,1,128]{2,1,0:T(1,128)S(1)} %get-tuple-element.30), channel_id=1, source_target_pairs={{0,1},{1,2},{2,3},{4,5},{5,6},{6,7},{8,9},{9,10},{10,11},{12,13},{... | collective-permute-start | bytes 49160 | tf_op jit(solution)/shard_map/ppermute | solution.py:15
  382.8 8.8 %collective-permute-start.12 = (f32[32,1,128]{2,1,0:T(1,128)S(1)}, f32[32,1,128]{2,1,0:T(1,128)S(1)}, u32[]{:S(2)}, u32[]{:S(2)}) collective-permute-start(f32[32,1,128]{2,1,0:T(1,128)S(1)} %get-tuple-element.31), channel_id=1, source_target_pairs={{1,0},{2,1},{3,2},{5,4},{6,5},{7,6},{9,8},{10,9},{11,10},{13,12},{... | collective-permute-start | bytes 49160 | tf_op jit(solution)/shard_map/ppermute | solution.py:18
  391.5 91.2 %all-reduce.37.cloned.1.call-start = ((), (), s32[]{:S(2)}) async-start(), calls=%async_computation.8 | async-start | bytes 1048576 | tf_op jit(solution)/shard_map/psum | solution.py:51
  446.1 88.5 %all-reduce.39.cloned.1.call-start = ((), (), s32[]{:S(2)}) async-start(), calls=%async_computation.9 | async-start | bytes 294912 | tf_op jit(solution)/shard_map/psum | solution.py:39
  447.6 4.6 collective-permute-start.14
  490.5 10.3 %collective-permute-start.17 = (f32[32,1,128]{2,1,0:T(1,128)S(1)}, f32[32,1,128]{2,1,0:T(1,128)S(1)}, u32[]{:S(2)}, u32[]{:S(2)}) collective-permute-start(f32[32,1,128]{2,1,0:T(1,128)S(1)} %get-tuple-element.26), channel_id=1, source_target_pairs={{0,1},{1,2},{2,3},{4,5},{5,6},{6,7},{8,9},{9,10},{10,11},{12,13},{... | collective-permute-start | bytes 49160 | tf_op jit(solution)/shard_map/ppermute | solution.py:15
  492.2 8.6 %collective-permute-start.16 = (f32[32,1,128]{2,1,0:T(1,128)S(1)}, f32[32,1,128]{2,1,0:T(1,128)S(1)}, u32[]{:S(2)}, u32[]{:S(2)}) collective-permute-start(f32[32,1,128]{2,1,0:T(1,128)S(1)} %get-tuple-element.27), channel_id=1, source_target_pairs={{1,0},{2,1},{3,2},{5,4},{6,5},{7,6},{9,8},{10,9},{11,10},{13,12},{... | collective-permute-start | bytes 49160 | tf_op jit(solution)/shard_map/ppermute | solution.py:18
  (15 other events, 219.0 us)
Sparse Core Ops, SparseCore 0:
  13.6 41.2 all-reduce.20
  66.4 33.8 all-reduce.22
  119.6 36.4 all-reduce.24
  174.3 33.6 all-reduce.26
  228.1 36.4 all-reduce.28
  282.8 33.6 all-reduce.30
  335.8 36.4 all-reduce.32
  391.7 33.6 all-reduce.34
  446.2 36.4 all-reduce.36
  500.9 33.6 all-reduce.38
where the time goes:
time: 559 us; the launch traced here: 557 us
  waiting for transfers between devices  294 us (53%)
  blocking collectives  123 us (22%)
  matrix products  67.6 us (12%)
  other arithmetic  30.8 us (6%)
  starting transfers between devices  25.8 us (5%)
  between operations  14.8 us (3%)
    psum x5, waiting for transfers between devices, backward_sum(): lax.psum(jnp.dot(rounded, green_matrix, preferred_element_type=jnp.float3...  160 us
    psum x5, waiting for transfers between devices, forward(): return lax.psum(partial_value, 'par')  121 us
    psum x5, blocking collectives, curvatures(): image_sq = lax.psum(local_image, 'pix')  58.5 us
    dot_general x5, matrix products, forward(): lax.dot_general(rounded, green_matrix, (((1,), (1,)), ((), ())), preferre...  36.2 us
    psum x4, blocking collectives, curvatures(): smooth_sq = lax.psum(local_smooth, 'par')  33.2 us
    dot_general x5, matrix products, backward_sum(): jnp.dot(rounded, green_matrix, preferred_element_type=jnp.float32)  31.5 us
    psum x5, blocking collectives, column_squares(): return lax.psum(jnp.sum(gradient * gradient, axis=1), 'par')  31.1 us
    ppermute x9, starting transfers between devices, padded_2(): lax.ppermute(lax.slice_in_dim(block, block.shape[dim] - width, None, axis...  13.5 us
  transfers between devices with their start and end apart: 28, of which 14 were waited for; matrix products, arithmetic and copies ran while one was open for 8% of the time, Pallas kernels for 0%

commit v1 on v0

v1 whole, which is shorter than its diff:
```python
import jax
import jax.numpy as jnp
from jax import lax
from jax.sharding import PartitionSpec as P

GRID = 128
ITERS = 5
LANES = 128
BF16 = jnp.bfloat16
F32 = jnp.float32


def xor_pairs(count, offset):
    return [(i, i ^ offset) for i in range(count)]


def split3(values):
    high = lax.reduce_precision(values, 8, 7)
    rest = values - high
    mid = lax.reduce_precision(rest, 8, 7)
    low = lax.reduce_precision(rest - mid, 8, 7)
    return high.astype(BF16), mid.astype(BF16), low.astype(BF16)


def join3(terms):
    high, mid, low = (term.astype(F32) for term in terms)
    return (high + mid) + low


def pack_scalars(columns):
    terms = [term[:, None] for column in columns for term in split3(column)]
    block = jnp.concatenate(terms, axis=1)
    return jnp.pad(block, ((0, 0), (0, LANES - block.shape[1])))


def unpack_scalars(block, count):
    return [join3([block[:, 3 * i + t] for t in range(3)]) for i in range(count)]


def tree_sum(parts):
    while len(parts) > 1:
        parts = [parts[i] + parts[i + 1] for i in range(0, len(parts), 2)]
    return parts[0]


def beside(row):
    padded = jnp.pad(row, ((0, 0), (0, 0), (1, 1)))
    return padded[:, :, 2:] + padded[:, :, :-2]


def inner_smooth(tiles):
    mid = tiles[:, 1:-1]
    return mid - 0.25 * ((tiles[:, 2:] + tiles[:, :-2]) + beside(mid))


def seam(lower, upper):
    low0, low1 = lower[:, :1], lower[:, 1:]
    up0, up1 = upper[:, :1], upper[:, 1:]
    low_s = low1 - 0.25 * (low0 + beside(low1))
    up_s = up0 - 0.25 * (up1 + beside(up0))
    cross = -0.5 * (low_s * up0 + up_s * low1)
    return jnp.sum(cross + 0.0625 * (up0 * up0 + low1 * low1), axis=(1, 2))


def gather_pix(shard, count):
    index = lax.axis_index("pix")
    parts = [shard]
    for offset in range(1, count):
        parts.append(lax.ppermute(shard, "pix", xor_pairs(count, offset)))
    step = 1
    while step < count:
        swap = (index // step) % 2 == 1
        parts = [jnp.where(swap, parts[i ^ step], parts[i]) for i in range(count)]
        step *= 2
    return jnp.concatenate(parts, axis=1)


def par_sum(value, scalars, first, last, count):
    sets, width = value.shape
    index = lax.axis_index("par")
    rows = first.shape
    above = jnp.zeros(rows, F32)
    below = jnp.zeros(rows, F32)
    step = 1
    while step < count:
        upper_side = (index // step) % 2 == 1
        inside = index % step
        flat = [first.reshape(sets, -1), last.reshape(sets, -1)]
        if step == 1:
            packed = jnp.stack(scalars, axis=1)
            packed = jnp.pad(packed, ((0, 0), (0, LANES - packed.shape[1])))
            message = jnp.concatenate([value, packed] + flat, axis=1)
        else:
            message = jnp.concatenate(
                [value.astype(BF16), pack_scalars(scalars)] + [rows_.astype(BF16) for rows_ in flat], axis=1
            )
        got = lax.ppermute(message, "par", xor_pairs(count, step))
        if step == 1:
            value = value + got[:, :width]
            others = [got[:, width + i] for i in range(len(scalars))]
        else:
            value = message[:, :width].astype(F32) + got[:, :width].astype(F32)
            others = unpack_scalars(got[:, width : width + LANES], len(scalars))
        got_rows = got[:, width + LANES :].astype(F32)
        half = got_rows.shape[1] // 2
        got_first = got_rows[:, :half].reshape(rows)
        got_last = got_rows[:, half:].reshape(rows)
        lower_last = jnp.where(upper_side, got_last, last)
        upper_first = jnp.where(upper_side, first, got_first)
        scalars = [mine + other for mine, other in zip(scalars, others)]
        scalars[1] = scalars[1] + seam(lower_last, upper_first)
        above = jnp.where(upper_side & (inside == 0), lower_last, above)
        below = jnp.where(jnp.logical_not(upper_side) & (inside == step - 1), upper_first, below)
        first = jnp.where(upper_side, got_first, first)
        last = jnp.where(upper_side, last, got_last)
        step *= 2
    return value, scalars, above, below


def on_device(green_matrix, observed):
    sets = observed.shape[0]
    pixels, cells = green_matrix.shape
    n_pix, n_par = lax.axis_size("pix"), lax.axis_size("par")
    here, tile = lax.axis_index("pix"), lax.axis_index("par")
    width = cells // n_pix
    rows = cells // GRID
    direct = n_pix <= 8

    def block_of(whole, offset):
        return lax.dynamic_slice_in_dim(whole, (here ^ offset) * width, width, axis=1)

    own_mask = (jnp.arange(cells) // width == here)[None, :]

    def scatter_pix(partial, scalar):
        if not direct:
            shard = lax.psum_scatter(partial, "pix", scatter_dimension=1, tiled=True)
            return shard, lax.psum(scalar, "pix"), jnp.zeros_like(partial)
        rounded = lax.reduce_precision(partial, 8, 7)
        lost = jnp.where(own_mask, 0.0, partial - rounded)
        sent = rounded.astype(BF16)
        tail = pack_scalars([scalar])
        shards, totals = [block_of(partial, 0)], [scalar]
        for offset in range(1, n_pix):
            message = jnp.concatenate([block_of(sent, offset), tail], axis=1)
            got = lax.ppermute(message, "pix", xor_pairs(n_pix, offset))
            shards.append(got[:, :width].astype(F32))
            totals.append(unpack_scalars(got[:, width:], 1)[0])
        return tree_sum(shards), tree_sum(totals), lost

    def gather(shard):
        if direct:
            return gather_pix(shard, n_pix)
        return lax.all_gather(shard, "pix", axis=1, tiled=True)

    residual = observed.astype(F32)
    partial = jnp.dot(observed, green_matrix, preferred_element_type=F32)
    zero_set = jnp.zeros((sets,), F32)
    grad, _, lost = scatter_pix(partial, zero_set)
    solution = jnp.zeros((sets, cells), F32)
    for sweep in range(ITERS):
        whole = gather(grad.astype(BF16))
        fresh = whole.astype(F32)
        tiles = fresh.reshape(sets, rows, GRID)
        image = lax.dot_general(whole, green_matrix, (((1,), (1,)), ((), ())), preferred_element_type=F32)
        alone = inner_smooth(jnp.pad(tiles, ((0, 0), (1, 1), (0, 0))))
        scalars = [jnp.sum(fresh * fresh, axis=1), jnp.sum(alone * alone, axis=(1, 2))]
        if sweep:
            scalars.append(jnp.sum(tiles * twice, axis=(1, 2)))
        image, scalars, above, below = par_sum(image, scalars, tiles[:, :2], tiles[:, -2:], n_par)
        padded = jnp.concatenate([above, tiles, below], axis=1)
        if sweep:
            beta = scalars[0] / grad_sq
            forward = image + beta[:, None] * forward
            direction = padded + beta[:, None, None] * direction
            smooth_sq = scalars[1] + 2.0 * beta * scalars[2] + beta * beta * smooth_sq
        else:
            forward, direction, smooth_sq = image, padded, scalars[1]
        grad_sq = scalars[0]
        image_sq = jnp.sum(forward * forward, axis=1)
        if sweep + 1 < ITERS:
            once = inner_smooth(direction)
            row_id = jnp.arange(rows + 2)[None, :, None]
            outside = ((row_id == 0) & (tile == 0)) | ((row_id == rows + 1) & (tile == n_par - 1))
            twice = inner_smooth(jnp.where(outside, 0.0, once))
            partial = jnp.dot(forward.astype(BF16), green_matrix, preferred_element_type=F32)
            guess = (n_pix * image_sq + smooth_sq) / grad_sq
            aimed = partial - guess[:, None] * lost
            change, image_sq, dropped = scatter_pix(aimed, image_sq)
            change = change + block_of(twice.reshape(sets, cells), 0)
        elif direct:
            tail = pack_scalars([image_sq])
            totals = [image_sq]
            for offset in range(1, n_pix):
                got = lax.ppermute(tail, "pix", xor_pairs(n_pix, offset))
                totals.append(unpack_scalars(got, 1)[0])
            image_sq = tree_sum(totals)
        else:
            image_sq = lax.psum(image_sq, "pix")
        step_len = (grad_sq / (image_sq + smooth_sq))[:, None]
        solution = solution + step_len * direction[:, 2:-2].reshape(sets, cells)
        residual = residual - step_len * forward
        if sweep + 1 < ITERS:
            lost = lost - step_len * (partial - aimed + dropped)
            grad = grad - step_len * change
    return (solution, residual)


def solution(mesh):
    return jax.shard_map(
        on_device,
        mesh=mesh,
        in_specs=(P("pix", "par"), P("parts", "pix")),
        out_specs=(P("parts", "par"), P("parts", "pix")),
        check_vma=False,
    )
```

time: 559 us -> 577 us (1.032); the launches traced: 557 us -> 567 us
  blocking collectives: 123 us -> 0 us
  local copies, waits for them, and re-layouts: 1.4 us -> 97 us
  waiting for transfers between devices: 294 us -> 223 us
  other arithmetic: 30.8 us -> 93.2 us
  starting transfers between devices: 25.8 us -> 78.7 us
  between operations: 14.8 us -> 3.13 us
    psum x10 -> x0, waiting for transfers between devices: 281 us -> none  [the longest x5 160 us: backward_sum(): lax.psum(jnp.dot(rounded, green_matrix, preferred_element_type=jnp.float3...]
    ppermute x18 -> x43, waiting for transfers between devices: 13.2 us -> 223 us  [the longest x15 85.4 us: scatter_pix(): got = lax.ppermute(message, 'pix', xor_pairs(n_pix, offset))]
    psum x14 -> x0, blocking collectives: 123 us -> none  [the longest x5 58.5 us: curvatures(): image_sq = lax.psum(local_image, 'pix')]
    ppermute x18 -> x43, starting transfers between devices: 25.4 us -> 78.7 us  [the longest x15 43.3 us: gather_pix(): parts.append(lax.ppermute(shard, 'pix', xor_pairs(count, offset)))]
    convert_element_type x4 -> x56, other arithmetic: 2.5 us -> 34.7 us  [the longest x5 9.31 us: on_device(): whole = gather(grad.astype(BF16))]
    unnamed x27 -> x259, local copies, waits for them, and re-layouts: 1.18 us -> 23.4 us
    slice x9 -> x49, local copies, waits for them, and re-layouts: 0.23 us -> 20 us  [the longest x6 9.15 us: on_device(): solution = solution + step_len * direction[:, 2:-2].reshape(sets, cells)]
    concatenate x0 -> x26, local copies, waits for them, and re-layouts: none -> 15.1 us  [the longest x20 11.5 us: gather_pix(): return jnp.concatenate(parts, axis=1)]
  transfers between devices with their start and end apart: 28 -> 43, of which waited for: 14 -> 27; matrix products, arithmetic and copies ran while one was open for 8% -> 6% of each run, Pallas kernels for 0% -> 0%
where the time goes in v1:
time: 577 us; the launch traced here: 567 us
  waiting for transfers between devices  223 us (39%)
  local copies, waits for them, and re-layouts  97 us (17%)
  other arithmetic  93.2 us (16%)
  starting transfers between devices  78.7 us (14%)
  matrix products  71.9 us (12%)
    ppermute x15, waiting for transfers between devices, scatter_pix(): got = lax.ppermute(message, 'pix', xor_pairs(n_pix, offset))  85.4 us
    ppermute x15, waiting for transfers between devices, gather_pix(): parts.append(lax.ppermute(shard, 'pix', xor_pairs(count, offset)))  82.1 us
    ppermute x10, waiting for transfers between devices, par_sum(): got = lax.ppermute(message, 'par', xor_pairs(count, step))  55.5 us
    ppermute x15, starting transfers between devices, gather_pix(): parts.append(lax.ppermute(shard, 'pix', xor_pairs(count, offset)))  43.3 us
    dot_general x5, matrix products, on_device(): lax.dot_general(whole, green_matrix, (((1,), (1,)), ((), ())), preferred_...  34.9 us
    dot_general x4, matrix products, on_device(): jnp.dot(forward.astype(BF16), green_matrix, preferred_element_type=F32)  30.9 us
    unnamed x259, local copies, waits for them, and re-layouts  23.4 us
    ppermute x15, starting transfers between devices, scatter_pix(): got = lax.ppermute(message, 'pix', xor_pairs(n_pix, offset))  23.2 us
  transfers between devices with their start and end apart: 43, of which 27 were waited for; matrix products, arithmetic and copies ran while one was open for 6% of the time, Pallas kernels for 0%

profile of v1, /device:TPU:0, one launch (start us, length us, event | category | flops | bytes accessed | tf_op | source)
XLA Modules:
  0.0 566.9 jit_solution(7567199932878730940)
XLA Ops:
  13.6 10.2 %collective-permute-done = bf16[32,1152]{0,1:T(8,128)(2,1)S(1)} collective-permute-done((bf16[32,1152]{0,1:T(8,128)(2,1)}, bf16[32,1152]{0,1:T(8,128)(2,1)S(1)}, u32[]{:S(2)}, u32[]{:S(2)}) %collective-permute-start) | collective-permute-done | bytes 73760 | tf_op jit(solution)/shard_map/ppermute | solution.py:145
  23.8 10.8 %collective-permute-done.1 = bf16[32,1152]{0,1:T(8,128)(2,1)S(1)} collective-permute-done((bf16[32,1152]{0,1:T(8,128)(2,1)}, bf16[32,1152]{0,1:T(8,128)(2,1)S(1)}, u32[]{:S(2)}, u32[]{:S(2)}) %collective-permute-start.1) | collective-permute-done | bytes 73760 | tf_op jit(solution)/shard_map/ppermute | solution.py:145
  37.3 10.1 %collective-permute-start.4 = (bf16[32,1024]{0,1:T(8,128)(2,1)S(1)}, bf16[32,1024]{0,1:T(8,128)(2,1)}, u32[]{:S(2)}, u32[]{:S(2)}) collective-permute-start(bf16[32,1024]{0,1:T(8,128)(2,1)S(1)} %fusion.460), channel_id=1, source_target_pairs={{0,8},{4,12},{8,0},{12,4},{1,9},{5,13},{9,1},{13,5},{2,10},{6,14},... | collective-permute-start | bytes 196616 | tf_op jit(solution)/shard_map/ppermute | solution.py:69
  47.6 16.1 %collective-permute-done.4 = bf16[32,1024]{0,1:T(8,128)(2,1)} collective-permute-done((bf16[32,1024]{0,1:T(8,128)(2,1)S(1)}, bf16[32,1024]{0,1:T(8,128)(2,1)}, u32[]{:S(2)}, u32[]{:S(2)}) %collective-permute-start.4) | collective-permute-done | bytes 65568 | tf_op jit(solution)/shard_map/ppermute | solution.py:69
  65.0 6.8 %fusion.461 = f32[32,1152]{1,0:T(8,128)S(1)} fusion(bf16[1152,4096]{1,0:T(8,128)(2,1)} %param.2, bf16[32,1024]{0,1:T(8,128)(2,1)S(1)} %get-tuple-element.131, bf16[32,1024]{0,1:T(8,128)(2,1)S(1)} %get-tuple-element.130, bf16[32,1024]{0,1:T(8,128)(2,1)S(1)} %get-tuple-element.129, bf16[32,1024]{0,1:T(8,128)(2,1)S(1)} %get-tuple-element.128), kind=kOutput, calls=%fused_computation.979 | convolution fusion | flops 303038464 | bytes 9846784 | tf_op jit(solution)/shard_map/dot_general | solution.py:164
  89.0 11.3 %collective-permute-done.7 = bf16[32,1792]{0,1:T(8,128)(2,1)S(1)} collective-permute-done((bf16[32,1792]{0,1:T(8,128)(2,1)}, bf16[32,1792]{0,1:T(8,128)(2,1)S(1)}, u32[]{:S(2)}, u32[]{:S(2)}) %collective-permute-start.7) | collective-permute-done | bytes 114720 | tf_op jit(solution)/shard_map/ppermute | solution.py:97
  105.8 8.0 %reduce-precision_convert_fusion.2 = (bf16[32,4096]{0,1:T(8,128)(2,1)S(1)}, f32[32,4096]{0,1:T(8,128)}, f32[32,4096]{0,1:T(8,128)}) fusion(f32[32,4096]{0,1:T(8,128)S(1)} %get-tuple-element.272, pred[4096]{0:T(1024)(128)(4,1)S(1)} %fusion.151, f32[32]{0:T(128)S(1)} %get-tuple-element.88, bf16[1152,4096]{1,0:T(8,128)(2,1)} %param.2, ...), kind=kOutput, calls=%fused_computation.6 | convolution fusion | flops 303054848 | bytes 13439488 | tf_op jit(solution)/shard_map/dot_general | solution.py:185
  126.9 7.7 %collective-permute-done.8 = bf16[32,1152]{0,1:T(8,128)(2,1)} collective-permute-done((bf16[32,1152]{0,1:T(8,128)(2,1)}, bf16[32,1152]{0,1:T(8,128)(2,1)}, u32[]{:S(2)}, u32[]{:S(2)}) %collective-permute-start.8) | collective-permute-done | bytes 73760 | tf_op jit(solution)/shard_map/ppermute | solution.py:145
  155.9 10.3 %collective-permute-done.12 = bf16[32,1024]{0,1:T(8,128)(2,1)S(1)} collective-permute-done((bf16[32,1024]{0,1:T(8,128)(2,1)S(1)}, bf16[32,1024]{0,1:T(8,128)(2,1)S(1)}, u32[]{:S(2)}, u32[]{:S(2)}) %collective-permute-start.12) | collective-permute-done | bytes 65568 | tf_op jit(solution)/shard_map/ppermute | solution.py:69
  171.3 7.4 %fusion.140 = f32[32,1152]{1,0:T(8,128)} fusion(bf16[1152,4096]{1,0:T(8,128)(2,1)} %param.2, bf16[32,1024]{1,0:T(8,128)(2,1)} %copy.697, bf16[32,1024]{1,0:T(8,128)(2,1)} %copy.696, bf16[32,1024]{1,0:T(8,128)(2,1)} %copy.695, bf16[32,1024]{1,0:T(8,128)(2,1)S(1)} %copy.694), kind=kOutput, calls=%fused_computation.322 | convolution fusion | flops 303038464 | bytes 9846784 | tf_op jit(solution)/shard_map/dot_general | solution.py:164
  218.6 11.4 %collective-permute-done.15 = bf16[32,1792]{0,1:T(8,128)(2,1)S(1)} collective-permute-done((bf16[32,1792]{0,1:T(8,128)(2,1)S(1)}, bf16[32,1792]{0,1:T(8,128)(2,1)S(1)}, u32[]{:S(2)}, u32[]{:S(2)}) %collective-permute-start.15) | collective-permute-done | bytes 114720 | tf_op jit(solution)/shard_map/ppermute | solution.py:97
  238.4 8.6 %reduce-precision_convert_fusion.1 = (bf16[32,4096]{0,1:T(8,128)(2,1)S(1)}, f32[32,4096]{0,1:T(8,128)}, f32[32,4096]{0,1:T(8,128)}, f32[32,4096]{0,1:T(8,128)}) fusion(f32[32]{0:T(128)S(1)} %get-tuple-element.67, f32[32,4096]{0,1:T(8,128)S(1)} %copy-done.5, f32[32,4096]{0,1:T(8,128)} %get-tuple-element.273, f32[32]{0:T(128)S(1)} %fusion.445, ...), kind=kOutput, calls=%fused_computation.4 | convolution fusion | flops 303861760 | bytes 12996864 | tf_op jit(solution)/shard_map/dot_general | solution.py:185
  255.6 7.0 %collective-permute-done.16 = bf16[32,1152]{0,1:T(8,128)(2,1)} collective-permute-done((bf16[32,1152]{0,1:T(8,128)(2,1)}, bf16[32,1152]{0,1:T(8,128)(2,1)}, u32[]{:S(2)}, u32[]{:S(2)}) %collective-permute-start.16) | collective-permute-done | bytes 73760 | tf_op jit(solution)/shard_map/ppermute | solution.py:145
  262.7 9.5 %collective-permute-done.17 = bf16[32,1152]{0,1:T(8,128)(2,1)} collective-permute-done((bf16[32,1152]{0,1:T(8,128)(2,1)}, bf16[32,1152]{0,1:T(8,128)(2,1)}, u32[]{:S(2)}, u32[]{:S(2)}) %collective-permute-start.17) | collective-permute-done | bytes 73760 | tf_op jit(solution)/shard_map/ppermute | solution.py:145
  283.7 16.7 %collective-permute-done.20 = bf16[32,1024]{0,1:T(8,128)(2,1)S(1)} collective-permute-done((bf16[32,1024]{0,1:T(8,128)(2,1)S(1)}, bf16[32,1024]{0,1:T(8,128)(2,1)S(1)}, u32[]{:S(2)}, u32[]{:S(2)}) %collective-permute-start.20) | collective-permute-done | bytes 65568 | tf_op jit(solution)/shard_map/ppermute | solution.py:69
  315.5 11.1 %collective-permute-done.23 = bf16[32,1792]{0,1:T(8,128)(2,1)S(1)} collective-permute-done((bf16[32,1792]{0,1:T(8,128)(2,1)S(1)}, bf16[32,1792]{0,1:T(8,128)(2,1)S(1)}, u32[]{:S(2)}, u32[]{:S(2)}) %collective-permute-start.23) | collective-permute-done | bytes 114720 | tf_op jit(solution)/shard_map/ppermute | solution.py:97
  355.1 9.8 %collective-permute-done.25 = bf16[32,1152]{0,1:T(8,128)(2,1)} collective-permute-done((bf16[32,1152]{0,1:T(8,128)(2,1)}, bf16[32,1152]{0,1:T(8,128)(2,1)}, u32[]{:S(2)}, u32[]{:S(2)}) %collective-permute-start.25) | collective-permute-done | bytes 73760 | tf_op jit(solution)/shard_map/ppermute | solution.py:145
  377.9 15.5 %collective-permute-done.28 = bf16[32,1024]{0,1:T(8,128)(2,1)S(1)} collective-permute-done((bf16[32,1024]{0,1:T(8,128)(2,1)S(1)}, bf16[32,1024]{0,1:T(8,128)(2,1)S(1)}, u32[]{:S(2)}, u32[]{:S(2)}) %collective-permute-start.28) | collective-permute-done | bytes 65568 | tf_op jit(solution)/shard_map/ppermute | solution.py:69
  400.2 7.4 %fusion.138 = f32[32,1152]{1,0:T(8,128)} fusion(bf16[1152,4096]{1,0:T(8,128)(2,1)} %param.2, bf16[32,1024]{1,0:T(8,128)(2,1)} %copy.757, bf16[32,1024]{1,0:T(8,128)(2,1)} %copy.756, bf16[32,1024]{1,0:T(8,128)(2,1)} %copy.755, bf16[32,1024]{1,0:T(8,128)(2,1)} %copy.754), kind=kOutput, calls=%fused_computation.320 | convolution fusion | flops 303038464 | bytes 9846784 | tf_op jit(solution)/shard_map/dot_general | solution.py:164
  434.2 11.1 %collective-permute-done.31 = bf16[32,1792]{0,1:T(8,128)(2,1)S(1)} collective-permute-done((bf16[32,1792]{0,1:T(8,128)(2,1)S(1)}, bf16[32,1792]{0,1:T(8,128)(2,1)S(1)}, u32[]{:S(2)}, u32[]{:S(2)}) %collective-permute-start.31) | collective-permute-done | bytes 114720 | tf_op jit(solution)/shard_map/ppermute | solution.py:97
  451.0 7.9 %reduce-precision_convert_fusion.4 = (bf16[32,4096]{0,1:T(8,128)(2,1)S(1)}, f32[32,4096]{0,1:T(8,128)}) fusion(f32[32,4096]{0,1:T(8,128)} %get-tuple-element.44, f32[32,4096]{0,1:T(8,128)S(1)} %copy-done.4, pred[4096]{0:T(1024)(128)(4,1)S(1)} %fusion.151, f32[32,4096]{0,1:T(8,128)S(1)} %fusion.106, f32[32]{0:T(128)S(1)} %fusion.447, ...), kind=kOutput, calls=%fused_computation.34 | convolution fusion | flops 303468544 | bytes 11948288 | tf_op jit(solution)/shard_map/dot_general | solution.py:185
  473.9 9.5 %collective-permute-done.33 = bf16[32,1152]{0,1:T(8,128)(2,1)} collective-permute-done((bf16[32,1152]{0,1:T(8,128)(2,1)S(1)}, bf16[32,1152]{0,1:T(8,128)(2,1)}, u32[]{:S(2)}, u32[]{:S(2)}) %collective-permute-start.33) | collective-permute-done | bytes 73760 | tf_op jit(solution)/shard_map/ppermute | solution.py:145
  488.3 7.1 %collective-permute-start.36 = (bf16[32,1024]{0,1:T(8,128)(2,1)S(1)}, bf16[32,1024]{0,1:T(8,128)(2,1)S(1)}, u32[]{:S(2)}, u32[]{:S(2)}) collective-permute-start(bf16[32,1024]{0,1:T(8,128)(2,1)S(1)} %subtract_convert_fusion), channel_id=1, source_target_pairs={{0,8},{4,12},{8,0},{12,4},{1,9},{5,13},{9,1},{13,5},{2,10},{6,14},... | collective-permute-start | bytes 196616 | tf_op jit(solution)/shard_map/ppermute | solution.py:69
  495.5 15.5 %collective-permute-done.36 = bf16[32,1024]{0,1:T(8,128)(2,1)S(1)} collective-permute-done((bf16[32,1024]{0,1:T(8,128)(2,1)S(1)}, bf16[32,1024]{0,1:T(8,128)(2,1)S(1)}, u32[]{:S(2)}, u32[]{:S(2)}) %collective-permute-start.36) | collective-permute-done | bytes 65568 | tf_op jit(solution)/shard_map/ppermute | solution.py:69
  (624 shorter events, 316.7 us)
Async XLA Ops:
  8.0 15.8 %collective-permute-start = (bf16[32,1152]{0,1:T(8,128)(2,1)}, bf16[32,1152]{0,1:T(8,128)(2,1)S(1)}, u32[]{:S(2)}, u32[]{:S(2)}) collective-permute-start(bf16[32,1152]{0,1:T(8,128)(2,1)} %get-tuple-element.223), channel_id=1, source_target_pairs={{0,4},{4,0},{8,12},{12,8},{1,5},{5,1},{9,13},{13,9},{2,6},{6,2},{1... | collective-permute-start | bytes 221192 | tf_op jit(solution)/shard_map/ppermute | solution.py:145
  11.0 23.6 %collective-permute-start.1 = (bf16[32,1152]{0,1:T(8,128)(2,1)}, bf16[32,1152]{0,1:T(8,128)(2,1)S(1)}, u32[]{:S(2)}, u32[]{:S(2)}) collective-permute-start(bf16[32,1152]{0,1:T(8,128)(2,1)} %get-tuple-element.224), channel_id=1, source_target_pairs={{0,8},{4,12},{8,0},{12,4},{1,9},{5,13},{9,1},{13,5},{2,10},{6,14},... | collective-permute-start | bytes 221192 | tf_op jit(solution)/shard_map/ppermute | solution.py:145
  13.6 21.0 %collective-permute-start.2 = (bf16[32,1152]{0,1:T(8,128)(2,1)S(1)}, bf16[32,1152]{0,1:T(8,128)(2,1)S(1)}, u32[]{:S(2)}, u32[]{:S(2)}) collective-permute-start(bf16[32,1152]{0,1:T(8,128)(2,1)S(1)} %get-tuple-element.225), channel_id=1, source_target_pairs={{0,12},{4,8},{8,4},{12,0},{1,13},{5,9},{9,5},{13,1},{2,14},{6,10},... | collective-permute-start | bytes 221192 | tf_op jit(solution)/shard_map/ppermute | solution.py:145
  37.3 26.4 %collective-permute-start.4 = (bf16[32,1024]{0,1:T(8,128)(2,1)S(1)}, bf16[32,1024]{0,1:T(8,128)(2,1)}, u32[]{:S(2)}, u32[]{:S(2)}) collective-permute-start(bf16[32,1024]{0,1:T(8,128)(2,1)S(1)} %fusion.460), channel_id=1, source_target_pairs={{0,8},{4,12},{8,0},{12,4},{1,9},{5,13},{9,1},{13,5},{2,10},{6,14},... | collective-permute-start | bytes 196616 | tf_op jit(solution)/shard_map/ppermute | solution.py:69
  47.5 16.3 %collective-permute-start.5 = (bf16[32,1024]{0,1:T(8,128)(2,1)S(1)}, bf16[32,1024]{0,1:T(8,128)(2,1)}, u32[]{:S(2)}, u32[]{:S(2)}) collective-permute-start(bf16[32,1024]{0,1:T(8,128)(2,1)S(1)} %fusion.460), channel_id=1, source_target_pairs={{0,4},{4,0},{8,12},{12,8},{1,5},{5,1},{9,13},{13,9},{2,6},{6,2},{1... | collective-permute-start | bytes 196616 | tf_op jit(solution)/shard_map/ppermute | solution.py:69
  117.4 17.3 %collective-permute-start.8 = (bf16[32,1152]{0,1:T(8,128)(2,1)}, bf16[32,1152]{0,1:T(8,128)(2,1)}, u32[]{:S(2)}, u32[]{:S(2)}) collective-permute-start(bf16[32,1152]{0,1:T(8,128)(2,1)} %get-tuple-element.220), channel_id=1, source_target_pairs={{0,4},{4,0},{8,12},{12,8},{1,5},{5,1},{9,13},{13,9},{2,6},{6,2},{1... | collective-permute-start | bytes 221192 | tf_op jit(solution)/shard_map/ppermute | solution.py:145
  117.4 24.0 %collective-permute-start.9 = (bf16[32,1152]{0,1:T(8,128)(2,1)}, bf16[32,1152]{0,1:T(8,128)(2,1)}, u32[]{:S(2)}, u32[]{:S(2)}) collective-permute-start(bf16[32,1152]{0,1:T(8,128)(2,1)} %get-tuple-element.221), channel_id=1, source_target_pairs={{0,8},{4,12},{8,0},{12,4},{1,9},{5,13},{9,1},{13,5},{2,10},{6,14},... | collective-permute-start | bytes 221192 | tf_op jit(solution)/shard_map/ppermute | solution.py:145
  146.2 20.0 %collective-permute-start.12 = (bf16[32,1024]{0,1:T(8,128)(2,1)S(1)}, bf16[32,1024]{0,1:T(8,128)(2,1)S(1)}, u32[]{:S(2)}, u32[]{:S(2)}) collective-permute-start(bf16[32,1024]{0,1:T(8,128)(2,1)S(1)} %get-tuple-element.84), channel_id=1, source_target_pairs={{0,8},{4,12},{8,0},{12,4},{1,9},{5,13},{9,1},{13,5},{2,10},{6,14},... | collective-permute-start | bytes 196616 | tf_op jit(solution)/shard_map/ppermute | solution.py:69
  146.2 20.0 %collective-permute-start.13 = (bf16[32,1024]{0,1:T(8,128)(2,1)S(1)}, bf16[32,1024]{0,1:T(8,128)(2,1)S(1)}, u32[]{:S(2)}, u32[]{:S(2)}) collective-permute-start(bf16[32,1024]{0,1:T(8,128)(2,1)S(1)} %get-tuple-element.84), channel_id=1, source_target_pairs={{0,4},{4,0},{8,12},{12,8},{1,5},{5,1},{9,13},{13,9},{2,6},{6,2},{1... | collective-permute-start | bytes 196616 | tf_op jit(solution)/shard_map/ppermute | solution.py:69
  248.2 14.4 %collective-permute-start.16 = (bf16[32,1152]{0,1:T(8,128)(2,1)}, bf16[32,1152]{0,1:T(8,128)(2,1)}, u32[]{:S(2)}, u32[]{:S(2)}) collective-permute-start(bf16[32,1152]{0,1:T(8,128)(2,1)} %get-tuple-element.217), channel_id=1, source_target_pairs={{0,4},{4,0},{8,12},{12,8},{1,5},{5,1},{9,13},{13,9},{2,6},{6,2},{1... | collective-permute-start | bytes 221192 | tf_op jit(solution)/shard_map/ppermute | solution.py:145
  248.2 23.9 %collective-permute-start.17 = (bf16[32,1152]{0,1:T(8,128)(2,1)}, bf16[32,1152]{0,1:T(8,128)(2,1)}, u32[]{:S(2)}, u32[]{:S(2)}) collective-permute-start(bf16[32,1152]{0,1:T(8,128)(2,1)} %get-tuple-element.218), channel_id=1, source_target_pairs={{0,8},{4,12},{8,0},{12,4},{1,9},{5,13},{9,1},{13,5},{2,10},{6,14},... | collective-permute-start | bytes 221192 | tf_op jit(solution)/shard_map/ppermute | solution.py:145
  251.4 20.8 %collective-permute-start.18 = (bf16[32,1152]{0,1:T(8,128)(2,1)S(1)}, bf16[32,1152]{0,1:T(8,128)(2,1)}, u32[]{:S(2)}, u32[]{:S(2)}) collective-permute-start(bf16[32,1152]{0,1:T(8,128)(2,1)S(1)} %get-tuple-element.219), channel_id=1, source_target_pairs={{0,12},{4,8},{8,4},{12,0},{1,13},{5,9},{9,5},{13,1},{2,14},{6,10},... | collective-permute-start | bytes 221192 | tf_op jit(solution)/shard_map/ppermute | solution.py:145
  277.8 22.7 %collective-permute-start.20 = (bf16[32,1024]{0,1:T(8,128)(2,1)S(1)}, bf16[32,1024]{0,1:T(8,128)(2,1)S(1)}, u32[]{:S(2)}, u32[]{:S(2)}) collective-permute-start(bf16[32,1024]{0,1:T(8,128)(2,1)S(1)} %get-tuple-element.62), channel_id=1, source_target_pairs={{0,8},{4,12},{8,0},{12,4},{1,9},{5,13},{9,1},{13,5},{2,10},{6,14},... | collective-permute-start | bytes 196616 | tf_op jit(solution)/shard_map/ppermute | solution.py:69
  282.5 18.0 %collective-permute-start.21 = (bf16[32,1024]{0,1:T(8,128)(2,1)S(1)}, bf16[32,1024]{0,1:T(8,128)(2,1)S(1)}, u32[]{:S(2)}, u32[]{:S(2)}) collective-permute-start(bf16[32,1024]{0,1:T(8,128)(2,1)S(1)} %get-tuple-element.62), channel_id=1, source_target_pairs={{0,4},{4,0},{8,12},{12,8},{1,5},{5,1},{9,13},{13,9},{2,6},{6,2},{1... | collective-permute-start | bytes 196616 | tf_op jit(solution)/shard_map/ppermute | solution.py:69
  341.2 13.9 %collective-permute-start.24 = (bf16[32,1152]{0,1:T(8,128)(2,1)}, bf16[32,1152]{0,1:T(8,128)(2,1)}, u32[]{:S(2)}, u32[]{:S(2)}) collective-permute-start(bf16[32,1152]{0,1:T(8,128)(2,1)} %get-tuple-element.214), channel_id=1, source_target_pairs={{0,4},{4,0},{8,12},{12,8},{1,5},{5,1},{9,13},{13,9},{2,6},{6,2},{1... | collective-permute-start | bytes 221192 | tf_op jit(solution)/shard_map/ppermute | solution.py:145
  341.2 23.7 %collective-permute-start.25 = (bf16[32,1152]{0,1:T(8,128)(2,1)}, bf16[32,1152]{0,1:T(8,128)(2,1)}, u32[]{:S(2)}, u32[]{:S(2)}) collective-permute-start(bf16[32,1152]{0,1:T(8,128)(2,1)} %get-tuple-element.215), channel_id=1, source_target_pairs={{0,8},{4,12},{8,0},{12,4},{1,9},{5,13},{9,1},{13,5},{2,10},{6,14},... | collective-permute-start | bytes 221192 | tf_op jit(solution)/shard_map/ppermute | solution.py:145
  344.1 20.8 %collective-permute-start.26 = (bf16[32,1152]{0,1:T(8,128)(2,1)}, bf16[32,1152]{0,1:T(8,128)(2,1)}, u32[]{:S(2)}, u32[]{:S(2)}) collective-permute-start(bf16[32,1152]{0,1:T(8,128)(2,1)} %get-tuple-element.216), channel_id=1, source_target_pairs={{0,12},{4,8},{8,4},{12,0},{1,13},{5,9},{9,5},{13,1},{2,14},{6,10},... | collective-permute-start | bytes 221192 | tf_op jit(solution)/shard_map/ppermute | solution.py:145
  370.7 22.7 %collective-permute-start.28 = (bf16[32,1024]{0,1:T(8,128)(2,1)S(1)}, bf16[32,1024]{0,1:T(8,128)(2,1)S(1)}, u32[]{:S(2)}, u32[]{:S(2)}) collective-permute-start(bf16[32,1024]{0,1:T(8,128)(2,1)S(1)} %get-tuple-element.40), channel_id=1, source_target_pairs={{0,8},{4,12},{8,0},{12,4},{1,9},{5,13},{9,1},{13,5},{2,10},{6,14},... | collective-permute-start | bytes 196616 | tf_op jit(solution)/shard_map/ppermute | solution.py:69
  377.3 16.1 %collective-permute-start.29 = (bf16[32,1024]{0,1:T(8,128)(2,1)S(1)}, bf16[32,1024]{0,1:T(8,128)(2,1)S(1)}, u32[]{:S(2)}, u32[]{:S(2)}) collective-permute-start(bf16[32,1024]{0,1:T(8,128)(2,1)S(1)} %get-tuple-element.40), channel_id=1, source_target_pairs={{0,4},{4,0},{8,12},{12,8},{1,5},{5,1},{9,13},{13,9},{2,6},{6,2},{1... | collective-permute-start | bytes 196616 | tf_op jit(solution)/shard_map/ppermute | solution.py:69
  459.9 14.0 %collective-permute-start.32 = (bf16[32,1152]{0,1:T(8,128)(2,1)}, bf16[32,1152]{0,1:T(8,128)(2,1)}, u32[]{:S(2)}, u32[]{:S(2)}) collective-permute-start(bf16[32,1152]{0,1:T(8,128)(2,1)} %get-tuple-element.211), channel_id=1, source_target_pairs={{0,4},{4,0},{8,12},{12,8},{1,5},{5,1},{9,13},{13,9},{2,6},{6,2},{1... | collective-permute-start | bytes 221192 | tf_op jit(solution)/shard_map/ppermute | solution.py:145
  459.9 23.5 %collective-permute-start.33 = (bf16[32,1152]{0,1:T(8,128)(2,1)S(1)}, bf16[32,1152]{0,1:T(8,128)(2,1)}, u32[]{:S(2)}, u32[]{:S(2)}) collective-permute-start(bf16[32,1152]{0,1:T(8,128)(2,1)S(1)} %get-tuple-element.212), channel_id=1, source_target_pairs={{0,8},{4,12},{8,0},{12,4},{1,9},{5,13},{9,1},{13,5},{2,10},{6,14},... | collective-permute-start | bytes 221192 | tf_op jit(solution)/shard_map/ppermute | solution.py:145
  462.9 20.6 %collective-permute-start.34 = (bf16[32,1152]{0,1:T(8,128)(2,1)S(1)}, bf16[32,1152]{0,1:T(8,128)(2,1)}, u32[]{:S(2)}, u32[]{:S(2)}) collective-permute-start(bf16[32,1152]{0,1:T(8,128)(2,1)S(1)} %get-tuple-element.213), channel_id=1, source_target_pairs={{0,12},{4,8},{8,4},{12,0},{1,13},{5,9},{9,5},{13,1},{2,14},{6,10},... | collective-permute-start | bytes 221192 | tf_op jit(solution)/shard_map/ppermute | solution.py:145
  488.3 22.7 %collective-permute-start.36 = (bf16[32,1024]{0,1:T(8,128)(2,1)S(1)}, bf16[32,1024]{0,1:T(8,128)(2,1)S(1)}, u32[]{:S(2)}, u32[]{:S(2)}) collective-permute-start(bf16[32,1024]{0,1:T(8,128)(2,1)S(1)} %subtract_convert_fusion), channel_id=1, source_target_pairs={{0,8},{4,12},{8,0},{12,4},{1,9},{5,13},{9,1},{13,5},{2,10},{6,14},... | collective-permute-start | bytes 196616 | tf_op jit(solution)/shard_map/ppermute | solution.py:69
  495.5 15.5 %collective-permute-start.37 = (bf16[32,1024]{0,1:T(8,128)(2,1)S(1)}, bf16[32,1024]{0,1:T(8,128)(2,1)S(1)}, u32[]{:S(2)}, u32[]{:S(2)}) collective-permute-start(bf16[32,1024]{0,1:T(8,128)(2,1)S(1)} %subtract_convert_fusion), channel_id=1, source_target_pairs={{0,4},{4,0},{8,12},{12,8},{1,5},{5,1},{9,13},{13,9},{2,6},{6,2},{1... | collective-permute-start | bytes 196616 | tf_op jit(solution)/shard_map/ppermute | solution.py:69
  (130 other events, 1826.3 us)

commit v2 on v0

v2 whole, which is shorter than its diff:
```python
import functools

import jax
import jax.numpy as jnp
from jax import lax
from jax.experimental import pallas as pl
from jax.experimental.pallas import tpu as pltpu
from jax.sharding import PartitionSpec as P

GRID = 128
ITERS = 5
LANES = 128
EDGE = 2 * GRID
SLOTS = 8
BF16 = jnp.bfloat16
F32 = jnp.float32

GRAD_SQ, SMOOTH_SQ, CROSS = 0, 1, 2
IMAGE_SQ = 2
STEP = 3


def xor_pairs(count, offset):
    return [(i, i ^ offset) for i in range(count)]


def tree_sum(parts):
    while len(parts) > 1:
        parts = [parts[i] + parts[i + 1] for i in range(0, len(parts), 2)]
    return parts[0]


def lane_ids(sets):
    return lax.broadcasted_iota(jnp.int32, (sets, LANES), 1)


def beside(row):
    lane = lane_ids(row.shape[0])
    left = jnp.where(lane == 0, 0.0, pltpu.roll(row, 1, 1))
    right = jnp.where(lane == LANES - 1, 0.0, pltpu.roll(row, LANES - 1, 1))
    return left + right


def smooth_row(above, row, below):
    near = beside(row)
    if above is not None:
        near = near + above
    if below is not None:
        near = near + below
    return row - 0.25 * near


def lanes_of(columns, sets):
    lane = lane_ids(sets)
    block = jnp.zeros((sets, LANES), F32)
    for slot, column in columns.items():
        block = jnp.where(lane == slot, column, block)
    return block


def pack(block):
    block = jnp.where(lane_ids(block.shape[0]) < SLOTS, block, 0.0)
    high = block.astype(BF16).astype(F32)
    rest = block - high
    mid = rest.astype(BF16).astype(F32)
    low = (rest - mid).astype(BF16).astype(F32)
    return (high + pltpu.roll(mid, SLOTS, 1) + pltpu.roll(low, 2 * SLOTS, 1)).astype(BF16)


def unpack(packed):
    block = packed.astype(F32)
    mid = pltpu.roll(block, LANES - SLOTS, 1)
    low = pltpu.roll(block, LANES - 2 * SLOTS, 1)
    return jnp.where(lane_ids(block.shape[0]) < SLOTS, (block + mid) + low, 0.0)


def row_of(values, index):
    return values[:, index * GRID : (index + 1) * GRID]


def seam(lower, upper):
    low0, low1, up0, up1 = row_of(lower, 0), row_of(lower, 1), row_of(upper, 0), row_of(upper, 1)
    cross = smooth_row(low0, low1, None) * up0 + smooth_row(None, up0, up1) * low1
    return jnp.sum(0.0625 * (up0 * up0 + low1 * low1) - 0.5 * cross, axis=1, keepdims=True)


def merge(mine_ref, got_ref, above, below, pixels, step, tile):
    upper_side = (tile // step) % 2 == 1
    inside = tile % step
    scalar_at, row_at = pl.ds(pixels, LANES), pl.ds(pixels + LANES, 2 * EDGE)
    if mine_ref.dtype == F32:
        mine, got = mine_ref[:, scalar_at], got_ref[:, scalar_at]
    else:
        mine, got = unpack(mine_ref[:, scalar_at]), unpack(got_ref[:, scalar_at])
    edges, got_edges = mine_ref[:, row_at].astype(F32), got_ref[:, row_at].astype(F32)
    first = jnp.where(upper_side, got_edges[:, :EDGE], edges[:, :EDGE])
    last = jnp.where(upper_side, edges[:, EDGE:], got_edges[:, EDGE:])
    lower_last = jnp.where(upper_side, got_edges[:, EDGE:], edges[:, EDGE:])
    upper_first = jnp.where(upper_side, edges[:, :EDGE], got_edges[:, :EDGE])
    sets = mine.shape[0]
    scalars = mine + got + lanes_of({SMOOTH_SQ: seam(lower_last, upper_first)}, sets)
    above = jnp.where(upper_side & (inside == 0), lower_last, above)
    below = jnp.where(jnp.logical_not(upper_side) & (inside == step - 1), upper_first, below)
    value = mine_ref[:, :pixels].astype(F32) + got_ref[:, :pixels].astype(F32)
    return value, scalars, first, last, above, below


def forward_kernel(n_shards, first_sweep, *refs):
    shards, refs = refs[:n_shards], refs[n_shards:]
    if first_sweep:
        green, whole, message = refs
    else:
        twice, green, whole, message = refs
    sets, cells = whole.shape
    width = cells // n_shards
    pixels = green.shape[0]
    here = lax.axis_index("pix")
    image = jnp.zeros((sets, pixels), F32)
    for offset, shard in enumerate(shards):
        at = pl.ds(pl.multiple_of((here ^ offset if n_shards > 1 else 0) * width, LANES), width)
        value = shard[...]
        whole[:, at] = value
        image += lax.dot_general(value, green[:, at], (((1,), (1,)), ((), ())), preferred_element_type=F32)
    message[:, :pixels] = image
    rows = cells // GRID
    grad_sq = jnp.zeros((sets, LANES), F32)
    smooth_sq = jnp.zeros((sets, LANES), F32)
    cross = jnp.zeros((sets, LANES), F32)
    above, row = None, whole[:, :GRID].astype(F32)
    for r in range(rows):
        below = whole[:, (r + 1) * GRID : (r + 2) * GRID].astype(F32) if r + 1 < rows else None
        alone = smooth_row(above, row, below)
        grad_sq += row * row
        smooth_sq += alone * alone
        if not first_sweep:
            cross += row * twice[:, r * GRID : (r + 1) * GRID]
        above, row = row, below
    columns = {GRAD_SQ: jnp.sum(grad_sq, axis=1, keepdims=True), SMOOTH_SQ: jnp.sum(smooth_sq, axis=1, keepdims=True)}
    if not first_sweep:
        columns[CROSS] = jnp.sum(cross, axis=1, keepdims=True)
    message[:, pixels : pixels + LANES] = lanes_of(columns, sets)
    message[:, pixels + LANES : pixels + LANES + EDGE] = whole[:, :EDGE].astype(F32)
    message[:, pixels + LANES + EDGE :] = whole[:, cells - EDGE :].astype(F32)


def middle_kernel(step, *refs):
    if step == 1:
        mine, got, message, above, below = refs
        old_above = old_below = jnp.zeros(above.shape, F32)
    else:
        mine, got, above_in, below_in, message, above, below = refs
        old_above, old_below = above_in[...], below_in[...]
    pixels = mine.shape[1] - LANES - 2 * EDGE
    value, scalars, first, last, up, down = merge(mine, got, old_above, old_below, pixels, step, lax.axis_index("par"))
    message[:, :pixels] = value.astype(BF16)
    message[:, pixels : pixels + LANES] = pack(scalars)
    message[:, pixels + LANES : pixels + LANES + EDGE] = first.astype(BF16)
    message[:, pixels + LANES + EDGE :] = last.astype(BF16)
    above[...] = up
    below[...] = down


def advance(step, n_par, first_sweep, need_twice, refs):
    mine, got, above_in, below_in, whole, old_scalars, old_image, old_direction, scalars, image, direction, once, twice = refs
    tile = lax.axis_index("par")
    sets, pixels = image.shape
    cells = whole.shape[1]
    rows = cells // GRID
    value, sums, _, _, above, below = merge(mine, got, above_in[...], below_in[...], pixels, step, tile)
    grad_sq = sums[:, GRAD_SQ : GRAD_SQ + 1]
    smooth_sq = sums[:, SMOOTH_SQ : SMOOTH_SQ + 1]
    if first_sweep:
        image[...] = value
        direction[:, :EDGE] = above
        direction[:, EDGE : EDGE + cells] = whole[...].astype(F32)
        direction[:, EDGE + cells :] = below
    else:
        beta = grad_sq / old_scalars[:, GRAD_SQ : GRAD_SQ + 1]
        old_smooth = old_scalars[:, SMOOTH_SQ : SMOOTH_SQ + 1]
        smooth_sq = smooth_sq + beta * (2.0 * sums[:, CROSS : CROSS + 1] + beta * old_smooth)
        image[...] = value + beta * old_image[...]
        direction[:, :EDGE] = above + beta * old_direction[:, :EDGE]
        direction[:, EDGE : EDGE + cells] = whole[...].astype(F32) + beta * old_direction[:, EDGE : EDGE + cells]
        direction[:, EDGE + cells :] = below + beta * old_direction[:, EDGE + cells :]
    image_sq = jnp.zeros((sets, LANES), F32)
    for at in range(0, pixels, LANES):
        part = image[:, at : at + LANES]
        image_sq += part * part
    image_sq = jnp.sum(image_sq, axis=1, keepdims=True)
    scalars[...] = lanes_of({GRAD_SQ: grad_sq, SMOOTH_SQ: smooth_sq, IMAGE_SQ: image_sq}, sets)
    if need_twice:
        def direction_row(r):
            return direction[:, r * GRID : (r + 1) * GRID]

        for r in range(rows + 2):
            row = smooth_row(direction_row(r), direction_row(r + 1), direction_row(r + 2))
            if r == 0:
                row = jnp.where(tile == 0, 0.0, row)
            if r == rows + 1:
                row = jnp.where(tile == n_par - 1, 0.0, row)
            once[:, r * GRID : (r + 1) * GRID] = row

        def once_row(r):
            return once[:, r * GRID : (r + 1) * GRID]

        for r in range(rows):
            twice[:, r * GRID : (r + 1) * GRID] = smooth_row(once_row(r), once_row(r + 1), once_row(r + 2))
    return grad_sq, smooth_sq, image_sq


def send_blocks(image, green, blocks, own, missed, lost, guess, tail):
    here = lax.axis_index("pix")
    width = own.shape[1]
    for offset in range(len(blocks), -1, -1):
        at = pl.ds(pl.multiple_of((here ^ offset) * width, LANES), width)
        part = jnp.dot(image, green[:, at], preferred_element_type=F32)
        if offset == 0:
            own[...] = part
            missed[:, at] = jnp.zeros_like(part)
        else:
            aimed = part if lost is None else part - guess * lost[:, at]
            sent = aimed.astype(BF16)
            blocks[offset - 1][:, :width] = sent
            missed[:, at] = part - sent.astype(F32)
            if tail is not None:
                blocks[offset - 1][:, width:] = tail


def backward_kernel(step, n_pix, n_par, first_sweep, direct, *refs):
    refs = list(refs)
    green = refs.pop(0)
    lost = refs.pop(0) if direct else None
    mine, got, above, below, whole = refs[:5]
    refs = refs[5:]
    if first_sweep:
        olds = [None] * 3
    else:
        olds, refs = refs[:3], refs[3:]
    scalars, image, direction, twice = refs[:4]
    once = refs[-1]
    refs = refs[4:-1]
    sums = advance(
        step, n_par, first_sweep, True,
        [mine, got, above, below, whole, *olds, scalars, image, direction, once, twice],
    )
    rounded = image[...].astype(BF16)
    if not direct:
        refs[0][...] = jnp.dot(rounded, green[...], preferred_element_type=F32)
        return
    grad_sq, smooth_sq, image_sq = sums
    guess = (n_pix * image_sq + smooth_sq) / grad_sq
    own, missed, blocks = refs[0], refs[1], refs[2:]
    send_blocks(rounded, green, blocks, own, missed, lost, guess, pack(scalars[...]))
    width = own.shape[1]
    at = pl.ds(pl.multiple_of(lax.axis_index("pix") * width, LANES), width)
    own[...] += twice[:, at]


def last_kernel(step, n_par, *refs):
    ins, (scalars, image, direction) = refs[:8], refs[8:]
    advance(step, n_par, False, False, [*ins, scalars, image, direction, None, None])


def start_kernel(observed, green, own, missed, *blocks):
    send_blocks(observed[...], green, blocks, own, missed, None, None, None)


def receive_start_kernel(n_got, own, *refs):
    got, (grad, rounded) = refs[:n_got], refs[n_got:]
    value = tree_sum([own[...]] + [ref[...].astype(F32) for ref in got])
    grad[...] = value
    rounded[...] = value.astype(BF16)


def step_length(scalars, totals):
    image_sq = tree_sum(totals)[:, IMAGE_SQ : IMAGE_SQ + 1]
    return scalars[:, GRAD_SQ : GRAD_SQ + 1] / (image_sq + scalars[:, SMOOTH_SQ : SMOOTH_SQ + 1])


def receive_kernel(n_got, own, scalars, old_grad, *refs):
    got, (grad, rounded, length) = refs[:n_got], refs[n_got:]
    width = own.shape[1]
    mine = scalars[...]
    step_len = step_length(mine, [mine] + [unpack(ref[:, width:]) for ref in got])
    change = tree_sum([own[...]] + [ref[:, :width].astype(F32) for ref in got])
    value = old_grad[...] - step_len * change
    grad[...] = value
    rounded[...] = value.astype(BF16)
    length[...] = jnp.broadcast_to(step_len, length.shape)


def update_kernel(has_lost, length, direction, image, solution, residual, *refs):
    step_len = length[:, :1]
    if has_lost:
        lost, missed, new_solution, new_residual, new_lost = refs
        new_lost[...] = lost[...] - step_len * missed[...]
    else:
        new_solution, new_residual = refs
    cells = solution.shape[1]
    new_solution[...] = solution[...] + step_len * direction[:, EDGE : EDGE + cells]
    new_residual[...] = residual[...] - step_len * image[...]


def finish_kernel(n_got, *refs):
    scalars, got = refs[0], refs[1 : 1 + n_got]
    direction, image, solution, residual, new_solution, new_residual = refs[1 + n_got :]
    mine = scalars[...]
    step_len = step_length(mine, [mine] + [ref[...] for ref in got])
    cells = solution.shape[1]
    new_solution[...] = solution[...] + step_len * direction[:, EDGE : EDGE + cells]
    new_residual[...] = residual[...] - step_len * image[...]


def call(kernel, operands, outs, scratch=(), flops=0, limit=24 << 20):
    vmem = pl.BlockSpec(memory_space=pltpu.VMEM)
    shapes = [jax.ShapeDtypeStruct(*out) for out in outs]
    moved = sum(x.size * x.dtype.itemsize for x in [*operands, *shapes])
    return pl.pallas_call(
        kernel,
        in_specs=[vmem] * len(operands),
        out_specs=[vmem] * len(outs),
        out_shape=shapes,
        scratch_shapes=list(scratch),
        compiler_params=pltpu.CompilerParams(vmem_limit_bytes=limit),
        cost_estimate=pl.CostEstimate(flops=flops or moved, bytes_accessed=moved, transcendentals=0),
    )(*operands)


def exchange(blocks, axis, count):
    return [lax.ppermute(block, axis, xor_pairs(count, k + 1)) for k, block in enumerate(blocks)]


def on_device(green, observed):
    sets = observed.shape[0]
    pixels, cells = green.shape
    n_pix, n_par = lax.axis_size("pix"), lax.axis_size("par")
    here = lax.axis_index("pix")
    width = cells // n_pix
    direct = n_pix <= 8 and width % LANES == 0
    flops = 2 * sets * pixels * cells
    block, shard = ((sets, width + LANES), BF16), ((sets, width), F32)
    scalar = ((sets, LANES), F32)
    line, wide, edge = ((sets, pixels), F32), ((sets, cells), F32), ((sets, EDGE), F32)
    ring = ((sets, cells + 2 * EDGE), F32)

    def gather(rounded):
        if direct:
            return [rounded] + exchange([rounded] * (n_pix - 1), "pix", n_pix)
        return [lax.all_gather(rounded, "pix", axis=1, tiled=True)]

    lost = None
    if direct:
        own, lost, *blocks = call(
            start_kernel, [observed, green], [shard, wide] + [((sets, width), BF16)] * (n_pix - 1), flops=flops
        )
        got = exchange(blocks, "pix", n_pix)
    else:
        partial = jnp.dot(observed, green, preferred_element_type=F32)
        own, got = lax.psum_scatter(partial, "pix", scatter_dimension=1, tiled=True), []
    grad, rounded = call(
        functools.partial(receive_start_kernel, len(got)), [own, *got], [shard, ((sets, width), BF16)]
    )
    solution = jnp.zeros((sets, cells), F32)
    residual = observed.astype(F32)
    scalars = image = direction = twice = None
    for sweep in range(ITERS):
        shards = gather(rounded)
        first, final = sweep == 0, sweep + 1 == ITERS
        length_of = pixels + LANES + 2 * EDGE
        whole, message = call(
            functools.partial(forward_kernel, len(shards), first),
            [*shards, *([] if first else [twice]), green],
            [((sets, cells), BF16), ((sets, length_of), F32)],
            flops=flops,
        )
        step, above, below = 1, None, None
        while True:
            got = lax.ppermute(message, "par", xor_pairs(n_par, step))
            if 2 * step >= n_par:
                break
            message, above, below = call(
                functools.partial(middle_kernel, step),
                [message, got, *([] if step == 1 else [above, below])],
                [((sets, length_of), BF16), edge, edge],
            )
            step *= 2
        if above is None:
            above = below = jnp.zeros(edge[0], F32)
        ins = [message, got, above, below, whole, *([] if first else [scalars, image, direction])]
        if final:
            scalars, image, direction = call(
                functools.partial(last_kernel, step, n_par), ins, [scalar, line, ring]
            )
            if direct:
                got = exchange([scalars] * (n_pix - 1), "pix", n_pix)
            else:
                got = []
                scalars = scalars.at[:, IMAGE_SQ].set(lax.psum(scalars[:, IMAGE_SQ], "pix"))
            return tuple(
                call(
                    functools.partial(finish_kernel, len(got)),
                    [scalars, *got, direction, image, solution, residual],
                    [wide, line],
                )
            )
        kernel = functools.partial(backward_kernel, step, n_pix, n_par, first, direct)
        scratch = [pltpu.VMEM((sets, cells + EDGE), F32)]
        outs = [scalar, line, ring, wide]
        if direct:
            scalars, image, direction, twice, own, missed, *blocks = call(
                kernel, [green, lost, *ins], outs + [shard, wide] + [block] * (n_pix - 1), scratch, flops
            )
            got = exchange(blocks, "pix", n_pix)
        else:
            scalars, image, direction, twice, partial = call(kernel, [green, *ins], outs + [wide], scratch, flops)
            own = lax.psum_scatter(partial, "pix", scatter_dimension=1, tiled=True)
            own = own + lax.dynamic_slice_in_dim(twice, here * width, width, axis=1)
            image_sq = lax.psum(scalars[:, IMAGE_SQ], "pix")
            scalars = scalars.at[:, IMAGE_SQ].set(image_sq)
            got = []
        grad, rounded, length = call(
            functools.partial(receive_kernel, len(got)),
            [own, scalars, grad, *got],
            [shard, ((sets, width), BF16), scalar],
        )
        tail = call(
            functools.partial(update_kernel, direct),
            [length, direction, image, solution, residual, *([lost, missed] if direct else [])],
            [wide, line] + ([wide] if direct else []),
        )
        solution, residual = tail[:2]
        lost = tail[2] if direct else None


def solution(mesh):
    return jax.shard_map(
        on_device,
        mesh=mesh,
        in_specs=(P("pix", "par"), P("parts", "pix")),
        out_specs=(P("parts", "par"), P("parts", "pix")),
        check_vma=False,
    )
```

time: 559 us -> 161 us (0.29)
  waiting for transfers between devices: 294 us -> 67.3 us
  blocking collectives: 123 us -> 0 us
  matrix products: 67.6 us -> 0 us
  starting transfers between devices: 25.8 us -> 57.5 us
  Pallas kernels: 0 us -> 30.9 us
  other arithmetic: 30.8 us -> 0.01 us
  between operations: 14.8 us -> 0.78 us
    psum x10 -> x0, waiting for transfers between devices: 281 us -> none  [the longest x5 160 us: backward_sum(): lax.psum(jnp.dot(rounded, green_matrix, preferred_element_type=jnp.float3...]
    psum x14 -> x0, blocking collectives: 123 us -> none  [the longest x5 58.5 us: curvatures(): image_sq = lax.psum(local_image, 'pix')]
    dot_general x10 -> x0, matrix products: 67.6 us -> none  [the longest x5 36.2 us: forward(): lax.dot_general(rounded, green_matrix, (((1,), (1,)), ((), ())), preferre...]
    ppermute x18 -> x43, waiting for transfers between devices: 13.2 us -> 67.3 us  [the longest x33 42.2 us: exchange(): lax.ppermute(block, axis, xor_pairs(count, k + 1))]
    ppermute x18 -> x43, starting transfers between devices: 25.4 us -> 57.5 us  [the longest x33 50 us: exchange(): lax.ppermute(block, axis, xor_pairs(count, k + 1))]
    pallas_call x0 -> x26, Pallas kernels: none -> 30.9 us  [call(): pl.pallas_call(kernel, in_specs=[vmem] * len(operands), out_specs=[vmem]...]
    reduce_sum x15 -> x0, other arithmetic: 16 us -> none  [the longest x5 7.39 us: column_squares(): return lax.psum(jnp.sum(gradient * gradient, axis=1), 'par')]
  transfers between devices with their start and end apart: 28 -> 43, of which waited for: 14 -> 36; matrix products, arithmetic and copies ran while one was open for 8% -> 0% of each run, Pallas kernels for 0% -> 1%
where the time goes in v2:
time: 161 us
  waiting for transfers between devices  67.3 us (42%)
  starting transfers between devices  57.5 us (36%)
  Pallas kernels  30.9 us (19%)
  local copies, waits for them, and re-layouts  4.6 us (3%)
    ppermute x33, starting transfers between devices, exchange(): lax.ppermute(block, axis, xor_pairs(count, k + 1))  50 us
    ppermute x33, waiting for transfers between devices, exchange(): lax.ppermute(block, axis, xor_pairs(count, k + 1))  42.2 us
    pallas_call x26, Pallas kernels, call(): pl.pallas_call(kernel, in_specs=[vmem] * len(operands), out_specs=[vmem]...  30.9 us
    ppermute x10, waiting for transfers between devices, on_device(): got = lax.ppermute(message, 'par', xor_pairs(n_par, step))  25.1 us
    ppermute x10, starting transfers between devices, on_device(): got = lax.ppermute(message, 'par', xor_pairs(n_par, step))  7.49 us
    unnamed x8, local copies, waits for them, and re-layouts  4.56 us
  transfers between devices with their start and end apart: 43, of which 36 were waited for; matrix products, arithmetic and copies ran while one was open for 0% of the time, Pallas kernels for 1%

profile of v2, /device:TPU:0, one launch (start us, length us, event | category | flops | bytes accessed | tf_op | source)
XLA Modules:
  0.0 161.1 jit_solution(5567264369377305207)
XLA Ops:
  0.6 3.7 %copy-done = bf16[1152,4096]{1,0:T(8,128)(2,1)S(1)} copy-done((bf16[1152,4096]{1,0:T(8,128)(2,1)S(1)}, bf16[1152,4096]{1,0:T(8,128)(2,1)}, u32[]{:S(2)}) %copy-start) | copy-done | bytes 9437208
  6.9 3.1 %collective-permute-start = (bf16[32,1024]{1,0:T(8,128)(2,1)S(1)}, bf16[32,1024]{1,0:T(8,128)(2,1)S(1)}, u32[]{:S(2)}, u32[]{:S(2)}) collective-permute-start(bf16[32,1024]{1,0:T(8,128)(2,1)S(1)} %get-tuple-element.97), channel_id=1, source_target_pairs={{0,4},{4,0},{8,12},{12,8},{1,5},{5,1},{9,13},{13,9},{2,6},{6,2},{1... | collective-permute-start | bytes 196616 | tf_op jit(solution)/shard_map/ppermute | solution.py:330
  10.0 2.6 %collective-permute-start.1 = (bf16[32,1024]{1,0:T(8,128)(2,1)S(1)}, bf16[32,1024]{1,0:T(8,128)(2,1)S(1)}, u32[]{:S(2)}, u32[]{:S(2)}) collective-permute-start(bf16[32,1024]{1,0:T(8,128)(2,1)S(1)} %get-tuple-element.98), channel_id=1, source_target_pairs={{0,8},{4,12},{8,0},{12,4},{1,9},{5,13},{9,1},{13,5},{2,10},{6,14},... | collective-permute-start | bytes 196616 | tf_op jit(solution)/shard_map/ppermute | solution.py:330
  12.6 4.7 %collective-permute-done.1.refs_1_ = bf16[32,1024]{1,0:T(8,128)(2,1)S(1)} collective-permute-done((bf16[32,1024]{1,0:T(8,128)(2,1)S(1)}, bf16[32,1024]{1,0:T(8,128)(2,1)S(1)}, u32[]{:S(2)}, u32[]{:S(2)}) %collective-permute-start.1) | collective-permute-done | bytes 65568 | tf_op jit(solution)/shard_map/ppermute | solution.py:330
  20.6 2.6 %collective-permute-start.3 = (bf16[32,1024]{1,0:T(8,128)(2,1)S(1)}, bf16[32,1024]{1,0:T(8,128)(2,1)S(1)}, u32[]{:S(2)}, u32[]{:S(2)}) collective-permute-start(bf16[32,1024]{1,0:T(8,128)(2,1)S(1)} %get-tuple-element.100.refs_0_), channel_id=1, source_target_pairs={{0,4},{4,0},{8,12},{12,8},{1,5},{5,1},{9,13},{13,9},{2,6},{6,2},{1... | collective-permute-start | bytes 196616 | tf_op jit(solution)/shard_map/ppermute | solution.py:330
  26.3 2.9 %shard_map.43 = (bf16[32,4096]{1,0:T(8,128)(2,1)S(1)}, f32[32,1792]{1,0:T(8,128)S(1)}) custom-call(bf16[32,1024]{1,0:T(8,128)(2,1)S(1)} %get-tuple-element.100.refs_0_, bf16[32,1024]{1,0:T(8,128)(2,1)S(1)} %collective-permute-done.3.refs_1_, bf16[32,1024]{1,0:T(8,128)(2,1)S(1)} %collective-permute-done.4.refs_2_, ...), custom_call_target="tpu_custom_call" | custom-call | flops 301989888 | bytes 10190848 | tf_op jit(solution)/shard_map/pallas_call | solution.py:318
  32.4 3.7 %collective-permute-done.7.refs_3_ = bf16[32,1792]{1,0:T(8,128)(2,1)S(1)} collective-permute-done((bf16[32,1792]{1,0:T(8,128)(2,1)S(1)}, bf16[32,1792]{1,0:T(8,128)(2,1)S(1)}, u32[]{:S(2)}, u32[]{:S(2)}) %collective-permute-start.7) | collective-permute-done | bytes 114720 | tf_op jit(solution)/shard_map/ppermute | solution.py:378
  42.8 4.4 %collective-permute-done.9.refs_1_ = bf16[32,1152]{1,0:T(8,128)(2,1)S(1)} collective-permute-done((bf16[32,1152]{1,0:T(8,128)(2,1)S(1)}, bf16[32,1152]{1,0:T(8,128)(2,1)S(1)}, u32[]{:S(2)}, u32[]{:S(2)}) %collective-permute-start.9) | collective-permute-done | bytes 73760 | tf_op jit(solution)/shard_map/ppermute | solution.py:330
  55.3 2.9 %shard_map.48 = (bf16[32,4096]{1,0:T(8,128)(2,1)S(1)}, f32[32,1792]{1,0:T(8,128)S(1)}) custom-call(bf16[32,1024]{1,0:T(8,128)(2,1)S(1)} %get-tuple-element.117.refs_0_, bf16[32,1024]{1,0:T(8,128)(2,1)S(1)} %collective-permute-done.11.refs_1_, bf16[32,1024]{1,0:T(8,128)(2,1)S(1)} %collective-permute-done.12.refs_2_, ...), custom_call_target="tpu_custom_call" | custom-call | flops 301989888 | bytes 10715136 | tf_op jit(solution)/shard_map/pallas_call | solution.py:318
  61.8 3.4 %collective-permute-done.15.refs_3_ = bf16[32,1792]{1,0:T(8,128)(2,1)S(1)} collective-permute-done((bf16[32,1792]{1,0:T(8,128)(2,1)S(1)}, bf16[32,1792]{1,0:T(8,128)(2,1)S(1)}, u32[]{:S(2)}, u32[]{:S(2)}) %collective-permute-start.15) | collective-permute-done | bytes 114720 | tf_op jit(solution)/shard_map/ppermute | solution.py:378
  65.2 2.1 %shard_map.50 = (f32[32,128]{1,0:T(8,128)S(1)}, f32[32,1152]{1,0:T(8,128)S(1)}, f32[32,4608]{1,0:T(8,128)S(1)}, f32[32,4096]{1,0:T(8,128)S(1)}, f32[32,1024]{1,0...) custom-call(bf16[1152,4096]{1,0:T(8,128)(2,1)S(1)} %copy-done.1, ...), custom_call_target="tpu_custom_call" | custom-call | flops 301989888 | bytes 13426688 | tf_op jit(solution)/shard_map/pallas_call | solution.py:318
  69.7 2.0 %collective-permute-start.18 = (bf16[32,1152]{1,0:T(8,128)(2,1)S(1)}, bf16[32,1152]{1,0:T(8,128)(2,1)S(1)}, u32[]{:S(2)}, u32[]{:S(2)}) collective-permute-start(bf16[32,1152]{1,0:T(8,128)(2,1)S(1)} %get-tuple-element.129), channel_id=1, source_target_pairs={{0,12},{4,8},{8,4},{12,0},{1,13},{5,9},{9,5},{13,1},{2,14},{6,10},... | collective-permute-start | bytes 221192 | tf_op jit(solution)/shard_map/ppermute | solution.py:330
  72.3 3.9 %collective-permute-done.17.refs_1_ = bf16[32,1152]{1,0:T(8,128)(2,1)S(1)} collective-permute-done((bf16[32,1152]{1,0:T(8,128)(2,1)S(1)}, bf16[32,1152]{1,0:T(8,128)(2,1)S(1)}, u32[]{:S(2)}, u32[]{:S(2)}) %collective-permute-start.17) | collective-permute-done | bytes 73760 | tf_op jit(solution)/shard_map/ppermute | solution.py:330
  84.3 2.9 %shard_map.53 = (bf16[32,4096]{1,0:T(8,128)(2,1)S(1)}, f32[32,1792]{1,0:T(8,128)S(1)}) custom-call(bf16[32,1024]{1,0:T(8,128)(2,1)S(1)} %get-tuple-element.137.refs_0_, bf16[32,1024]{1,0:T(8,128)(2,1)S(1)} %collective-permute-done.19.refs_1_, bf16[32,1024]{1,0:T(8,128)(2,1)S(1)} %collective-permute-done.20.refs_2_, ...), custom_call_target="tpu_custom_call" | custom-call | flops 301989888 | bytes 10715136 | tf_op jit(solution)/shard_map/pallas_call | solution.py:318
  90.8 3.5 %collective-permute-done.23.refs_3_ = bf16[32,1792]{1,0:T(8,128)(2,1)S(1)} collective-permute-done((bf16[32,1792]{1,0:T(8,128)(2,1)S(1)}, bf16[32,1792]{1,0:T(8,128)(2,1)S(1)}, u32[]{:S(2)}, u32[]{:S(2)}) %collective-permute-start.23) | collective-permute-done | bytes 114720 | tf_op jit(solution)/shard_map/ppermute | solution.py:378
  94.2 2.1 %shard_map.55 = (f32[32,128]{1,0:T(8,128)S(1)}, f32[32,1152]{1,0:T(8,128)S(1)}, f32[32,4608]{1,0:T(8,128)S(1)}, f32[32,4096]{1,0:T(8,128)S(1)}, f32[32,1024]{1,0...) custom-call(bf16[1152,4096]{1,0:T(8,128)(2,1)S(1)} %copy-done.1, ...), custom_call_target="tpu_custom_call" | custom-call | flops 301989888 | bytes 13426688 | tf_op jit(solution)/shard_map/pallas_call | solution.py:318
  101.4 3.9 %collective-permute-done.25.refs_1_ = bf16[32,1152]{1,0:T(8,128)(2,1)S(1)} collective-permute-done((bf16[32,1152]{1,0:T(8,128)(2,1)S(1)}, bf16[32,1152]{1,0:T(8,128)(2,1)S(1)}, u32[]{:S(2)}, u32[]{:S(2)}) %collective-permute-start.25) | collective-permute-done | bytes 73760 | tf_op jit(solution)/shard_map/ppermute | solution.py:330
  113.4 2.9 %shard_map.58 = (bf16[32,4096]{1,0:T(8,128)(2,1)S(1)}, f32[32,1792]{1,0:T(8,128)S(1)}) custom-call(bf16[32,1024]{1,0:T(8,128)(2,1)S(1)} %get-tuple-element.157.refs_0_, bf16[32,1024]{1,0:T(8,128)(2,1)S(1)} %collective-permute-done.27.refs_1_, bf16[32,1024]{1,0:T(8,128)(2,1)S(1)} %collective-permute-done.28.refs_2_, ...), custom_call_target="tpu_custom_call" | custom-call | flops 301989888 | bytes 10715136 | tf_op jit(solution)/shard_map/pallas_call | solution.py:318
  119.8 3.5 %collective-permute-done.31.refs_3_ = bf16[32,1792]{1,0:T(8,128)(2,1)S(1)} collective-permute-done((bf16[32,1792]{1,0:T(8,128)(2,1)S(1)}, bf16[32,1792]{1,0:T(8,128)(2,1)S(1)}, u32[]{:S(2)}, u32[]{:S(2)}) %collective-permute-start.31) | collective-permute-done | bytes 114720 | tf_op jit(solution)/shard_map/ppermute | solution.py:378
  123.3 2.1 %shard_map.60 = (f32[32,128]{1,0:T(8,128)S(1)}, f32[32,1152]{1,0:T(8,128)S(1)}, f32[32,4608]{1,0:T(8,128)S(1)}, f32[32,4096]{1,0:T(8,128)S(1)}, f32[32,1024]{1,0...) custom-call(bf16[1152,4096]{1,0:T(8,128)(2,1)S(1)} %copy-done.1, ...), custom_call_target="tpu_custom_call" | custom-call | flops 301989888 | bytes 13426688 | tf_op jit(solution)/shard_map/pallas_call | solution.py:318
  130.4 3.9 %collective-permute-done.33.refs_1_ = bf16[32,1152]{1,0:T(8,128)(2,1)S(1)} collective-permute-done((bf16[32,1152]{1,0:T(8,128)(2,1)S(1)}, bf16[32,1152]{1,0:T(8,128)(2,1)S(1)}, u32[]{:S(2)}, u32[]{:S(2)}) %collective-permute-start.33) | collective-permute-done | bytes 73760 | tf_op jit(solution)/shard_map/ppermute | solution.py:330
  143.0 3.0 %shard_map.62 = (bf16[32,4096]{1,0:T(8,128)(2,1)S(1)}, f32[32,1792]{1,0:T(8,128)S(1)}) custom-call(bf16[32,1024]{1,0:T(8,128)(2,1)S(1)} %get-tuple-element.170.refs_0_, bf16[32,1024]{1,0:T(8,128)(2,1)S(1)} %collective-permute-done.35.refs_1_, bf16[32,1024]{1,0:T(8,128)(2,1)S(1)} %collective-permute-done.36.refs_2_, ...), custom_call_target="tpu_custom_call" | custom-call | flops 301989888 | bytes 10715136 | tf_op jit(solution)/shard_map/pallas_call | solution.py:318
  149.2 3.7 %collective-permute-done.39.refs_1_ = bf16[32,1792]{1,0:T(8,128)(2,1)S(1)} collective-permute-done((bf16[32,1792]{1,0:T(8,128)(2,1)S(1)}, bf16[32,1792]{1,0:T(8,128)(2,1)S(1)}, u32[]{:S(2)}, u32[]{:S(2)}) %collective-permute-start.39) | collective-permute-done | bytes 114720 | tf_op jit(solution)/shard_map/ppermute | solution.py:378
  155.8 2.0 %collective-permute-start.40 = (f32[32,128]{1,0:T(8,128)S(1)}, f32[32,128]{1,0:T(8,128)S(1)}, u32[]{:S(2)}, u32[]{:S(2)}) collective-permute-start(f32[32,128]{1,0:T(8,128)S(1)} %get-tuple-element.179.refs_0_), channel_id=1, source_target_pairs={{0,4},{4,0},{8,12},{12,8},{1,5},{5,1},{9,13},{13,9},{2,6},{6,2},{1... | collective-permute-start | bytes 49160 | tf_op jit(solution)/shard_map/ppermute | solution.py:330
  (98 shorter events, 84.6 us)
Async XLA Ops:
  6.9 5.7 %collective-permute-start = (bf16[32,1024]{1,0:T(8,128)(2,1)S(1)}, bf16[32,1024]{1,0:T(8,128)(2,1)S(1)}, u32[]{:S(2)}, u32[]{:S(2)}) collective-permute-start(bf16[32,1024]{1,0:T(8,128)(2,1)S(1)} %get-tuple-element.97), channel_id=1, source_target_pairs={{0,4},{4,0},{8,12},{12,8},{1,5},{5,1},{9,13},{13,9},{2,6},{6,2},{1... | collective-permute-start | bytes 196616 | tf_op jit(solution)/shard_map/ppermute | solution.py:330
  10.0 7.3 %collective-permute-start.1 = (bf16[32,1024]{1,0:T(8,128)(2,1)S(1)}, bf16[32,1024]{1,0:T(8,128)(2,1)S(1)}, u32[]{:S(2)}, u32[]{:S(2)}) collective-permute-start(bf16[32,1024]{1,0:T(8,128)(2,1)S(1)} %get-tuple-element.98), channel_id=1, source_target_pairs={{0,8},{4,12},{8,0},{12,4},{1,9},{5,13},{9,1},{13,5},{2,10},{6,14},... | collective-permute-start | bytes 196616 | tf_op jit(solution)/shard_map/ppermute | solution.py:330
  12.6 6.1 %collective-permute-start.2 = (bf16[32,1024]{1,0:T(8,128)(2,1)S(1)}, bf16[32,1024]{1,0:T(8,128)(2,1)S(1)}, u32[]{:S(2)}, u32[]{:S(2)}) collective-permute-start(bf16[32,1024]{1,0:T(8,128)(2,1)S(1)} %get-tuple-element.99), channel_id=1, source_target_pairs={{0,12},{4,8},{8,4},{12,0},{1,13},{5,9},{9,5},{13,1},{2,14},{6,10},... | collective-permute-start | bytes 196616 | tf_op jit(solution)/shard_map/ppermute | solution.py:330
  18.7 6.1 %collective-permute-start.5 = (bf16[32,1024]{1,0:T(8,128)(2,1)S(1)}, bf16[32,1024]{1,0:T(8,128)(2,1)S(1)}, u32[]{:S(2)}, u32[]{:S(2)}) collective-permute-start(bf16[32,1024]{1,0:T(8,128)(2,1)S(1)} %get-tuple-element.100.refs_0_), channel_id=1, source_target_pairs={{0,12},{4,8},{8,4},{12,0},{1,13},{5,9},{9,5},{13,1},{2,14},{6,10},... | collective-permute-start | bytes 196616 | tf_op jit(solution)/shard_map/ppermute | solution.py:330
  20.6 5.7 %collective-permute-start.4 = (bf16[32,1024]{1,0:T(8,128)(2,1)S(1)}, bf16[32,1024]{1,0:T(8,128)(2,1)S(1)}, u32[]{:S(2)}, u32[]{:S(2)}) collective-permute-start(bf16[32,1024]{1,0:T(8,128)(2,1)S(1)} %get-tuple-element.100.refs_0_), channel_id=1, source_target_pairs={{0,8},{4,12},{8,0},{12,4},{1,9},{5,13},{9,1},{13,5},{2,10},{6,14},... | collective-permute-start | bytes 196616 | tf_op jit(solution)/shard_map/ppermute | solution.py:330
  20.6 5.7 %collective-permute-start.3 = (bf16[32,1024]{1,0:T(8,128)(2,1)S(1)}, bf16[32,1024]{1,0:T(8,128)(2,1)S(1)}, u32[]{:S(2)}, u32[]{:S(2)}) collective-permute-start(bf16[32,1024]{1,0:T(8,128)(2,1)S(1)} %get-tuple-element.100.refs_0_), channel_id=1, source_target_pairs={{0,4},{4,0},{8,12},{12,8},{1,5},{5,1},{9,13},{13,9},{2,6},{6,2},{1... | collective-permute-start | bytes 196616 | tf_op jit(solution)/shard_map/ppermute | solution.py:330
  39.2 8.0 %collective-permute-start.9 = (bf16[32,1152]{1,0:T(8,128)(2,1)S(1)}, bf16[32,1152]{1,0:T(8,128)(2,1)S(1)}, u32[]{:S(2)}, u32[]{:S(2)}) collective-permute-start(bf16[32,1152]{1,0:T(8,128)(2,1)S(1)} %get-tuple-element.110), channel_id=1, source_target_pairs={{0,8},{4,12},{8,0},{12,4},{1,9},{5,13},{9,1},{13,5},{2,10},{6,14},... | collective-permute-start | bytes 221192 | tf_op jit(solution)/shard_map/ppermute | solution.py:330
  40.6 6.6 %collective-permute-start.10 = (bf16[32,1152]{1,0:T(8,128)(2,1)S(1)}, bf16[32,1152]{1,0:T(8,128)(2,1)S(1)}, u32[]{:S(2)}, u32[]{:S(2)}) collective-permute-start(bf16[32,1152]{1,0:T(8,128)(2,1)S(1)} %get-tuple-element.111), channel_id=1, source_target_pairs={{0,12},{4,8},{8,4},{12,0},{1,13},{5,9},{9,5},{13,1},{2,14},{6,10},... | collective-permute-start | bytes 221192 | tf_op jit(solution)/shard_map/ppermute | solution.py:330
  47.5 6.1 %collective-permute-start.13 = (bf16[32,1024]{1,0:T(8,128)(2,1)S(1)}, bf16[32,1024]{1,0:T(8,128)(2,1)S(1)}, u32[]{:S(2)}, u32[]{:S(2)}) collective-permute-start(bf16[32,1024]{1,0:T(8,128)(2,1)S(1)} %get-tuple-element.117.refs_0_), channel_id=1, source_target_pairs={{0,12},{4,8},{8,4},{12,0},{1,13},{5,9},{9,5},{13,1},{2,14},{6,10},... | collective-permute-start | bytes 196616 | tf_op jit(solution)/shard_map/ppermute | solution.py:330
  49.3 5.9 %collective-permute-start.12 = (bf16[32,1024]{1,0:T(8,128)(2,1)S(1)}, bf16[32,1024]{1,0:T(8,128)(2,1)S(1)}, u32[]{:S(2)}, u32[]{:S(2)}) collective-permute-start(bf16[32,1024]{1,0:T(8,128)(2,1)S(1)} %get-tuple-element.117.refs_0_), channel_id=1, source_target_pairs={{0,8},{4,12},{8,0},{12,4},{1,9},{5,13},{9,1},{13,5},{2,10},{6,14},... | collective-permute-start | bytes 196616 | tf_op jit(solution)/shard_map/ppermute | solution.py:330
  68.2 8.0 %collective-permute-start.17 = (bf16[32,1152]{1,0:T(8,128)(2,1)S(1)}, bf16[32,1152]{1,0:T(8,128)(2,1)S(1)}, u32[]{:S(2)}, u32[]{:S(2)}) collective-permute-start(bf16[32,1152]{1,0:T(8,128)(2,1)S(1)} %get-tuple-element.128), channel_id=1, source_target_pairs={{0,8},{4,12},{8,0},{12,4},{1,9},{5,13},{9,1},{13,5},{2,10},{6,14},... | collective-permute-start | bytes 221192 | tf_op jit(solution)/shard_map/ppermute | solution.py:330
  69.7 6.5 %collective-permute-start.18 = (bf16[32,1152]{1,0:T(8,128)(2,1)S(1)}, bf16[32,1152]{1,0:T(8,128)(2,1)S(1)}, u32[]{:S(2)}, u32[]{:S(2)}) collective-permute-start(bf16[32,1152]{1,0:T(8,128)(2,1)S(1)} %get-tuple-element.129), channel_id=1, source_target_pairs={{0,12},{4,8},{8,4},{12,0},{1,13},{5,9},{9,5},{13,1},{2,14},{6,10},... | collective-permute-start | bytes 221192 | tf_op jit(solution)/shard_map/ppermute | solution.py:330
  76.5 6.1 %collective-permute-start.21 = (bf16[32,1024]{1,0:T(8,128)(2,1)S(1)}, bf16[32,1024]{1,0:T(8,128)(2,1)S(1)}, u32[]{:S(2)}, u32[]{:S(2)}) collective-permute-start(bf16[32,1024]{1,0:T(8,128)(2,1)S(1)} %get-tuple-element.137.refs_0_), channel_id=1, source_target_pairs={{0,12},{4,8},{8,4},{12,0},{1,13},{5,9},{9,5},{13,1},{2,14},{6,10},... | collective-permute-start | bytes 196616 | tf_op jit(solution)/shard_map/ppermute | solution.py:330
  78.4 5.9 %collective-permute-start.20 = (bf16[32,1024]{1,0:T(8,128)(2,1)S(1)}, bf16[32,1024]{1,0:T(8,128)(2,1)S(1)}, u32[]{:S(2)}, u32[]{:S(2)}) collective-permute-start(bf16[32,1024]{1,0:T(8,128)(2,1)S(1)} %get-tuple-element.137.refs_0_), channel_id=1, source_target_pairs={{0,8},{4,12},{8,0},{12,4},{1,9},{5,13},{9,1},{13,5},{2,10},{6,14},... | collective-permute-start | bytes 196616 | tf_op jit(solution)/shard_map/ppermute | solution.py:330
  89.1 5.2 %collective-permute-start.23 = (bf16[32,1792]{1,0:T(8,128)(2,1)S(1)}, bf16[32,1792]{1,0:T(8,128)(2,1)S(1)}, u32[]{:S(2)}, u32[]{:S(2)}) collective-permute-start(bf16[32,1792]{1,0:T(8,128)(2,1)S(1)} %get-tuple-element.140.refs_2_), channel_id=1, source_target_pairs={{0,2},{1,3},{2,0},{3,1},{4,6},{5,7},{6,4},{7,5},{8,10},{9,11},{10,... | collective-permute-start | bytes 344072 | tf_op jit(solution)/shard_map/ppermute | solution.py:378
  97.3 8.0 %collective-permute-start.25 = (bf16[32,1152]{1,0:T(8,128)(2,1)S(1)}, bf16[32,1152]{1,0:T(8,128)(2,1)S(1)}, u32[]{:S(2)}, u32[]{:S(2)}) collective-permute-start(bf16[32,1152]{1,0:T(8,128)(2,1)S(1)} %get-tuple-element.148), channel_id=1, source_target_pairs={{0,8},{4,12},{8,0},{12,4},{1,9},{5,13},{9,1},{13,5},{2,10},{6,14},... | collective-permute-start | bytes 221192 | tf_op jit(solution)/shard_map/ppermute | solution.py:330
  98.8 6.5 %collective-permute-start.26 = (bf16[32,1152]{1,0:T(8,128)(2,1)S(1)}, bf16[32,1152]{1,0:T(8,128)(2,1)S(1)}, u32[]{:S(2)}, u32[]{:S(2)}) collective-permute-start(bf16[32,1152]{1,0:T(8,128)(2,1)S(1)} %get-tuple-element.149), channel_id=1, source_target_pairs={{0,12},{4,8},{8,4},{12,0},{1,13},{5,9},{9,5},{13,1},{2,14},{6,10},... | collective-permute-start | bytes 221192 | tf_op jit(solution)/shard_map/ppermute | solution.py:330
  105.6 6.1 %collective-permute-start.29 = (bf16[32,1024]{1,0:T(8,128)(2,1)S(1)}, bf16[32,1024]{1,0:T(8,128)(2,1)S(1)}, u32[]{:S(2)}, u32[]{:S(2)}) collective-permute-start(bf16[32,1024]{1,0:T(8,128)(2,1)S(1)} %get-tuple-element.157.refs_0_), channel_id=1, source_target_pairs={{0,12},{4,8},{8,4},{12,0},{1,13},{5,9},{9,5},{13,1},{2,14},{6,10},... | collective-permute-start | bytes 196616 | tf_op jit(solution)/shard_map/ppermute | solution.py:330
  107.4 5.9 %collective-permute-start.28 = (bf16[32,1024]{1,0:T(8,128)(2,1)S(1)}, bf16[32,1024]{1,0:T(8,128)(2,1)S(1)}, u32[]{:S(2)}, u32[]{:S(2)}) collective-permute-start(bf16[32,1024]{1,0:T(8,128)(2,1)S(1)} %get-tuple-element.157.refs_0_), channel_id=1, source_target_pairs={{0,8},{4,12},{8,0},{12,4},{1,9},{5,13},{9,1},{13,5},{2,10},{6,14},... | collective-permute-start | bytes 196616 | tf_op jit(solution)/shard_map/ppermute | solution.py:330
  126.3 8.0 %collective-permute-start.33 = (bf16[32,1152]{1,0:T(8,128)(2,1)S(1)}, bf16[32,1152]{1,0:T(8,128)(2,1)S(1)}, u32[]{:S(2)}, u32[]{:S(2)}) collective-permute-start(bf16[32,1152]{1,0:T(8,128)(2,1)S(1)} %get-tuple-element.168), channel_id=1, source_target_pairs={{0,8},{4,12},{8,0},{12,4},{1,9},{5,13},{9,1},{13,5},{2,10},{6,14},... | collective-permute-start | bytes 221192 | tf_op jit(solution)/shard_map/ppermute | solution.py:330
  127.8 6.5 %collective-permute-start.34 = (bf16[32,1152]{1,0:T(8,128)(2,1)S(1)}, bf16[32,1152]{1,0:T(8,128)(2,1)S(1)}, u32[]{:S(2)}, u32[]{:S(2)}) collective-permute-start(bf16[32,1152]{1,0:T(8,128)(2,1)S(1)} %get-tuple-element.169), channel_id=1, source_target_pairs={{0,12},{4,8},{8,4},{12,0},{1,13},{5,9},{9,5},{13,1},{2,14},{6,10},... | collective-permute-start | bytes 221192 | tf_op jit(solution)/shard_map/ppermute | solution.py:330
  135.2 6.1 %collective-permute-start.37 = (bf16[32,1024]{1,0:T(8,128)(2,1)S(1)}, bf16[32,1024]{1,0:T(8,128)(2,1)S(1)}, u32[]{:S(2)}, u32[]{:S(2)}) collective-permute-start(bf16[32,1024]{1,0:T(8,128)(2,1)S(1)} %get-tuple-element.170.refs_0_), channel_id=1, source_target_pairs={{0,12},{4,8},{8,4},{12,0},{1,13},{5,9},{9,5},{13,1},{2,14},{6,10},... | collective-permute-start | bytes 196616 | tf_op jit(solution)/shard_map/ppermute | solution.py:330
  137.0 5.9 %collective-permute-start.36 = (bf16[32,1024]{1,0:T(8,128)(2,1)S(1)}, bf16[32,1024]{1,0:T(8,128)(2,1)S(1)}, u32[]{:S(2)}, u32[]{:S(2)}) collective-permute-start(bf16[32,1024]{1,0:T(8,128)(2,1)S(1)} %get-tuple-element.170.refs_0_), channel_id=1, source_target_pairs={{0,8},{4,12},{8,0},{12,4},{1,9},{5,13},{9,1},{13,5},{2,10},{6,14},... | collective-permute-start | bytes 196616 | tf_op jit(solution)/shard_map/ppermute | solution.py:330
  153.4 5.6 %collective-permute-start.42 = (f32[32,128]{1,0:T(8,128)S(1)}, f32[32,128]{1,0:T(8,128)S(1)}, u32[]{:S(2)}, u32[]{:S(2)}) collective-permute-start(f32[32,128]{1,0:T(8,128)S(1)} %get-tuple-element.179.refs_0_), channel_id=1, source_target_pairs={{0,12},{4,8},{8,4},{12,0},{1,13},{5,9},{9,5},{13,1},{2,14},{6,10},... | collective-permute-start | bytes 49160 | tf_op jit(solution)/shard_map/ppermute | solution.py:330
  (23 other events, 127.6 us)

commit v3 on v2

v3 whole, which is shorter than its diff:
```python
import functools

import jax
import jax.numpy as jnp
from jax import lax
from jax.experimental import pallas as pl
from jax.experimental.pallas import tpu as pltpu
from jax.sharding import PartitionSpec as P

GRID = 128
ITERS = 5
LANES = 128
EDGE = 2 * GRID
SLOTS = 8
TAIL = 16
BF16 = jnp.bfloat16
F32 = jnp.float32

GRAD_SQ, SMOOTH_SQ, CROSS = 0, 1, 2
IMAGE_SQ, BETA, GUESS = 2, 3, 4


def xor_pairs(count, offset):
    return [(i, i ^ offset) for i in range(count)]


def tree_sum(parts):
    while len(parts) > 1:
        parts = [parts[i] + parts[i + 1] for i in range(0, len(parts), 2)]
    return parts[0]


def lane_ids(sets):
    return lax.broadcasted_iota(jnp.int32, (sets, LANES), 1)


def beside(row):
    lane = lane_ids(row.shape[0])
    left = jnp.where(lane == 0, 0.0, pltpu.roll(row, 1, 1))
    right = jnp.where(lane == LANES - 1, 0.0, pltpu.roll(row, LANES - 1, 1))
    return left + right


def smooth_row(above, row, below):
    near = beside(row)
    if above is not None:
        near = near + above
    if below is not None:
        near = near + below
    return row - 0.25 * near


def lanes_of(columns, sets):
    lane = lane_ids(sets)
    block = jnp.zeros((sets, LANES), F32)
    for slot, column in columns.items():
        block = jnp.where(lane == slot, column, block)
    return block


def pack(block):
    block = jnp.where(lane_ids(block.shape[0]) < SLOTS, block, 0.0)
    high = block.astype(BF16).astype(F32)
    rest = block - high
    mid = rest.astype(BF16).astype(F32)
    low = (rest - mid).astype(BF16).astype(F32)
    return (high + pltpu.roll(mid, SLOTS, 1) + pltpu.roll(low, 2 * SLOTS, 1)).astype(BF16)


def unpack(packed):
    block = packed.astype(F32)
    mid = pltpu.roll(block, LANES - SLOTS, 1)
    low = pltpu.roll(block, LANES - 2 * SLOTS, 1)
    return jnp.where(lane_ids(block.shape[0]) < SLOTS, (block + mid) + low, 0.0)


def row_of(values, index):
    return values[:, index * GRID : (index + 1) * GRID]


def seam(lower, upper):
    low0, low1, up0, up1 = row_of(lower, 0), row_of(lower, 1), row_of(upper, 0), row_of(upper, 1)
    cross = smooth_row(low0, low1, None) * up0 + smooth_row(None, up0, up1) * low1
    return jnp.sum(0.0625 * (up0 * up0 + low1 * low1) - 0.5 * cross, axis=1, keepdims=True)


def merge(mine_ref, got_ref, above, below, pixels, step, final, tile):
    upper_side = (tile // step) % 2 == 1
    inside = tile % step
    scalar_at = pl.ds(pixels, LANES)
    if mine_ref.dtype == F32:
        mine, got = mine_ref[:, scalar_at], got_ref[:, scalar_at]
    else:
        mine, got = unpack(mine_ref[:, scalar_at]), unpack(got_ref[:, scalar_at])
    edges, got_edges = mine_ref[:, pixels + LANES :].astype(F32), got_ref[:, pixels + LANES :].astype(F32)
    if final:
        first = last = None
        lower_last = jnp.where(upper_side, got_edges, edges)
        upper_first = jnp.where(upper_side, edges, got_edges)
    else:
        first = jnp.where(upper_side, got_edges[:, :EDGE], edges[:, :EDGE])
        last = jnp.where(upper_side, edges[:, EDGE:], got_edges[:, EDGE:])
        lower_last = jnp.where(upper_side, got_edges[:, EDGE:], edges[:, EDGE:])
        upper_first = jnp.where(upper_side, edges[:, :EDGE], got_edges[:, :EDGE])
    sets = mine.shape[0]
    scalars = mine + got + lanes_of({SMOOTH_SQ: seam(lower_last, upper_first)}, sets)
    above = jnp.where(upper_side & (inside == 0), lower_last, above)
    below = jnp.where(jnp.logical_not(upper_side) & (inside == step - 1), upper_first, below)
    value = mine_ref[:, :pixels].astype(F32) + got_ref[:, :pixels].astype(F32)
    return value, scalars, first, last, above, below


def edge_columns(step, n_par):
    return EDGE if 2 * step >= n_par else 2 * EDGE


def store_edges(message, at, first, last, step, n_par, tile):
    if 2 * step >= n_par:
        edges = jnp.where((tile // step) % 2 == 1, first, last)
    else:
        edges = jnp.concatenate([first, last], axis=1)
    message[:, at:] = edges.astype(message.dtype)


def own_columns(offset, width):
    return pl.ds(pl.multiple_of((lax.axis_index("pix") ^ offset) * width, LANES), width)


def store_block(block, sent, scalar):
    sets, width = sent.shape
    for r in range(width // LANES):
        block[r * sets : (r + 1) * sets, :] = sent[:, r * LANES : (r + 1) * LANES]
    if scalar is not None:
        diagonal = lax.broadcasted_iota(jnp.int32, (sets, LANES), 0) == lane_ids(sets)
        row = jnp.sum(jnp.where(diagonal, scalar, 0.0), axis=0, keepdims=True)
        high = row.astype(BF16).astype(F32)
        mid = (row - high).astype(BF16).astype(F32)
        low = row - high - mid
        line = lax.broadcasted_iota(jnp.int32, (TAIL, LANES), 0)
        tail = jnp.where(line == 0, high, jnp.where(line == 1, mid, jnp.where(line == 2, low, 0.0)))
        block[sets * width // LANES :, :] = tail.astype(BF16)


def load_block(block, sets, width):
    rows = width // LANES
    return jnp.concatenate([block[r * sets : (r + 1) * sets, :].astype(F32) for r in range(rows)], axis=1)


def load_scalar(block, sets, width):
    tail = block[sets * width // LANES :, :].astype(F32)
    row = (tail[0:1] + tail[1:2]) + tail[2:3]
    diagonal = lax.broadcasted_iota(jnp.int32, (sets, LANES), 0) == lane_ids(sets)
    return jnp.sum(jnp.where(diagonal, row, 0.0), axis=1, keepdims=True)


def shard_kernel(offset, n_shards, first_sweep, closing, n_par, *refs):
    refs = list(refs)
    shard, green = refs.pop(0), refs.pop(0)
    twice = None if first_sweep else refs.pop(0)
    image_in = refs.pop(0) if offset else None
    sets, width = shard.shape
    pixels = green.shape[0]
    at = own_columns(offset, width) if n_shards > 1 else slice(None)
    value = shard[...]
    image = lax.dot_general(value, green[:, at], (((1,), (1,)), ((), ())), preferred_element_type=F32)
    if image_in is not None:
        image += image_in[...]
    rows = width // GRID
    grad_sq = jnp.zeros((sets, LANES), F32)
    smooth_sq = jnp.zeros((sets, LANES), F32)
    cross = jnp.zeros((sets, LANES), F32)
    wide = value.astype(F32)
    beside_it = None if first_sweep else twice[:, at]
    for r in range(rows):
        row = row_of(wide, r)
        alone = smooth_row(row_of(wide, r - 1) if r else None, row, row_of(wide, r + 1) if r + 1 < rows else None)
        grad_sq += row * row
        smooth_sq += alone * alone
        if not first_sweep:
            cross += row * row_of(beside_it, r)
    columns = {GRAD_SQ: jnp.sum(grad_sq, axis=1, keepdims=True), SMOOTH_SQ: jnp.sum(smooth_sq, axis=1, keepdims=True)}
    if not first_sweep:
        columns[CROSS] = jnp.sum(cross, axis=1, keepdims=True)
    scalars = lanes_of(columns, sets)
    if not closing:
        refs[0][...] = image
        refs[1][...] = scalars
        return
    others, other_scalars = refs[: n_shards - 1], refs[n_shards - 1 : 2 * n_shards - 2]
    whole, message = refs[2 * n_shards - 2 :]
    cells = whole.shape[1]
    order = [k for k in range(n_shards) if k != offset]
    found = {offset: scalars}
    if n_shards > 1:
        whole[:, at] = value
    else:
        whole[...] = value
    for k, other, other_scalar in zip(order, others, other_scalars):
        whole[:, own_columns(k, width)] = other[...]
        found[k] = other_scalar[...]
    total = tree_sum([found[k] for k in range(n_shards)])
    seams = jnp.zeros((sets, 1), F32)
    for k in range(1, n_shards):
        edge = k * width
        seams += seam(whole[:, edge - EDGE : edge].astype(F32), whole[:, edge : edge + EDGE].astype(F32))
    message[:, :pixels] = image
    message[:, pixels : pixels + LANES] = total + lanes_of({SMOOTH_SQ: seams}, sets)
    first, last = whole[:, :EDGE].astype(F32), whole[:, cells - EDGE :].astype(F32)
    store_edges(message, pixels + LANES, first, last, 1, n_par, lax.axis_index("par"))


def middle_kernel(step, n_par, *refs):
    if step == 1:
        mine, got, message, above, below = refs
        old_above = old_below = jnp.zeros(above.shape, F32)
    else:
        mine, got, above_in, below_in, message, above, below = refs
        old_above, old_below = above_in[...], below_in[...]
    pixels = mine.shape[1] - LANES - 2 * EDGE
    tile = lax.axis_index("par")
    value, scalars, first, last, up, down = merge(mine, got, old_above, old_below, pixels, step, False, tile)
    message[:, :pixels] = value.astype(BF16)
    message[:, pixels : pixels + LANES] = pack(scalars)
    store_edges(message, pixels + LANES, first, last, 2 * step, n_par, tile)
    above[...] = up
    below[...] = down


def image_kernel(step, n_pix, first_sweep, has_block, *refs):
    refs = list(refs)
    mine, got, above_in, below_in = (refs.pop(0) for _ in range(4))
    old_scalars, old_image = (None, None) if first_sweep else (refs.pop(0), refs.pop(0))
    green, lost = (refs.pop(0), refs.pop(0)) if has_block else (None, None)
    scalars, image, rounded, above, below = (refs.pop(0) for _ in range(5))
    sets, pixels = image.shape
    value, sums, _, _, up, down = merge(
        mine, got, above_in[...], below_in[...], pixels, step, True, lax.axis_index("par")
    )
    above[...] = up
    below[...] = down
    grad_sq = sums[:, GRAD_SQ : GRAD_SQ + 1]
    smooth_sq = sums[:, SMOOTH_SQ : SMOOTH_SQ + 1]
    beta = jnp.zeros((sets, 1), F32)
    if not first_sweep:
        beta = grad_sq / old_scalars[:, GRAD_SQ : GRAD_SQ + 1]
        old_smooth = old_scalars[:, SMOOTH_SQ : SMOOTH_SQ + 1]
        smooth_sq = smooth_sq + beta * (2.0 * sums[:, CROSS : CROSS + 1] + beta * old_smooth)
        value = value + beta * old_image[...]
    image[...] = value
    rounded[...] = value.astype(BF16)
    image_sq = jnp.zeros((sets, LANES), F32)
    for at in range(0, pixels, LANES):
        part = value[:, at : at + LANES]
        image_sq += part * part
    image_sq = jnp.sum(image_sq, axis=1, keepdims=True)
    guess = (n_pix * image_sq + smooth_sq) / grad_sq
    scalars[...] = lanes_of(
        {GRAD_SQ: grad_sq, SMOOTH_SQ: smooth_sq, IMAGE_SQ: image_sq, BETA: beta, GUESS: guess}, sets
    )
    if has_block:
        send_block(n_pix - 1, value.astype(BF16), green, lost, guess, image_sq, *refs)


def send_block(offset, image, green, lost, guess, image_sq, block, missed):
    part = jnp.dot(image, green[:, own_columns(offset, missed.shape[1])], preferred_element_type=F32)
    aimed = part if lost is None else part - guess * lost[...]
    sent = aimed.astype(BF16)
    store_block(block, sent, image_sq)
    missed[...] = part - sent.astype(F32)


def block_kernel(offset, rounded, scalars, green, lost, block, missed):
    guess, image_sq = scalars[:, GUESS : GUESS + 1], scalars[:, IMAGE_SQ : IMAGE_SQ + 1]
    send_block(offset, rounded[...], green, lost, guess, image_sq, block, missed)


def own_kernel(first_sweep, n_par, direct, has_product, *refs):
    refs = list(refs)
    scalars, above, below, whole = (refs.pop(0) for _ in range(4))
    old_direction = None if first_sweep else refs.pop(0)
    rounded, green = (refs.pop(0), refs.pop(0)) if has_product else (None, None)
    direction = refs.pop(0)
    cells = whole.shape[1]
    rows = cells // GRID
    if first_sweep:
        direction[:, :EDGE] = above[...]
        direction[:, EDGE : EDGE + cells] = whole[...].astype(F32)
        direction[:, EDGE + cells :] = below[...]
    else:
        beta = scalars[:, BETA : BETA + 1]
        direction[:, :EDGE] = above[...] + beta * old_direction[:, :EDGE]
        direction[:, EDGE : EDGE + cells] = whole[...].astype(F32) + beta * old_direction[:, EDGE : EDGE + cells]
        direction[:, EDGE + cells :] = below[...] + beta * old_direction[:, EDGE + cells :]
    if not has_product:
        return
    twice, own, once = refs
    tile = lax.axis_index("par")

    def from_ref(ref, r):
        return ref[:, r * GRID : (r + 1) * GRID]

    for r in range(rows + 2):
        row = smooth_row(from_ref(direction, r), from_ref(direction, r + 1), from_ref(direction, r + 2))
        if r == 0:
            row = jnp.where(tile == 0, 0.0, row)
        if r == rows + 1:
            row = jnp.where(tile == n_par - 1, 0.0, row)
        once[:, r * GRID : (r + 1) * GRID] = row
    for r in range(rows):
        row = smooth_row(from_ref(once, r), from_ref(once, r + 1), from_ref(once, r + 2))
        twice[:, r * GRID : (r + 1) * GRID] = row
    if direct:
        at = own_columns(0, own.shape[1])
        own[...] = jnp.dot(rounded[...], green[:, at], preferred_element_type=F32) + twice[:, at]
    else:
        own[...] = jnp.dot(rounded[...], green[...], preferred_element_type=F32)


def start_kernel(observed, green, own, *refs):
    count = len(refs) // 2
    image = observed[...]
    for offset in range(count, 0, -1):
        send_block(offset, image, green, None, None, None, refs[offset - 1], refs[count + offset - 1])
    own[...] = jnp.dot(image, green[:, own_columns(0, own.shape[1])], preferred_element_type=F32)


def receive_start_kernel(own, *refs):
    got, (grad, rounded) = refs[:-2][::-1], refs[-2:]
    sets, width = own.shape
    value = tree_sum([own[...]] + [load_block(ref, sets, width) for ref in got])
    grad[...] = value
    rounded[...] = value.astype(BF16)


def step_length(scalars, others):
    image_sq = tree_sum([scalars[:, IMAGE_SQ : IMAGE_SQ + 1]] + others)
    return scalars[:, GRAD_SQ : GRAD_SQ + 1] / (image_sq + scalars[:, SMOOTH_SQ : SMOOTH_SQ + 1])


def receive_kernel(own, scalars, old_grad, *refs):
    got, (grad, rounded, length) = refs[:-3][::-1], refs[-3:]
    sets, width = own.shape
    step_len = step_length(scalars, [load_scalar(ref, sets, width) for ref in got])
    change = tree_sum([own[...]] + [load_block(ref, sets, width) for ref in got])
    value = old_grad[...] - step_len * change
    grad[...] = value
    rounded[...] = value.astype(BF16)
    length[...] = jnp.broadcast_to(step_len, length.shape)


def update_kernel(count, length, direction, image, solution, residual, *refs):
    step_len = length[:, :1]
    lost, missed = refs[:count], refs[count : 2 * count]
    new_solution, new_residual = refs[2 * count : 2 * count + 2]
    for old, change, new in zip(lost, missed, refs[2 * count + 2 :]):
        new[...] = old[...] - step_len * change[...]
    cells = solution.shape[1]
    new_solution[...] = solution[...] + step_len * direction[:, EDGE : EDGE + cells]
    new_residual[...] = residual[...] - step_len * image[...]


def finish_kernel(scalars, *refs):
    got, (direction, image, solution, residual, new_solution, new_residual) = refs[:-6][::-1], refs[-6:]
    step_len = step_length(scalars, [ref[:, IMAGE_SQ : IMAGE_SQ + 1] for ref in got])
    cells = solution.shape[1]
    new_solution[...] = solution[...] + step_len * direction[:, EDGE : EDGE + cells]
    new_residual[...] = residual[...] - step_len * image[...]


def call(kernel, operands, outs, scratch=(), flops=0, limit=24 << 20):
    vmem = pl.BlockSpec(memory_space=pltpu.VMEM)
    shapes = [jax.ShapeDtypeStruct(*out) for out in outs]
    moved = sum(x.size * x.dtype.itemsize for x in [*operands, *shapes])
    return pl.pallas_call(
        kernel,
        in_specs=[vmem] * len(operands),
        out_specs=[vmem] * len(outs),
        out_shape=shapes,
        scratch_shapes=list(scratch),
        name=getattr(kernel, "func", kernel).__name__,
        compiler_params=pltpu.CompilerParams(vmem_limit_bytes=limit),
        cost_estimate=pl.CostEstimate(flops=flops or moved, bytes_accessed=moved, transcendentals=0),
    )(*operands)


def exchange(blocks, axis, count):
    got = [lax.ppermute(blocks[k - 1], axis, xor_pairs(count, k)) for k in range(count - 1, 0, -1)]
    return got[::-1]


def on_device(green, observed):
    sets = observed.shape[0]
    pixels, cells = green.shape
    n_pix, n_par = lax.axis_size("pix"), lax.axis_size("par")
    here = lax.axis_index("pix")
    width = cells // n_pix
    direct = n_pix <= 8 and width % LANES == 0
    flops = 2 * sets * pixels * cells
    part_flops = flops // n_pix
    count = n_pix - 1 if direct else 0
    shard, rounded_shard = ((sets, width), F32), ((sets, width), BF16)
    plain = ((sets * width // LANES, LANES), BF16)
    block = ((sets * width // LANES + TAIL, LANES), BF16)
    scalar = ((sets, LANES), F32)
    line, wide, edge = ((sets, pixels), F32), ((sets, cells), F32), ((sets, EDGE), F32)
    ring = ((sets, cells + 2 * EDGE), F32)

    lost = []
    if direct:
        own, *rest = call(start_kernel, [observed, green], [shard] + [plain] * count + [shard] * count, flops=flops)
        blocks, lost = rest[:count], rest[count:]
        got = exchange(blocks, "pix", n_pix)
    else:
        partial = jnp.dot(observed, green, preferred_element_type=F32)
        own, got = lax.psum_scatter(partial, "pix", scatter_dimension=1, tiled=True), []
    grad, rounded_grad = call(receive_start_kernel, [own, *got[::-1]], [shard, rounded_shard])
    solution = jnp.zeros((sets, cells), F32)
    residual = observed.astype(F32)
    scalars = image = direction = twice = None
    for sweep in range(ITERS):
        first, final = sweep == 0, sweep + 1 == ITERS
        if direct:
            shards = [rounded_grad] + exchange([rounded_grad] * count, "pix", n_pix)
        else:
            shards = [lax.all_gather(rounded_grad, "pix", axis=1, tiled=True)]
        beside_them = [] if first else [twice]

        def message_of(step):
            return ((sets, pixels + LANES + edge_columns(step, n_par)), F32 if step == 1 else BF16)

        order = [0] + list(range(len(shards) - 1, 0, -1))
        partial, parts = [], {}
        for k in order[:-1]:
            kernel = functools.partial(shard_kernel, k, len(shards), first, False, n_par)
            out, parts[k] = call(kernel, [shards[k], green, *beside_them, *partial], [line, scalar], flops=part_flops)
            partial = [out]
        k = order[-1]
        others = sorted(parts)
        whole, message = call(
            functools.partial(shard_kernel, k, len(shards), first, True, n_par),
            [shards[k], green, *beside_them, *partial]
            + [shards[o] for o in others]
            + [parts[o] for o in others],
            [((sets, cells), BF16), message_of(1)],
            flops=part_flops,
        )
        step, above, below = 1, None, None
        while True:
            got = lax.ppermute(message, "par", xor_pairs(n_par, step))
            if 2 * step >= n_par:
                break
            message, above, below = call(
                functools.partial(middle_kernel, step, n_par),
                [message, got, *([] if step == 1 else [above, below])],
                [message_of(2 * step), edge, edge],
            )
            step *= 2
        if above is None:
            above = below = jnp.zeros(edge[0], F32)
        has_block = direct and not final
        missed = [None] * count
        blocks = [None] * count
        scalars, image, rounded, above, below, *rest = call(
            functools.partial(image_kernel, step, n_pix, first, has_block),
            [message, got, above, below]
            + ([] if first else [scalars, image])
            + ([green, lost[-1]] if has_block else []),
            [scalar, line, ((sets, pixels), BF16), edge, edge] + ([block, shard] if has_block else []),
            flops=part_flops if has_block else 0,
        )
        olds = [] if first else [direction]
        if final:
            (direction,) = call(
                functools.partial(own_kernel, first, n_par, direct, False),
                [scalars, above, below, whole, *olds],
                [ring],
            )
            if direct:
                got = exchange([scalars] * count, "pix", n_pix)
            else:
                got = []
                scalars = scalars.at[:, IMAGE_SQ].set(lax.psum(scalars[:, IMAGE_SQ], "pix"))
            return tuple(call(finish_kernel, [scalars, *got[::-1], direction, image, solution, residual], [wide, line]))
        if direct:
            blocks[-1], missed[-1] = rest
            for k in range(count - 1, 0, -1):
                blocks[k - 1], missed[k - 1] = call(
                    functools.partial(block_kernel, k),
                    [rounded, scalars, green, lost[k - 1]],
                    [block, shard],
                    flops=part_flops,
                )
        direction, twice, own = call(
            functools.partial(own_kernel, first, n_par, direct, True),
            [scalars, above, below, whole, *olds, rounded, green],
            [ring, wide, shard if direct else wide],
            [pltpu.VMEM((sets, cells + EDGE), F32)],
            part_flops if direct else flops,
        )
        if direct:
            got = exchange(blocks, "pix", n_pix)
        else:
            got = []
            own = lax.psum_scatter(own, "pix", scatter_dimension=1, tiled=True)
            own = own + lax.dynamic_slice_in_dim(twice, here * width, width, axis=1)
            scalars = scalars.at[:, IMAGE_SQ].set(lax.psum(scalars[:, IMAGE_SQ], "pix"))
        grad, rounded_grad, length = call(
            receive_kernel, [own, scalars, grad, *got[::-1]], [shard, rounded_shard, scalar]
        )
        solution, residual, *lost = call(
            functools.partial(update_kernel, count),
            [length, direction, image, solution, residual, *lost, *missed],
            [wide, line] + [shard] * count,
        )


def solution(mesh):
    return jax.shard_map(
        on_device,
        mesh=mesh,
        in_specs=(P("pix", "par"), P("parts", "pix")),
        out_specs=(P("parts", "par"), P("parts", "pix")),
        check_vma=False,
    )
```

time: 161 us -> 152 us (0.944)
  waiting for transfers between devices: 67.3 us -> 53.4 us
  Pallas kernels: 30.9 us -> 34.7 us
    ppermute x33, waiting for transfers between devices: 42.2 us -> 30.3 us  [exchange(): lax.ppermute(blocks[k - 1], axis, xor_pairs(count, k))]
    pallas_call x26 -> x54, Pallas kernels: 30.9 us -> 34.7 us  [call(): pl.pallas_call(kernel, in_specs=[vmem] * len(operands), out_specs=[vmem]...]
    ppermute x10, waiting for transfers between devices: 25.1 us -> 23.1 us  [on_device(): got = lax.ppermute(message, 'par', xor_pairs(n_par, step))]
  transfers between devices with their start and end apart: 43 -> 43, of which waited for: 36 -> 32; matrix products, arithmetic and copies ran while one was open for 0% -> 0% of each run, Pallas kernels for 1% -> 14%
where the time goes in v3:
time: 152 us
  starting transfers between devices  58.3 us (38%)
  waiting for transfers between devices  53.4 us (35%)
  Pallas kernels  34.7 us (23%)
  local copies, waits for them, and re-layouts  4.6 us (3%)
    ppermute x33, starting transfers between devices, exchange(): lax.ppermute(blocks[k - 1], axis, xor_pairs(count, k))  50.6 us
    pallas_call x54, Pallas kernels, call(): pl.pallas_call(kernel, in_specs=[vmem] * len(operands), out_specs=[vmem]...  34.7 us
    ppermute x33, waiting for transfers between devices, exchange(): lax.ppermute(blocks[k - 1], axis, xor_pairs(count, k))  30.3 us
    ppermute x10, waiting for transfers between devices, on_device(): got = lax.ppermute(message, 'par', xor_pairs(n_par, step))  23.1 us
    ppermute x10, starting transfers between devices, on_device(): got = lax.ppermute(message, 'par', xor_pairs(n_par, step))  7.71 us
    unnamed x8, local copies, waits for them, and re-layouts  4.56 us
  transfers between devices with their start and end apart: 43, of which 32 were waited for; matrix products, arithmetic and copies ran while one was open for 0% of the time, Pallas kernels for 14%

profile of v3, /device:TPU:0, one launch (start us, length us, event | category | flops | bytes accessed | tf_op | source)
XLA Modules:
  0.0 152.0 jit_solution(9549700998653361803)
XLA Ops:
  0.6 3.7 %copy-done = bf16[1152,4096]{1,0:T(8,128)(2,1)S(1)} copy-done((bf16[1152,4096]{1,0:T(8,128)(2,1)S(1)}, bf16[1152,4096]{1,0:T(8,128)(2,1)}, u32[]{:S(2)}) %copy-start) | copy-done | bytes 9437208
  5.2 1.7 %start_kernel.1 = (f32[32,1024]{1,0:T(8,128)S(1)}, bf16[256,128]{1,0:T(8,128)(2,1)S(1)}, bf16[256,128]{1,0:T(8,128)(2,1)S(1)}, bf16[256,128]{1,0:T(8,128)(2,1)S(...) custom-call(bf16[32,1152]{1,0:T(8,128)(2,1)S(1)} %copy-done.2, ...), custom_call_target="tpu_custom_call" | custom-call | flops 301989888 | bytes 10231808 | tf_op jit(solution)/shard_map/start_kernel/pallas_call | solution.py:374
  6.9 5.1 %collective-permute-start = (bf16[256,128]{1,0:T(8,128)(2,1)S(1)}, bf16[256,128]{1,0:T(8,128)(2,1)S(1)}, u32[]{:S(2)}, u32[]{:S(2)}) collective-permute-start(bf16[256,128]{1,0:T(8,128)(2,1)S(1)} %get-tuple-element.155), channel_id=1, source_target_pairs={{0,12},{4,8},{8,4},{12,0},{1,13},{5,9},{9,5},{13,1},{2,14},{6,10},... | collective-permute-start | bytes 196616 | tf_op jit(solution)/shard_map/ppermute | solution.py:387
  12.6 1.9 %collective-permute-done.refs_0_ = bf16[256,128]{1,0:T(8,128)(2,1)S(1)} collective-permute-done((bf16[256,128]{1,0:T(8,128)(2,1)S(1)}, bf16[256,128]{1,0:T(8,128)(2,1)S(1)}, u32[]{:S(2)}, u32[]{:S(2)}) %collective-permute-start) | collective-permute-done | bytes 65568 | tf_op jit(solution)/shard_map/ppermute | solution.py:387
  14.5 3.1 %collective-permute-done.1.refs_1_ = bf16[256,128]{1,0:T(8,128)(2,1)S(1)} collective-permute-done((bf16[256,128]{1,0:T(8,128)(2,1)S(1)}, bf16[256,128]{1,0:T(8,128)(2,1)S(1)}, u32[]{:S(2)}, u32[]{:S(2)}) %collective-permute-start.1) | collective-permute-done | bytes 65568 | tf_op jit(solution)/shard_map/ppermute | solution.py:387
  17.7 2.7 %collective-permute-start.5 = (bf16[32,1024]{1,0:T(8,128)(2,1)S(1)}, bf16[32,1024]{1,0:T(8,128)(2,1)S(1)}, u32[]{:S(2)}, u32[]{:S(2)}) collective-permute-start(bf16[32,1024]{1,0:T(8,128)(2,1)S(1)} %get-tuple-element.158.refs_0_.refs_3_), channel_id=1, source_target_pairs={{0,12},{4,8},{8,4},{12,0},{1,13},{5,9},{9,5},{13,1},{2,14},{6,10},... | collective-permute-start | bytes 196616 | tf_op jit(solution)/shard_map/ppermute | solution.py:387
  31.6 3.3 %collective-permute-done.7.refs_1_ = bf16[32,1536]{1,0:T(8,128)(2,1)S(1)} collective-permute-done((bf16[32,1536]{1,0:T(8,128)(2,1)S(1)}, bf16[32,1536]{1,0:T(8,128)(2,1)S(1)}, u32[]{:S(2)}, u32[]{:S(2)}) %collective-permute-start.7) | collective-permute-done | bytes 98336 | tf_op jit(solution)/shard_map/ppermute | solution.py:449
  38.8 2.3 %collective-permute-start.10 = (bf16[272,128]{1,0:T(8,128)(2,1)S(1)}, bf16[272,128]{1,0:T(8,128)(2,1)S(1)}, u32[]{:S(2)}, u32[]{:S(2)}) collective-permute-start(bf16[272,128]{1,0:T(8,128)(2,1)S(1)} %get-tuple-element.181), channel_id=1, source_target_pairs={{0,4},{4,0},{8,12},{12,8},{1,5},{5,1},{9,13},{13,9},{2,6},{6,2},{1... | collective-permute-start | bytes 208904 | tf_op jit(solution)/shard_map/ppermute | solution.py:387
  41.9 2.6 %collective-permute-done.9.refs_1_ = bf16[272,128]{1,0:T(8,128)(2,1)S(1)} collective-permute-done((bf16[272,128]{1,0:T(8,128)(2,1)S(1)}, bf16[272,128]{1,0:T(8,128)(2,1)S(1)}, u32[]{:S(2)}, u32[]{:S(2)}) %collective-permute-start.9) | collective-permute-done | bytes 69664 | tf_op jit(solution)/shard_map/ppermute | solution.py:387
  47.3 2.2 %collective-permute-start.11 = (bf16[32,1024]{1,0:T(8,128)(2,1)S(1)}, bf16[32,1024]{1,0:T(8,128)(2,1)S(1)}, u32[]{:S(2)}, u32[]{:S(2)}) collective-permute-start(bf16[32,1024]{1,0:T(8,128)(2,1)S(1)} %get-tuple-element.182.refs_0_.refs_4_), channel_id=1, source_target_pairs={{0,4},{4,0},{8,12},{12,8},{1,5},{5,1},{9,13},{13,9},{2,6},{6,2},{1... | collective-permute-start | bytes 196616 | tf_op jit(solution)/shard_map/ppermute | solution.py:387
  58.8 3.0 %collective-permute-done.15.refs_1_ = bf16[32,1536]{1,0:T(8,128)(2,1)S(1)} collective-permute-done((bf16[32,1536]{1,0:T(8,128)(2,1)S(1)}, bf16[32,1536]{1,0:T(8,128)(2,1)S(1)}, u32[]{:S(2)}, u32[]{:S(2)}) %collective-permute-start.15) | collective-permute-done | bytes 98336 | tf_op jit(solution)/shard_map/ppermute | solution.py:449
  66.0 2.3 %collective-permute-start.18 = (bf16[272,128]{1,0:T(8,128)(2,1)S(1)}, bf16[272,128]{1,0:T(8,128)(2,1)S(1)}, u32[]{:S(2)}, u32[]{:S(2)}) collective-permute-start(bf16[272,128]{1,0:T(8,128)(2,1)S(1)} %get-tuple-element.212), channel_id=1, source_target_pairs={{0,4},{4,0},{8,12},{12,8},{1,5},{5,1},{9,13},{13,9},{2,6},{6,2},{1... | collective-permute-start | bytes 208904 | tf_op jit(solution)/shard_map/ppermute | solution.py:387
  69.1 2.5 %collective-permute-done.17.refs_1_ = bf16[272,128]{1,0:T(8,128)(2,1)S(1)} collective-permute-done((bf16[272,128]{1,0:T(8,128)(2,1)S(1)}, bf16[272,128]{1,0:T(8,128)(2,1)S(1)}, u32[]{:S(2)}, u32[]{:S(2)}) %collective-permute-start.17) | collective-permute-done | bytes 69664 | tf_op jit(solution)/shard_map/ppermute | solution.py:387
  74.4 2.1 %collective-permute-start.19 = (bf16[32,1024]{1,0:T(8,128)(2,1)S(1)}, bf16[32,1024]{1,0:T(8,128)(2,1)S(1)}, u32[]{:S(2)}, u32[]{:S(2)}) collective-permute-start(bf16[32,1024]{1,0:T(8,128)(2,1)S(1)} %get-tuple-element.213.refs_0_.refs_4_), channel_id=1, source_target_pairs={{0,4},{4,0},{8,12},{12,8},{1,5},{5,1},{9,13},{13,9},{2,6},{6,2},{1... | collective-permute-start | bytes 196616 | tf_op jit(solution)/shard_map/ppermute | solution.py:387
  86.0 2.9 %collective-permute-done.23.refs_1_ = bf16[32,1536]{1,0:T(8,128)(2,1)S(1)} collective-permute-done((bf16[32,1536]{1,0:T(8,128)(2,1)S(1)}, bf16[32,1536]{1,0:T(8,128)(2,1)S(1)}, u32[]{:S(2)}, u32[]{:S(2)}) %collective-permute-start.23) | collective-permute-done | bytes 98336 | tf_op jit(solution)/shard_map/ppermute | solution.py:449
  93.0 2.3 %collective-permute-start.26 = (bf16[272,128]{1,0:T(8,128)(2,1)S(1)}, bf16[272,128]{1,0:T(8,128)(2,1)S(1)}, u32[]{:S(2)}, u32[]{:S(2)}) collective-permute-start(bf16[272,128]{1,0:T(8,128)(2,1)S(1)} %get-tuple-element.245), channel_id=1, source_target_pairs={{0,4},{4,0},{8,12},{12,8},{1,5},{5,1},{9,13},{13,9},{2,6},{6,2},{1... | collective-permute-start | bytes 208904 | tf_op jit(solution)/shard_map/ppermute | solution.py:387
  96.1 2.5 %collective-permute-done.25.refs_1_ = bf16[272,128]{1,0:T(8,128)(2,1)S(1)} collective-permute-done((bf16[272,128]{1,0:T(8,128)(2,1)S(1)}, bf16[272,128]{1,0:T(8,128)(2,1)S(1)}, u32[]{:S(2)}, u32[]{:S(2)}) %collective-permute-start.25) | collective-permute-done | bytes 69664 | tf_op jit(solution)/shard_map/ppermute | solution.py:387
  101.4 2.2 %collective-permute-start.27 = (bf16[32,1024]{1,0:T(8,128)(2,1)S(1)}, bf16[32,1024]{1,0:T(8,128)(2,1)S(1)}, u32[]{:S(2)}, u32[]{:S(2)}) collective-permute-start(bf16[32,1024]{1,0:T(8,128)(2,1)S(1)} %get-tuple-element.246.refs_0_.refs_4_), channel_id=1, source_target_pairs={{0,4},{4,0},{8,12},{12,8},{1,5},{5,1},{9,13},{13,9},{2,6},{6,2},{1... | collective-permute-start | bytes 196616 | tf_op jit(solution)/shard_map/ppermute | solution.py:387
  112.9 3.1 %collective-permute-done.31.refs_1_ = bf16[32,1536]{1,0:T(8,128)(2,1)S(1)} collective-permute-done((bf16[32,1536]{1,0:T(8,128)(2,1)S(1)}, bf16[32,1536]{1,0:T(8,128)(2,1)S(1)}, u32[]{:S(2)}, u32[]{:S(2)}) %collective-permute-start.31) | collective-permute-done | bytes 98336 | tf_op jit(solution)/shard_map/ppermute | solution.py:449
  120.0 2.3 %collective-permute-start.34 = (bf16[272,128]{1,0:T(8,128)(2,1)S(1)}, bf16[272,128]{1,0:T(8,128)(2,1)S(1)}, u32[]{:S(2)}, u32[]{:S(2)}) collective-permute-start(bf16[272,128]{1,0:T(8,128)(2,1)S(1)} %get-tuple-element.278), channel_id=1, source_target_pairs={{0,4},{4,0},{8,12},{12,8},{1,5},{5,1},{9,13},{13,9},{2,6},{6,2},{1... | collective-permute-start | bytes 208904 | tf_op jit(solution)/shard_map/ppermute | solution.py:387
  123.2 2.5 %collective-permute-done.33.refs_1_ = bf16[272,128]{1,0:T(8,128)(2,1)S(1)} collective-permute-done((bf16[272,128]{1,0:T(8,128)(2,1)S(1)}, bf16[272,128]{1,0:T(8,128)(2,1)S(1)}, u32[]{:S(2)}, u32[]{:S(2)}) %collective-permute-start.33) | collective-permute-done | bytes 69664 | tf_op jit(solution)/shard_map/ppermute | solution.py:387
  129.1 2.2 %collective-permute-start.35 = (bf16[32,1024]{1,0:T(8,128)(2,1)S(1)}, bf16[32,1024]{1,0:T(8,128)(2,1)S(1)}, u32[]{:S(2)}, u32[]{:S(2)}) collective-permute-start(bf16[32,1024]{1,0:T(8,128)(2,1)S(1)} %get-tuple-element.279.refs_0_.refs_4_), channel_id=1, source_target_pairs={{0,4},{4,0},{8,12},{12,8},{1,5},{5,1},{9,13},{13,9},{2,6},{6,2},{1... | collective-permute-start | bytes 196616 | tf_op jit(solution)/shard_map/ppermute | solution.py:387
  140.3 3.3 %collective-permute-done.39.refs_1_ = bf16[32,1536]{1,0:T(8,128)(2,1)S(1)} collective-permute-done((bf16[32,1536]{1,0:T(8,128)(2,1)S(1)}, bf16[32,1536]{1,0:T(8,128)(2,1)S(1)}, u32[]{:S(2)}, u32[]{:S(2)}) %collective-permute-start.39) | collective-permute-done | bytes 98336 | tf_op jit(solution)/shard_map/ppermute | solution.py:449
  146.7 2.3 %collective-permute-start.42 = (f32[32,128]{1,0:T(8,128)S(1)}, f32[32,128]{1,0:T(8,128)S(1)}, u32[]{:S(2)}, u32[]{:S(2)}) collective-permute-start(f32[32,128]{1,0:T(8,128)S(1)} %get-tuple-element.292.refs_0_.scalars), channel_id=1, source_target_pairs={{0,4},{4,0},{8,12},{12,8},{1,5},{5,1},{9,13},{13,9},{2,6},{6,2},{1... | collective-permute-start | bytes 49160 | tf_op jit(solution)/shard_map/ppermute | solution.py:387
  (126 shorter events, 86.8 us)
Async XLA Ops:
  6.9 7.6 %collective-permute-start = (bf16[256,128]{1,0:T(8,128)(2,1)S(1)}, bf16[256,128]{1,0:T(8,128)(2,1)S(1)}, u32[]{:S(2)}, u32[]{:S(2)}) collective-permute-start(bf16[256,128]{1,0:T(8,128)(2,1)S(1)} %get-tuple-element.155), channel_id=1, source_target_pairs={{0,12},{4,8},{8,4},{12,0},{1,13},{5,9},{9,5},{13,1},{2,14},{6,10},... | collective-permute-start | bytes 196616 | tf_op jit(solution)/shard_map/ppermute | solution.py:387
  17.7 6.7 %collective-permute-start.5 = (bf16[32,1024]{1,0:T(8,128)(2,1)S(1)}, bf16[32,1024]{1,0:T(8,128)(2,1)S(1)}, u32[]{:S(2)}, u32[]{:S(2)}) collective-permute-start(bf16[32,1024]{1,0:T(8,128)(2,1)S(1)} %get-tuple-element.158.refs_0_.refs_3_), channel_id=1, source_target_pairs={{0,12},{4,8},{8,4},{12,0},{1,13},{5,9},{9,5},{13,1},{2,14},{6,10},... | collective-permute-start | bytes 196616 | tf_op jit(solution)/shard_map/ppermute | solution.py:387
  20.4 6.3 %collective-permute-start.4 = (bf16[32,1024]{1,0:T(8,128)(2,1)S(1)}, bf16[32,1024]{1,0:T(8,128)(2,1)S(1)}, u32[]{:S(2)}, u32[]{:S(2)}) collective-permute-start(bf16[32,1024]{1,0:T(8,128)(2,1)S(1)} %get-tuple-element.158.refs_0_.refs_3_), channel_id=1, source_target_pairs={{0,8},{4,12},{8,0},{12,4},{1,9},{5,13},{9,1},{13,5},{2,10},{6,14},... | collective-permute-start | bytes 196616 | tf_op jit(solution)/shard_map/ppermute | solution.py:387
  20.4 7.1 %collective-permute-start.3 = (bf16[32,1024]{1,0:T(8,128)(2,1)S(1)}, bf16[32,1024]{1,0:T(8,128)(2,1)S(1)}, u32[]{:S(2)}, u32[]{:S(2)}) collective-permute-start(bf16[32,1024]{1,0:T(8,128)(2,1)S(1)} %get-tuple-element.158.refs_0_.refs_3_), channel_id=1, source_target_pairs={{0,4},{4,0},{8,12},{12,8},{1,5},{5,1},{9,13},{13,9},{2,6},{6,2},{1... | collective-permute-start | bytes 196616 | tf_op jit(solution)/shard_map/ppermute | solution.py:387
  35.5 6.3 %collective-permute-start.8 = (bf16[272,128]{1,0:T(8,128)(2,1)S(1)}, bf16[272,128]{1,0:T(8,128)(2,1)S(1)}, u32[]{:S(2)}, u32[]{:S(2)}) collective-permute-start(bf16[272,128]{1,0:T(8,128)(2,1)S(1)} %get-tuple-element.177), channel_id=1, source_target_pairs={{0,12},{4,8},{8,4},{12,0},{1,13},{5,9},{9,5},{13,1},{2,14},{6,10},... | collective-permute-start | bytes 208904 | tf_op jit(solution)/shard_map/ppermute | solution.py:387
  37.7 6.7 %collective-permute-start.9 = (bf16[272,128]{1,0:T(8,128)(2,1)S(1)}, bf16[272,128]{1,0:T(8,128)(2,1)S(1)}, u32[]{:S(2)}, u32[]{:S(2)}) collective-permute-start(bf16[272,128]{1,0:T(8,128)(2,1)S(1)} %get-tuple-element.179), channel_id=1, source_target_pairs={{0,8},{4,12},{8,0},{12,4},{1,9},{5,13},{9,1},{13,5},{2,10},{6,14},... | collective-permute-start | bytes 208904 | tf_op jit(solution)/shard_map/ppermute | solution.py:387
  45.0 6.5 %collective-permute-start.13 = (bf16[32,1024]{1,0:T(8,128)(2,1)S(1)}, bf16[32,1024]{1,0:T(8,128)(2,1)S(1)}, u32[]{:S(2)}, u32[]{:S(2)}) collective-permute-start(bf16[32,1024]{1,0:T(8,128)(2,1)S(1)} %get-tuple-element.182.refs_0_.refs_4_), channel_id=1, source_target_pairs={{0,12},{4,8},{8,4},{12,0},{1,13},{5,9},{9,5},{13,1},{2,14},{6,10},... | collective-permute-start | bytes 196616 | tf_op jit(solution)/shard_map/ppermute | solution.py:387
  46.5 7.1 %collective-permute-start.12 = (bf16[32,1024]{1,0:T(8,128)(2,1)S(1)}, bf16[32,1024]{1,0:T(8,128)(2,1)S(1)}, u32[]{:S(2)}, u32[]{:S(2)}) collective-permute-start(bf16[32,1024]{1,0:T(8,128)(2,1)S(1)} %get-tuple-element.182.refs_0_.refs_4_), channel_id=1, source_target_pairs={{0,8},{4,12},{8,0},{12,4},{1,9},{5,13},{9,1},{13,5},{2,10},{6,14},... | collective-permute-start | bytes 196616 | tf_op jit(solution)/shard_map/ppermute | solution.py:387
  47.3 7.1 %collective-permute-start.11 = (bf16[32,1024]{1,0:T(8,128)(2,1)S(1)}, bf16[32,1024]{1,0:T(8,128)(2,1)S(1)}, u32[]{:S(2)}, u32[]{:S(2)}) collective-permute-start(bf16[32,1024]{1,0:T(8,128)(2,1)S(1)} %get-tuple-element.182.refs_0_.refs_4_), channel_id=1, source_target_pairs={{0,4},{4,0},{8,12},{12,8},{1,5},{5,1},{9,13},{13,9},{2,6},{6,2},{1... | collective-permute-start | bytes 196616 | tf_op jit(solution)/shard_map/ppermute | solution.py:387
  62.6 6.5 %collective-permute-start.16 = (bf16[272,128]{1,0:T(8,128)(2,1)S(1)}, bf16[272,128]{1,0:T(8,128)(2,1)S(1)}, u32[]{:S(2)}, u32[]{:S(2)}) collective-permute-start(bf16[272,128]{1,0:T(8,128)(2,1)S(1)} %get-tuple-element.208), channel_id=1, source_target_pairs={{0,12},{4,8},{8,4},{12,0},{1,13},{5,9},{9,5},{13,1},{2,14},{6,10},... | collective-permute-start | bytes 208904 | tf_op jit(solution)/shard_map/ppermute | solution.py:387
  64.5 7.1 %collective-permute-start.17 = (bf16[272,128]{1,0:T(8,128)(2,1)S(1)}, bf16[272,128]{1,0:T(8,128)(2,1)S(1)}, u32[]{:S(2)}, u32[]{:S(2)}) collective-permute-start(bf16[272,128]{1,0:T(8,128)(2,1)S(1)} %get-tuple-element.210), channel_id=1, source_target_pairs={{0,8},{4,12},{8,0},{12,4},{1,9},{5,13},{9,1},{13,5},{2,10},{6,14},... | collective-permute-start | bytes 208904 | tf_op jit(solution)/shard_map/ppermute | solution.py:387
  72.0 6.7 %collective-permute-start.21 = (bf16[32,1024]{1,0:T(8,128)(2,1)S(1)}, bf16[32,1024]{1,0:T(8,128)(2,1)S(1)}, u32[]{:S(2)}, u32[]{:S(2)}) collective-permute-start(bf16[32,1024]{1,0:T(8,128)(2,1)S(1)} %get-tuple-element.213.refs_0_.refs_4_), channel_id=1, source_target_pairs={{0,12},{4,8},{8,4},{12,0},{1,13},{5,9},{9,5},{13,1},{2,14},{6,10},... | collective-permute-start | bytes 196616 | tf_op jit(solution)/shard_map/ppermute | solution.py:387
  73.5 7.1 %collective-permute-start.20 = (bf16[32,1024]{1,0:T(8,128)(2,1)S(1)}, bf16[32,1024]{1,0:T(8,128)(2,1)S(1)}, u32[]{:S(2)}, u32[]{:S(2)}) collective-permute-start(bf16[32,1024]{1,0:T(8,128)(2,1)S(1)} %get-tuple-element.213.refs_0_.refs_4_), channel_id=1, source_target_pairs={{0,8},{4,12},{8,0},{12,4},{1,9},{5,13},{9,1},{13,5},{2,10},{6,14},... | collective-permute-start | bytes 196616 | tf_op jit(solution)/shard_map/ppermute | solution.py:387
  74.4 7.1 %collective-permute-start.19 = (bf16[32,1024]{1,0:T(8,128)(2,1)S(1)}, bf16[32,1024]{1,0:T(8,128)(2,1)S(1)}, u32[]{:S(2)}, u32[]{:S(2)}) collective-permute-start(bf16[32,1024]{1,0:T(8,128)(2,1)S(1)} %get-tuple-element.213.refs_0_.refs_4_), channel_id=1, source_target_pairs={{0,4},{4,0},{8,12},{12,8},{1,5},{5,1},{9,13},{13,9},{2,6},{6,2},{1... | collective-permute-start | bytes 196616 | tf_op jit(solution)/shard_map/ppermute | solution.py:387
  89.6 6.5 %collective-permute-start.24 = (bf16[272,128]{1,0:T(8,128)(2,1)S(1)}, bf16[272,128]{1,0:T(8,128)(2,1)S(1)}, u32[]{:S(2)}, u32[]{:S(2)}) collective-permute-start(bf16[272,128]{1,0:T(8,128)(2,1)S(1)} %get-tuple-element.241), channel_id=1, source_target_pairs={{0,12},{4,8},{8,4},{12,0},{1,13},{5,9},{9,5},{13,1},{2,14},{6,10},... | collective-permute-start | bytes 208904 | tf_op jit(solution)/shard_map/ppermute | solution.py:387
  91.7 6.9 %collective-permute-start.25 = (bf16[272,128]{1,0:T(8,128)(2,1)S(1)}, bf16[272,128]{1,0:T(8,128)(2,1)S(1)}, u32[]{:S(2)}, u32[]{:S(2)}) collective-permute-start(bf16[272,128]{1,0:T(8,128)(2,1)S(1)} %get-tuple-element.243), channel_id=1, source_target_pairs={{0,8},{4,12},{8,0},{12,4},{1,9},{5,13},{9,1},{13,5},{2,10},{6,14},... | collective-permute-start | bytes 208904 | tf_op jit(solution)/shard_map/ppermute | solution.py:387
  99.1 6.7 %collective-permute-start.29 = (bf16[32,1024]{1,0:T(8,128)(2,1)S(1)}, bf16[32,1024]{1,0:T(8,128)(2,1)S(1)}, u32[]{:S(2)}, u32[]{:S(2)}) collective-permute-start(bf16[32,1024]{1,0:T(8,128)(2,1)S(1)} %get-tuple-element.246.refs_0_.refs_4_), channel_id=1, source_target_pairs={{0,12},{4,8},{8,4},{12,0},{1,13},{5,9},{9,5},{13,1},{2,14},{6,10},... | collective-permute-start | bytes 196616 | tf_op jit(solution)/shard_map/ppermute | solution.py:387
  100.6 7.1 %collective-permute-start.28 = (bf16[32,1024]{1,0:T(8,128)(2,1)S(1)}, bf16[32,1024]{1,0:T(8,128)(2,1)S(1)}, u32[]{:S(2)}, u32[]{:S(2)}) collective-permute-start(bf16[32,1024]{1,0:T(8,128)(2,1)S(1)} %get-tuple-element.246.refs_0_.refs_4_), channel_id=1, source_target_pairs={{0,8},{4,12},{8,0},{12,4},{1,9},{5,13},{9,1},{13,5},{2,10},{6,14},... | collective-permute-start | bytes 196616 | tf_op jit(solution)/shard_map/ppermute | solution.py:387
  101.4 7.1 %collective-permute-start.27 = (bf16[32,1024]{1,0:T(8,128)(2,1)S(1)}, bf16[32,1024]{1,0:T(8,128)(2,1)S(1)}, u32[]{:S(2)}, u32[]{:S(2)}) collective-permute-start(bf16[32,1024]{1,0:T(8,128)(2,1)S(1)} %get-tuple-element.246.refs_0_.refs_4_), channel_id=1, source_target_pairs={{0,4},{4,0},{8,12},{12,8},{1,5},{5,1},{9,13},{13,9},{2,6},{6,2},{1... | collective-permute-start | bytes 196616 | tf_op jit(solution)/shard_map/ppermute | solution.py:387
  116.7 6.5 %collective-permute-start.32 = (bf16[272,128]{1,0:T(8,128)(2,1)S(1)}, bf16[272,128]{1,0:T(8,128)(2,1)S(1)}, u32[]{:S(2)}, u32[]{:S(2)}) collective-permute-start(bf16[272,128]{1,0:T(8,128)(2,1)S(1)} %get-tuple-element.274), channel_id=1, source_target_pairs={{0,12},{4,8},{8,4},{12,0},{1,13},{5,9},{9,5},{13,1},{2,14},{6,10},... | collective-permute-start | bytes 208904 | tf_op jit(solution)/shard_map/ppermute | solution.py:387
  118.9 6.8 %collective-permute-start.33 = (bf16[272,128]{1,0:T(8,128)(2,1)S(1)}, bf16[272,128]{1,0:T(8,128)(2,1)S(1)}, u32[]{:S(2)}, u32[]{:S(2)}) collective-permute-start(bf16[272,128]{1,0:T(8,128)(2,1)S(1)} %get-tuple-element.276), channel_id=1, source_target_pairs={{0,8},{4,12},{8,0},{12,4},{1,9},{5,13},{9,1},{13,5},{2,10},{6,14},... | collective-permute-start | bytes 208904 | tf_op jit(solution)/shard_map/ppermute | solution.py:387
  126.9 6.7 %collective-permute-start.37 = (bf16[32,1024]{1,0:T(8,128)(2,1)S(1)}, bf16[32,1024]{1,0:T(8,128)(2,1)S(1)}, u32[]{:S(2)}, u32[]{:S(2)}) collective-permute-start(bf16[32,1024]{1,0:T(8,128)(2,1)S(1)} %get-tuple-element.279.refs_0_.refs_4_), channel_id=1, source_target_pairs={{0,12},{4,8},{8,4},{12,0},{1,13},{5,9},{9,5},{13,1},{2,14},{6,10},... | collective-permute-start | bytes 196616 | tf_op jit(solution)/shard_map/ppermute | solution.py:387
  128.5 6.9 %collective-permute-start.36 = (bf16[32,1024]{1,0:T(8,128)(2,1)S(1)}, bf16[32,1024]{1,0:T(8,128)(2,1)S(1)}, u32[]{:S(2)}, u32[]{:S(2)}) collective-permute-start(bf16[32,1024]{1,0:T(8,128)(2,1)S(1)} %get-tuple-element.279.refs_0_.refs_4_), channel_id=1, source_target_pairs={{0,8},{4,12},{8,0},{12,4},{1,9},{5,13},{9,1},{13,5},{2,10},{6,14},... | collective-permute-start | bytes 196616 | tf_op jit(solution)/shard_map/ppermute | solution.py:387
  129.1 7.1 %collective-permute-start.35 = (bf16[32,1024]{1,0:T(8,128)(2,1)S(1)}, bf16[32,1024]{1,0:T(8,128)(2,1)S(1)}, u32[]{:S(2)}, u32[]{:S(2)}) collective-permute-start(bf16[32,1024]{1,0:T(8,128)(2,1)S(1)} %get-tuple-element.279.refs_0_.refs_4_), channel_id=1, source_target_pairs={{0,4},{4,0},{8,12},{12,8},{1,5},{5,1},{9,13},{13,9},{2,6},{6,2},{1... | collective-permute-start | bytes 196616 | tf_op jit(solution)/shard_map/ppermute | solution.py:387
  (23 other events, 107.3 us)

commit v4 on v3

--- a/solution.py
+++ b/solution.py
@@ -1,4 +1,5 @@
 import functools
+import math
 
 import jax
 import jax.numpy as jnp
@@ -22,6 +23,10 @@
 
 def xor_pairs(count, offset):
     return [(i, i ^ offset) for i in range(count)]
+
+
+def send_order(count):
+    return [count - 1] + list(range(1, count - 1))
 
 
 def tree_sum(parts):
@@ -258,7 +263,7 @@
         {GRAD_SQ: grad_sq, SMOOTH_SQ: smooth_sq, IMAGE_SQ: image_sq, BETA: beta, GUESS: guess}, sets
     )
     if has_block:
-        send_block(n_pix - 1, value.astype(BF16), green, lost, guess, image_sq, *refs)
+        send_block(send_order(n_pix)[0], value.astype(BF16), green, lost, guess, image_sq, *refs)
 
 
 def send_block(offset, image, green, lost, guess, image_sq, block, missed):
@@ -316,32 +321,48 @@
         own[...] = jnp.dot(rounded[...], green[...], preferred_element_type=F32)
 
 
-def start_kernel(observed, green, own, *refs):
-    count = len(refs) // 2
+def start_kernel(observed_at, green_at, green, own, *refs):
+    refs, (observed, observed_sem, sems) = refs[:-3], refs[-3:]
+    n_pix = len(refs) // 2 + 1
+    width = own.shape[1]
+    order = send_order(n_pix) + [0]
+    first = pltpu.make_async_copy(observed_at, observed, observed_sem)
+    first.start()
+    copies = []
+    for i, offset in enumerate(order):
+        at = own_columns(offset, width)
+        copies.append(pltpu.make_async_copy(green_at.at[:, at], green.at[:, at], sems.at[i]))
+        copies[-1].start()
+    first.wait()
     image = observed[...]
-    for offset in range(count, 0, -1):
-        send_block(offset, image, green, None, None, None, refs[offset - 1], refs[count + offset - 1])
-    own[...] = jnp.dot(image, green[:, own_columns(0, own.shape[1])], preferred_element_type=F32)
+    for i, offset in enumerate(order):
+        copies[i].wait()
+        if offset:
+            send_block(offset, image, green, None, None, None, refs[i], refs[n_pix - 1 + i])
+        else:
+            own[...] = jnp.dot(image, green[:, own_columns(0, width)], preferred_element_type=F32)
 
 
 def receive_start_kernel(own, *refs):
-    got, (grad, rounded) = refs[:-2][::-1], refs[-2:]
+    got, (grad, rounded) = refs[:-2], refs[-2:]
     sets, width = own.shape
-    value = tree_sum([own[...]] + [load_block(ref, sets, width) for ref in got])
+    count = len(got) + 1
+    value = tree_sum(by_offset(count, own[...], [load_block(ref, sets, width) for ref in got]))
     grad[...] = value
     rounded[...] = value.astype(BF16)
 
 
 def step_length(scalars, others):
-    image_sq = tree_sum([scalars[:, IMAGE_SQ : IMAGE_SQ + 1]] + others)
+    own = scalars[:, IMAGE_SQ : IMAGE_SQ + 1]
+    image_sq = tree_sum(by_offset(len(others) + 1, own, others))
     return scalars[:, GRAD_SQ : GRAD_SQ + 1] / (image_sq + scalars[:, SMOOTH_SQ : SMOOTH_SQ + 1])
 
 
 def receive_kernel(own, scalars, old_grad, *refs):
-    got, (grad, rounded, length) = refs[:-3][::-1], refs[-3:]
+    got, (grad, rounded, length) = refs[:-3], refs[-3:]
     sets, width = own.shape
     step_len = step_length(scalars, [load_scalar(ref, sets, width) for ref in got])
-    change = tree_sum([own[...]] + [load_block(ref, sets, width) for ref in got])
+    change = tree_sum(by_offset(len(got) + 1, own[...], [load_block(ref, sets, width) for ref in got]))
     value = old_grad[...] - step_len * change
     grad[...] = value
     rounded[...] = value.astype(BF16)
@@ -360,20 +381,20 @@
 
 
 def finish_kernel(scalars, *refs):
-    got, (direction, image, solution, residual, new_solution, new_residual) = refs[:-6][::-1], refs[-6:]
+    got, (direction, image, solution, residual, new_solution, new_residual) = refs[:-6], refs[-6:]
     step_len = step_length(scalars, [ref[:, IMAGE_SQ : IMAGE_SQ + 1] for ref in got])
     cells = solution.shape[1]
     new_solution[...] = solution[...] + step_len * direction[:, EDGE : EDGE + cells]
     new_residual[...] = residual[...] - step_len * image[...]
 
 
-def call(kernel, operands, outs, scratch=(), flops=0, limit=24 << 20):
+def call(kernel, operands, outs, scratch=(), flops=0, limit=24 << 20, space=pltpu.VMEM):
     vmem = pl.BlockSpec(memory_space=pltpu.VMEM)
-    shapes = [jax.ShapeDtypeStruct(*out) for out in outs]
-    moved = sum(x.size * x.dtype.itemsize for x in [*operands, *shapes])
+    shapes = [jax.ShapeDtypeStruct(*out) if isinstance(out, tuple) else out for out in outs]
+    moved = sum(math.prod(x.shape) * jnp.dtype(x.dtype).itemsize for x in [*operands, *shapes])
     return pl.pallas_call(
         kernel,
-        in_specs=[vmem] * len(operands),
+        in_specs=[pl.BlockSpec(memory_space=space)] * len(operands),
         out_specs=[vmem] * len(outs),
         out_shape=shapes,
         scratch_shapes=list(scratch),
@@ -384,8 +405,12 @@
 
 
 def exchange(blocks, axis, count):
-    got = [lax.ppermute(blocks[k - 1], axis, xor_pairs(count, k)) for k in range(count - 1, 0, -1)]
-    return got[::-1]
+    return {k: lax.ppermute(blocks[k], axis, xor_pairs(count, k)) for k in send_order(count)}
+
+
+def by_offset(count, own, got):
+    found = {0: own, **dict(zip(send_order(count), got))}
+    return [found[k] for k in range(count)]
 
 
 def on_device(green, observed):
@@ -405,40 +430,48 @@
     line, wide, edge = ((sets, pixels), F32), ((sets, cells), F32), ((sets, EDGE), F32)
     ring = ((sets, cells + 2 * EDGE), F32)
 
-    lost = []
+    order = send_order(n_pix) if direct else []
+    lost, got = {}, {}
     if direct:
-        own, *rest = call(start_kernel, [observed, green], [shard] + [plain] * count + [shard] * count, flops=flops)
-        blocks, lost = rest[:count], rest[count:]
-        got = exchange(blocks, "pix", n_pix)
+        green, own, *rest = call(
+            start_kernel,
+            [observed, green],
+            [pltpu.VMEM(*out) for out in [(green.shape, BF16), shard] + [plain] * count + [shard] * count],
+            [pltpu.VMEM(observed.shape, BF16), pltpu.SemaphoreType.DMA, pltpu.SemaphoreType.DMA((n_pix,))],
+            flops,
+            limit=48 << 20,
+            space=pltpu.HBM,
+        )
+        lost = dict(zip(order, rest[count:]))
+        got = exchange(dict(zip(order, rest)), "pix", n_pix)
     else:
         partial = jnp.dot(observed, green, preferred_element_type=F32)
-        own, got = lax.psum_scatter(partial, "pix", scatter_dimension=1, tiled=True), []
-    grad, rounded_grad = call(receive_start_kernel, [own, *got[::-1]], [shard, rounded_shard])
+        own = lax.psum_scatter(partial, "pix", scatter_dimension=1, tiled=True)
+    grad, rounded_grad = call(receive_start_kernel, [own, *got.values()], [shard, rounded_shard])
     solution = jnp.zeros((sets, cells), F32)
     residual = observed.astype(F32)
     scalars = image = direction = twice = None
     for sweep in range(ITERS):
         first, final = sweep == 0, sweep + 1 == ITERS
         if direct:
-            shards = [rounded_grad] + exchange([rounded_grad] * count, "pix", n_pix)
+            shards = {0: rounded_grad, **exchange(dict.fromkeys(order, rounded_grad), "pix", n_pix)}
         else:
-            shards = [lax.all_gather(rounded_grad, "pix", axis=1, tiled=True)]
+            shards = {0: lax.all_gather(rounded_grad, "pix", axis=1, tiled=True)}
         beside_them = [] if first else [twice]
 
         def message_of(step):
             return ((sets, pixels + LANES + edge_columns(step, n_par)), F32 if step == 1 else BF16)
 
-        order = [0] + list(range(len(shards) - 1, 0, -1))
         partial, parts = [], {}
-        for k in order[:-1]:
+        closing = ([0] + order)[-1]
+        for k in ([0] + order)[:-1]:
             kernel = functools.partial(shard_kernel, k, len(shards), first, False, n_par)
             out, parts[k] = call(kernel, [shards[k], green, *beside_them, *partial], [line, scalar], flops=part_flops)
             partial = [out]
-        k = order[-1]
         others = sorted(parts)
         whole, message = call(
-            functools.partial(shard_kernel, k, len(shards), first, True, n_par),
-            [shards[k], green, *beside_them, *partial]
+            functools.partial(shard_kernel, closing, len(shards), first, True, n_par),
+            [shards[closing], green, *beside_them, *partial]
             + [shards[o] for o in others]
             + [parts[o] for o in others],
             [((sets, cells), BF16), message_of(1)],
@@ -458,13 +491,12 @@
         if above is None:
             above = below = jnp.zeros(edge[0], F32)
         has_block = direct and not final
-        missed = [None] * count
-        blocks = [None] * count
+        blocks, missed = {}, {}
         scalars, image, rounded, above, below, *rest = call(
             functools.partial(image_kernel, step, n_pix, first, has_block),
             [message, got, above, below]
             + ([] if first else [scalars, image])
-            + ([green, lost[-1]] if has_block else []),
+            + ([green, lost[order[0]]] if has_block else []),
             [scalar, line, ((sets, pixels), BF16), edge, edge] + ([block, shard] if has_block else []),
             flops=part_flops if has_block else 0,
         )
@@ -476,17 +508,17 @@
                 [ring],
             )
             if direct:
-                got = exchange([scalars] * count, "pix", n_pix)
+                got = exchange(dict.fromkeys(order, scalars), "pix", n_pix)
             else:
-                got = []
+                got = {}
                 scalars = scalars.at[:, IMAGE_SQ].set(lax.psum(scalars[:, IMAGE_SQ], "pix"))
-            return tuple(call(finish_kernel, [scalars, *got[::-1], direction, image, solution, residual], [wide, line]))
+            return tuple(call(finish_kernel, [scalars, *got.values(), direction, image, solution, residual], [wide, line]))
         if direct:
-            blocks[-1], missed[-1] = rest
-            for k in range(count - 1, 0, -1):
-                blocks[k - 1], missed[k - 1] = call(
+            blocks[order[0]], missed[order[0]] = rest
+            for k in order[1:]:
+                blocks[k], missed[k] = call(
                     functools.partial(block_kernel, k),
-                    [rounded, scalars, green, lost[k - 1]],
+                    [rounded, scalars, green, lost[k]],
                     [block, shard],
                     flops=part_flops,
                 )
@@ -500,18 +532,19 @@
         if direct:
             got = exchange(blocks, "pix", n_pix)
         else:
-            got = []
+            got = {}
             own = lax.psum_scatter(own, "pix", scatter_dimension=1, tiled=True)
             own = own + lax.dynamic_slice_in_dim(twice, here * width, width, axis=1)
             scalars = scalars.at[:, IMAGE_SQ].set(lax.psum(scalars[:, IMAGE_SQ], "pix"))
         grad, rounded_grad, length = call(
-            receive_kernel, [own, scalars, grad, *got[::-1]], [shard, rounded_shard, scalar]
+            receive_kernel, [own, scalars, grad, *got.values()], [shard, rounded_shard, scalar]
         )
-        solution, residual, *lost = call(
+        solution, residual, *rest = call(
             functools.partial(update_kernel, count),
-            [length, direction, image, solution, residual, *lost, *missed],
+            [length, direction, image, solution, residual, *lost.values(), *missed.values()],
             [wide, line] + [shard] * count,
         )
+        lost = dict(zip(order, rest))
 
 
 def solution(mesh):

time: 152 us -> 144 us (0.947)
  waiting for transfers between devices: 53.4 us -> 47.9 us
  local copies, waits for them, and re-layouts: 4.6 us -> 0.04 us
  Pallas kernels: 34.7 us -> 37.2 us
    ppermute x33, waiting for transfers between devices: 30.3 us -> 24.6 us  [exchange(): lax.ppermute(blocks[k], axis, xor_pairs(count, k))]
    unnamed x8 -> x2, local copies, waits for them, and re-layouts: 4.56 us -> 0.01 us
    pallas_call x54, Pallas kernels: 34.7 us -> 37.2 us  [call(): pl.pallas_call(kernel, in_specs=[pl.BlockSpec(memory_space=space)] * len(...]
where the time goes in v4:
time: 144 us
  starting transfers between devices  58.2 us (40%)
  waiting for transfers between devices  47.9 us (33%)
  Pallas kernels  37.2 us (26%)
    ppermute x33, starting transfers between devices, exchange(): lax.ppermute(blocks[k], axis, xor_pairs(count, k))  50.6 us
    pallas_call x54, Pallas kernels, call(): pl.pallas_call(kernel, in_specs=[pl.BlockSpec(memory_space=space)] * len(...  37.2 us
    ppermute x33, waiting for transfers between devices, exchange(): lax.ppermute(blocks[k], axis, xor_pairs(count, k))  24.6 us
    ppermute x10, waiting for transfers between devices, on_device(): got = lax.ppermute(message, 'par', xor_pairs(n_par, step))  23.3 us
    ppermute x10, starting transfers between devices, on_device(): got = lax.ppermute(message, 'par', xor_pairs(n_par, step))  7.57 us
  transfers between devices with their start and end apart: 43, of which 32 were waited for; matrix products, arithmetic and copies ran while one was open for 0% of the time, Pallas kernels for 14%

profile of v4, /device:TPU:0, one launch (start us, length us, event | category | flops | bytes accessed | tf_op | source)
XLA Modules:
  0.0 144.3 jit_solution(1715458856993857659)
XLA Ops:
  0.6 4.4 %start_kernel.1 = (bf16[1152,4096]{1,0:T(8,128)(2,1)S(1)}, f32[32,1024]{1,0:T(8,128)S(1)}, bf16[256,128]{1,0:T(8,128)(2,1)S(1)}, bf16[256,128]{1,0:T(8,128)(2,1)...) custom-call(bf16[32,1152]{1,0:T(8,128)(2,1)} %observed_at.1, ...), custom_call_target="tpu_custom_call" | custom-call | flops 301989888 | bytes 19668992 | tf_op jit(solution)/shard_map/start_kernel/pallas_call | solution.py:395
  5.0 5.1 %collective-permute-start = (bf16[256,128]{1,0:T(8,128)(2,1)S(1)}, bf16[256,128]{1,0:T(8,128)(2,1)S(1)}, u32[]{:S(2)}, u32[]{:S(2)}) collective-permute-start(bf16[256,128]{1,0:T(8,128)(2,1)S(1)} %get-tuple-element.156), channel_id=1, source_target_pairs={{0,12},{4,8},{8,4},{12,0},{1,13},{5,9},{9,5},{13,1},{2,14},{6,10},... | collective-permute-start | bytes 196616 | tf_op jit(solution)/shard_map/ppermute | solution.py:408
  10.8 2.3 %collective-permute-done.refs_0_ = bf16[256,128]{1,0:T(8,128)(2,1)S(1)} collective-permute-done((bf16[256,128]{1,0:T(8,128)(2,1)S(1)}, bf16[256,128]{1,0:T(8,128)(2,1)S(1)}, u32[]{:S(2)}, u32[]{:S(2)}) %collective-permute-start) | collective-permute-done | bytes 65568 | tf_op jit(solution)/shard_map/ppermute | solution.py:408
  15.8 2.9 %collective-permute-start.5 = (bf16[32,1024]{1,0:T(8,128)(2,1)S(1)}, bf16[32,1024]{1,0:T(8,128)(2,1)S(1)}, u32[]{:S(2)}, u32[]{:S(2)}) collective-permute-start(bf16[32,1024]{1,0:T(8,128)(2,1)S(1)} %get-tuple-element.159.refs_0_.refs_3_), channel_id=1, source_target_pairs={{0,12},{4,8},{8,4},{12,0},{1,13},{5,9},{9,5},{13,1},{2,14},{6,10},... | collective-permute-start | bytes 196616 | tf_op jit(solution)/shard_map/ppermute | solution.py:408
  28.1 3.3 %collective-permute-done.7.refs_1_ = bf16[32,1536]{1,0:T(8,128)(2,1)S(1)} collective-permute-done((bf16[32,1536]{1,0:T(8,128)(2,1)S(1)}, bf16[32,1536]{1,0:T(8,128)(2,1)S(1)}, u32[]{:S(2)}, u32[]{:S(2)}) %collective-permute-start.7) | collective-permute-done | bytes 98336 | tf_op jit(solution)/shard_map/ppermute | solution.py:482
  32.0 2.6 %collective-permute-start.8 = (bf16[272,128]{1,0:T(8,128)(2,1)S(1)}, bf16[272,128]{1,0:T(8,128)(2,1)S(1)}, u32[]{:S(2)}, u32[]{:S(2)}) collective-permute-start(bf16[272,128]{1,0:T(8,128)(2,1)S(1)} %get-tuple-element.179), channel_id=1, source_target_pairs={{0,12},{4,8},{8,4},{12,0},{1,13},{5,9},{9,5},{13,1},{2,14},{6,10},... | collective-permute-start | bytes 208904 | tf_op jit(solution)/shard_map/ppermute | solution.py:408
  35.8 1.9 %collective-permute-start.10 = (bf16[272,128]{1,0:T(8,128)(2,1)S(1)}, bf16[272,128]{1,0:T(8,128)(2,1)S(1)}, u32[]{:S(2)}, u32[]{:S(2)}) collective-permute-start(bf16[272,128]{1,0:T(8,128)(2,1)S(1)} %get-tuple-element.183), channel_id=1, source_target_pairs={{0,8},{4,12},{8,0},{12,4},{1,9},{5,13},{9,1},{13,5},{2,10},{6,14},... | collective-permute-start | bytes 208904 | tf_op jit(solution)/shard_map/ppermute | solution.py:408
  41.6 2.8 %collective-permute-start.13 = (bf16[32,1024]{1,0:T(8,128)(2,1)S(1)}, bf16[32,1024]{1,0:T(8,128)(2,1)S(1)}, u32[]{:S(2)}, u32[]{:S(2)}) collective-permute-start(bf16[32,1024]{1,0:T(8,128)(2,1)S(1)} %get-tuple-element.184.refs_0_.refs_4_), channel_id=1, source_target_pairs={{0,12},{4,8},{8,4},{12,0},{1,13},{5,9},{9,5},{13,1},{2,14},{6,10},... | collective-permute-start | bytes 196616 | tf_op jit(solution)/shard_map/ppermute | solution.py:408
  54.4 3.1 %collective-permute-done.15.refs_1_ = bf16[32,1536]{1,0:T(8,128)(2,1)S(1)} collective-permute-done((bf16[32,1536]{1,0:T(8,128)(2,1)S(1)}, bf16[32,1536]{1,0:T(8,128)(2,1)S(1)}, u32[]{:S(2)}, u32[]{:S(2)}) %collective-permute-start.15) | collective-permute-done | bytes 98336 | tf_op jit(solution)/shard_map/ppermute | solution.py:482
  58.2 2.2 %collective-permute-start.16 = (bf16[272,128]{1,0:T(8,128)(2,1)S(1)}, bf16[272,128]{1,0:T(8,128)(2,1)S(1)}, u32[]{:S(2)}, u32[]{:S(2)}) collective-permute-start(bf16[272,128]{1,0:T(8,128)(2,1)S(1)} %get-tuple-element.210), channel_id=1, source_target_pairs={{0,12},{4,8},{8,4},{12,0},{1,13},{5,9},{9,5},{13,1},{2,14},{6,10},... | collective-permute-start | bytes 208904 | tf_op jit(solution)/shard_map/ppermute | solution.py:408
  61.6 2.3 %collective-permute-start.18 = (bf16[272,128]{1,0:T(8,128)(2,1)S(1)}, bf16[272,128]{1,0:T(8,128)(2,1)S(1)}, u32[]{:S(2)}, u32[]{:S(2)}) collective-permute-start(bf16[272,128]{1,0:T(8,128)(2,1)S(1)} %get-tuple-element.214), channel_id=1, source_target_pairs={{0,8},{4,12},{8,0},{12,4},{1,9},{5,13},{9,1},{13,5},{2,10},{6,14},... | collective-permute-start | bytes 208904 | tf_op jit(solution)/shard_map/ppermute | solution.py:408
  67.4 2.1 %collective-permute-start.21 = (bf16[32,1024]{1,0:T(8,128)(2,1)S(1)}, bf16[32,1024]{1,0:T(8,128)(2,1)S(1)}, u32[]{:S(2)}, u32[]{:S(2)}) collective-permute-start(bf16[32,1024]{1,0:T(8,128)(2,1)S(1)} %get-tuple-element.215.refs_0_.refs_4_), channel_id=1, source_target_pairs={{0,12},{4,8},{8,4},{12,0},{1,13},{5,9},{9,5},{13,1},{2,14},{6,10},... | collective-permute-start | bytes 196616 | tf_op jit(solution)/shard_map/ppermute | solution.py:408
  70.0 1.8 %collective-permute-start.19 = (bf16[32,1024]{1,0:T(8,128)(2,1)S(1)}, bf16[32,1024]{1,0:T(8,128)(2,1)S(1)}, u32[]{:S(2)}, u32[]{:S(2)}) collective-permute-start(bf16[32,1024]{1,0:T(8,128)(2,1)S(1)} %get-tuple-element.215.refs_0_.refs_4_), channel_id=1, source_target_pairs={{0,8},{4,12},{8,0},{12,4},{1,9},{5,13},{9,1},{13,5},{2,10},{6,14},... | collective-permute-start | bytes 196616 | tf_op jit(solution)/shard_map/ppermute | solution.py:408
  79.9 3.0 %collective-permute-done.23.refs_1_ = bf16[32,1536]{1,0:T(8,128)(2,1)S(1)} collective-permute-done((bf16[32,1536]{1,0:T(8,128)(2,1)S(1)}, bf16[32,1536]{1,0:T(8,128)(2,1)S(1)}, u32[]{:S(2)}, u32[]{:S(2)}) %collective-permute-start.23) | collective-permute-done | bytes 98336 | tf_op jit(solution)/shard_map/ppermute | solution.py:482
  83.6 2.7 %collective-permute-start.24 = (bf16[272,128]{1,0:T(8,128)(2,1)S(1)}, bf16[272,128]{1,0:T(8,128)(2,1)S(1)}, u32[]{:S(2)}, u32[]{:S(2)}) collective-permute-start(bf16[272,128]{1,0:T(8,128)(2,1)S(1)} %get-tuple-element.243), channel_id=1, source_target_pairs={{0,12},{4,8},{8,4},{12,0},{1,13},{5,9},{9,5},{13,1},{2,14},{6,10},... | collective-permute-start | bytes 208904 | tf_op jit(solution)/shard_map/ppermute | solution.py:408
  87.4 1.8 %collective-permute-start.26 = (bf16[272,128]{1,0:T(8,128)(2,1)S(1)}, bf16[272,128]{1,0:T(8,128)(2,1)S(1)}, u32[]{:S(2)}, u32[]{:S(2)}) collective-permute-start(bf16[272,128]{1,0:T(8,128)(2,1)S(1)} %get-tuple-element.247), channel_id=1, source_target_pairs={{0,8},{4,12},{8,0},{12,4},{1,9},{5,13},{9,1},{13,5},{2,10},{6,14},... | collective-permute-start | bytes 208904 | tf_op jit(solution)/shard_map/ppermute | solution.py:408
  93.0 1.8 %collective-permute-start.29 = (bf16[32,1024]{1,0:T(8,128)(2,1)S(1)}, bf16[32,1024]{1,0:T(8,128)(2,1)S(1)}, u32[]{:S(2)}, u32[]{:S(2)}) collective-permute-start(bf16[32,1024]{1,0:T(8,128)(2,1)S(1)} %get-tuple-element.248.refs_0_.refs_4_), channel_id=1, source_target_pairs={{0,12},{4,8},{8,4},{12,0},{1,13},{5,9},{9,5},{13,1},{2,14},{6,10},... | collective-permute-start | bytes 196616 | tf_op jit(solution)/shard_map/ppermute | solution.py:408
  95.3 2.1 %collective-permute-start.27 = (bf16[32,1024]{1,0:T(8,128)(2,1)S(1)}, bf16[32,1024]{1,0:T(8,128)(2,1)S(1)}, u32[]{:S(2)}, u32[]{:S(2)}) collective-permute-start(bf16[32,1024]{1,0:T(8,128)(2,1)S(1)} %get-tuple-element.248.refs_0_.refs_4_), channel_id=1, source_target_pairs={{0,8},{4,12},{8,0},{12,4},{1,9},{5,13},{9,1},{13,5},{2,10},{6,14},... | collective-permute-start | bytes 196616 | tf_op jit(solution)/shard_map/ppermute | solution.py:408
  105.8 3.1 %collective-permute-done.31.refs_1_ = bf16[32,1536]{1,0:T(8,128)(2,1)S(1)} collective-permute-done((bf16[32,1536]{1,0:T(8,128)(2,1)S(1)}, bf16[32,1536]{1,0:T(8,128)(2,1)S(1)}, u32[]{:S(2)}, u32[]{:S(2)}) %collective-permute-start.31) | collective-permute-done | bytes 98336 | tf_op jit(solution)/shard_map/ppermute | solution.py:482
  109.7 2.3 %collective-permute-start.32 = (bf16[272,128]{1,0:T(8,128)(2,1)S(1)}, bf16[272,128]{1,0:T(8,128)(2,1)S(1)}, u32[]{:S(2)}, u32[]{:S(2)}) collective-permute-start(bf16[272,128]{1,0:T(8,128)(2,1)S(1)} %get-tuple-element.276), channel_id=1, source_target_pairs={{0,12},{4,8},{8,4},{12,0},{1,13},{5,9},{9,5},{13,1},{2,14},{6,10},... | collective-permute-start | bytes 208904 | tf_op jit(solution)/shard_map/ppermute | solution.py:408
  113.2 2.1 %collective-permute-start.34 = (bf16[272,128]{1,0:T(8,128)(2,1)S(1)}, bf16[272,128]{1,0:T(8,128)(2,1)S(1)}, u32[]{:S(2)}, u32[]{:S(2)}) collective-permute-start(bf16[272,128]{1,0:T(8,128)(2,1)S(1)} %get-tuple-element.280), channel_id=1, source_target_pairs={{0,8},{4,12},{8,0},{12,4},{1,9},{5,13},{9,1},{13,5},{2,10},{6,14},... | collective-permute-start | bytes 208904 | tf_op jit(solution)/shard_map/ppermute | solution.py:408
  119.4 1.9 %collective-permute-start.37 = (bf16[32,1024]{1,0:T(8,128)(2,1)S(1)}, bf16[32,1024]{1,0:T(8,128)(2,1)S(1)}, u32[]{:S(2)}, u32[]{:S(2)}) collective-permute-start(bf16[32,1024]{1,0:T(8,128)(2,1)S(1)} %get-tuple-element.281.refs_0_.refs_4_), channel_id=1, source_target_pairs={{0,12},{4,8},{8,4},{12,0},{1,13},{5,9},{9,5},{13,1},{2,14},{6,10},... | collective-permute-start | bytes 196616 | tf_op jit(solution)/shard_map/ppermute | solution.py:408
  131.6 3.3 %collective-permute-done.39.refs_1_ = bf16[32,1536]{1,0:T(8,128)(2,1)S(1)} collective-permute-done((bf16[32,1536]{1,0:T(8,128)(2,1)S(1)}, bf16[32,1536]{1,0:T(8,128)(2,1)S(1)}, u32[]{:S(2)}, u32[]{:S(2)}) %collective-permute-start.39) | collective-permute-done | bytes 98336 | tf_op jit(solution)/shard_map/ppermute | solution.py:482
  135.9 2.7 %collective-permute-start.40 = (f32[32,128]{1,0:T(8,128)S(1)}, f32[32,128]{1,0:T(8,128)S(1)}, u32[]{:S(2)}, u32[]{:S(2)}) collective-permute-start(f32[32,128]{1,0:T(8,128)S(1)} %get-tuple-element.294.refs_0_.scalars), channel_id=1, source_target_pairs={{0,12},{4,8},{8,4},{12,0},{1,13},{5,9},{9,5},{13,1},{2,14},{6,10},... | collective-permute-start | bytes 49160 | tf_op jit(solution)/shard_map/ppermute | solution.py:408
  (120 shorter events, 79.5 us)
Async XLA Ops:
  5.0 8.0 %collective-permute-start = (bf16[256,128]{1,0:T(8,128)(2,1)S(1)}, bf16[256,128]{1,0:T(8,128)(2,1)S(1)}, u32[]{:S(2)}, u32[]{:S(2)}) collective-permute-start(bf16[256,128]{1,0:T(8,128)(2,1)S(1)} %get-tuple-element.156), channel_id=1, source_target_pairs={{0,12},{4,8},{8,4},{12,0},{1,13},{5,9},{9,5},{13,1},{2,14},{6,10},... | collective-permute-start | bytes 196616 | tf_op jit(solution)/shard_map/ppermute | solution.py:408
  10.2 5.6 %collective-permute-start.2 = (bf16[256,128]{1,0:T(8,128)(2,1)S(1)}, bf16[256,128]{1,0:T(8,128)(2,1)S(1)}, u32[]{:S(2)}, u32[]{:S(2)}) collective-permute-start(bf16[256,128]{1,0:T(8,128)(2,1)S(1)} %get-tuple-element.158), channel_id=1, source_target_pairs={{0,8},{4,12},{8,0},{12,4},{1,9},{5,13},{9,1},{13,5},{2,10},{6,14},... | collective-permute-start | bytes 196616 | tf_op jit(solution)/shard_map/ppermute | solution.py:408
  15.8 6.5 %collective-permute-start.5 = (bf16[32,1024]{1,0:T(8,128)(2,1)S(1)}, bf16[32,1024]{1,0:T(8,128)(2,1)S(1)}, u32[]{:S(2)}, u32[]{:S(2)}) collective-permute-start(bf16[32,1024]{1,0:T(8,128)(2,1)S(1)} %get-tuple-element.159.refs_0_.refs_3_), channel_id=1, source_target_pairs={{0,12},{4,8},{8,4},{12,0},{1,13},{5,9},{9,5},{13,1},{2,14},{6,10},... | collective-permute-start | bytes 196616 | tf_op jit(solution)/shard_map/ppermute | solution.py:408
  18.8 5.3 %collective-permute-start.3 = (bf16[32,1024]{1,0:T(8,128)(2,1)S(1)}, bf16[32,1024]{1,0:T(8,128)(2,1)S(1)}, u32[]{:S(2)}, u32[]{:S(2)}) collective-permute-start(bf16[32,1024]{1,0:T(8,128)(2,1)S(1)} %get-tuple-element.159.refs_0_.refs_3_), channel_id=1, source_target_pairs={{0,8},{4,12},{8,0},{12,4},{1,9},{5,13},{9,1},{13,5},{2,10},{6,14},... | collective-permute-start | bytes 196616 | tf_op jit(solution)/shard_map/ppermute | solution.py:408
  32.0 6.6 %collective-permute-start.8 = (bf16[272,128]{1,0:T(8,128)(2,1)S(1)}, bf16[272,128]{1,0:T(8,128)(2,1)S(1)}, u32[]{:S(2)}, u32[]{:S(2)}) collective-permute-start(bf16[272,128]{1,0:T(8,128)(2,1)S(1)} %get-tuple-element.179), channel_id=1, source_target_pairs={{0,12},{4,8},{8,4},{12,0},{1,13},{5,9},{9,5},{13,1},{2,14},{6,10},... | collective-permute-start | bytes 208904 | tf_op jit(solution)/shard_map/ppermute | solution.py:408
  35.8 5.5 %collective-permute-start.10 = (bf16[272,128]{1,0:T(8,128)(2,1)S(1)}, bf16[272,128]{1,0:T(8,128)(2,1)S(1)}, u32[]{:S(2)}, u32[]{:S(2)}) collective-permute-start(bf16[272,128]{1,0:T(8,128)(2,1)S(1)} %get-tuple-element.183), channel_id=1, source_target_pairs={{0,8},{4,12},{8,0},{12,4},{1,9},{5,13},{9,1},{13,5},{2,10},{6,14},... | collective-permute-start | bytes 208904 | tf_op jit(solution)/shard_map/ppermute | solution.py:408
  41.6 6.9 %collective-permute-start.13 = (bf16[32,1024]{1,0:T(8,128)(2,1)S(1)}, bf16[32,1024]{1,0:T(8,128)(2,1)S(1)}, u32[]{:S(2)}, u32[]{:S(2)}) collective-permute-start(bf16[32,1024]{1,0:T(8,128)(2,1)S(1)} %get-tuple-element.184.refs_0_.refs_4_), channel_id=1, source_target_pairs={{0,12},{4,8},{8,4},{12,0},{1,13},{5,9},{9,5},{13,1},{2,14},{6,10},... | collective-permute-start | bytes 196616 | tf_op jit(solution)/shard_map/ppermute | solution.py:408
  44.4 5.6 %collective-permute-start.11 = (bf16[32,1024]{1,0:T(8,128)(2,1)S(1)}, bf16[32,1024]{1,0:T(8,128)(2,1)S(1)}, u32[]{:S(2)}, u32[]{:S(2)}) collective-permute-start(bf16[32,1024]{1,0:T(8,128)(2,1)S(1)} %get-tuple-element.184.refs_0_.refs_4_), channel_id=1, source_target_pairs={{0,8},{4,12},{8,0},{12,4},{1,9},{5,13},{9,1},{13,5},{2,10},{6,14},... | collective-permute-start | bytes 196616 | tf_op jit(solution)/shard_map/ppermute | solution.py:408
  58.2 6.4 %collective-permute-start.16 = (bf16[272,128]{1,0:T(8,128)(2,1)S(1)}, bf16[272,128]{1,0:T(8,128)(2,1)S(1)}, u32[]{:S(2)}, u32[]{:S(2)}) collective-permute-start(bf16[272,128]{1,0:T(8,128)(2,1)S(1)} %get-tuple-element.210), channel_id=1, source_target_pairs={{0,12},{4,8},{8,4},{12,0},{1,13},{5,9},{9,5},{13,1},{2,14},{6,10},... | collective-permute-start | bytes 208904 | tf_op jit(solution)/shard_map/ppermute | solution.py:408
  61.6 5.5 %collective-permute-start.18 = (bf16[272,128]{1,0:T(8,128)(2,1)S(1)}, bf16[272,128]{1,0:T(8,128)(2,1)S(1)}, u32[]{:S(2)}, u32[]{:S(2)}) collective-permute-start(bf16[272,128]{1,0:T(8,128)(2,1)S(1)} %get-tuple-element.214), channel_id=1, source_target_pairs={{0,8},{4,12},{8,0},{12,4},{1,9},{5,13},{9,1},{13,5},{2,10},{6,14},... | collective-permute-start | bytes 208904 | tf_op jit(solution)/shard_map/ppermute | solution.py:408
  67.4 6.4 %collective-permute-start.21 = (bf16[32,1024]{1,0:T(8,128)(2,1)S(1)}, bf16[32,1024]{1,0:T(8,128)(2,1)S(1)}, u32[]{:S(2)}, u32[]{:S(2)}) collective-permute-start(bf16[32,1024]{1,0:T(8,128)(2,1)S(1)} %get-tuple-element.215.refs_0_.refs_4_), channel_id=1, source_target_pairs={{0,12},{4,8},{8,4},{12,0},{1,13},{5,9},{9,5},{13,1},{2,14},{6,10},... | collective-permute-start | bytes 196616 | tf_op jit(solution)/shard_map/ppermute | solution.py:408
  69.5 5.1 %collective-permute-start.20 = (bf16[32,1024]{1,0:T(8,128)(2,1)S(1)}, bf16[32,1024]{1,0:T(8,128)(2,1)S(1)}, u32[]{:S(2)}, u32[]{:S(2)}) collective-permute-start(bf16[32,1024]{1,0:T(8,128)(2,1)S(1)} %get-tuple-element.215.refs_0_.refs_4_), channel_id=1, source_target_pairs={{0,4},{4,0},{8,12},{12,8},{1,5},{5,1},{9,13},{13,9},{2,6},{6,2},{1... | collective-permute-start | bytes 196616 | tf_op jit(solution)/shard_map/ppermute | solution.py:408
  70.0 5.4 %collective-permute-start.19 = (bf16[32,1024]{1,0:T(8,128)(2,1)S(1)}, bf16[32,1024]{1,0:T(8,128)(2,1)S(1)}, u32[]{:S(2)}, u32[]{:S(2)}) collective-permute-start(bf16[32,1024]{1,0:T(8,128)(2,1)S(1)} %get-tuple-element.215.refs_0_.refs_4_), channel_id=1, source_target_pairs={{0,8},{4,12},{8,0},{12,4},{1,9},{5,13},{9,1},{13,5},{2,10},{6,14},... | collective-permute-start | bytes 196616 | tf_op jit(solution)/shard_map/ppermute | solution.py:408
  83.6 6.4 %collective-permute-start.24 = (bf16[272,128]{1,0:T(8,128)(2,1)S(1)}, bf16[272,128]{1,0:T(8,128)(2,1)S(1)}, u32[]{:S(2)}, u32[]{:S(2)}) collective-permute-start(bf16[272,128]{1,0:T(8,128)(2,1)S(1)} %get-tuple-element.243), channel_id=1, source_target_pairs={{0,12},{4,8},{8,4},{12,0},{1,13},{5,9},{9,5},{13,1},{2,14},{6,10},... | collective-permute-start | bytes 208904 | tf_op jit(solution)/shard_map/ppermute | solution.py:408
  87.4 5.3 %collective-permute-start.26 = (bf16[272,128]{1,0:T(8,128)(2,1)S(1)}, bf16[272,128]{1,0:T(8,128)(2,1)S(1)}, u32[]{:S(2)}, u32[]{:S(2)}) collective-permute-start(bf16[272,128]{1,0:T(8,128)(2,1)S(1)} %get-tuple-element.247), channel_id=1, source_target_pairs={{0,8},{4,12},{8,0},{12,4},{1,9},{5,13},{9,1},{13,5},{2,10},{6,14},... | collective-permute-start | bytes 208904 | tf_op jit(solution)/shard_map/ppermute | solution.py:408
  93.0 6.7 %collective-permute-start.29 = (bf16[32,1024]{1,0:T(8,128)(2,1)S(1)}, bf16[32,1024]{1,0:T(8,128)(2,1)S(1)}, u32[]{:S(2)}, u32[]{:S(2)}) collective-permute-start(bf16[32,1024]{1,0:T(8,128)(2,1)S(1)} %get-tuple-element.248.refs_0_.refs_4_), channel_id=1, source_target_pairs={{0,12},{4,8},{8,4},{12,0},{1,13},{5,9},{9,5},{13,1},{2,14},{6,10},... | collective-permute-start | bytes 196616 | tf_op jit(solution)/shard_map/ppermute | solution.py:408
  94.8 5.7 %collective-permute-start.28 = (bf16[32,1024]{1,0:T(8,128)(2,1)S(1)}, bf16[32,1024]{1,0:T(8,128)(2,1)S(1)}, u32[]{:S(2)}, u32[]{:S(2)}) collective-permute-start(bf16[32,1024]{1,0:T(8,128)(2,1)S(1)} %get-tuple-element.248.refs_0_.refs_4_), channel_id=1, source_target_pairs={{0,4},{4,0},{8,12},{12,8},{1,5},{5,1},{9,13},{13,9},{2,6},{6,2},{1... | collective-permute-start | bytes 196616 | tf_op jit(solution)/shard_map/ppermute | solution.py:408
  95.3 6.2 %collective-permute-start.27 = (bf16[32,1024]{1,0:T(8,128)(2,1)S(1)}, bf16[32,1024]{1,0:T(8,128)(2,1)S(1)}, u32[]{:S(2)}, u32[]{:S(2)}) collective-permute-start(bf16[32,1024]{1,0:T(8,128)(2,1)S(1)} %get-tuple-element.248.refs_0_.refs_4_), channel_id=1, source_target_pairs={{0,8},{4,12},{8,0},{12,4},{1,9},{5,13},{9,1},{13,5},{2,10},{6,14},... | collective-permute-start | bytes 196616 | tf_op jit(solution)/shard_map/ppermute | solution.py:408
  109.7 6.4 %collective-permute-start.32 = (bf16[272,128]{1,0:T(8,128)(2,1)S(1)}, bf16[272,128]{1,0:T(8,128)(2,1)S(1)}, u32[]{:S(2)}, u32[]{:S(2)}) collective-permute-start(bf16[272,128]{1,0:T(8,128)(2,1)S(1)} %get-tuple-element.276), channel_id=1, source_target_pairs={{0,12},{4,8},{8,4},{12,0},{1,13},{5,9},{9,5},{13,1},{2,14},{6,10},... | collective-permute-start | bytes 208904 | tf_op jit(solution)/shard_map/ppermute | solution.py:408
  113.2 5.3 %collective-permute-start.34 = (bf16[272,128]{1,0:T(8,128)(2,1)S(1)}, bf16[272,128]{1,0:T(8,128)(2,1)S(1)}, u32[]{:S(2)}, u32[]{:S(2)}) collective-permute-start(bf16[272,128]{1,0:T(8,128)(2,1)S(1)} %get-tuple-element.280), channel_id=1, source_target_pairs={{0,8},{4,12},{8,0},{12,4},{1,9},{5,13},{9,1},{13,5},{2,10},{6,14},... | collective-permute-start | bytes 208904 | tf_op jit(solution)/shard_map/ppermute | solution.py:408
  119.4 6.5 %collective-permute-start.37 = (bf16[32,1024]{1,0:T(8,128)(2,1)S(1)}, bf16[32,1024]{1,0:T(8,128)(2,1)S(1)}, u32[]{:S(2)}, u32[]{:S(2)}) collective-permute-start(bf16[32,1024]{1,0:T(8,128)(2,1)S(1)} %get-tuple-element.281.refs_0_.refs_4_), channel_id=1, source_target_pairs={{0,12},{4,8},{8,4},{12,0},{1,13},{5,9},{9,5},{13,1},{2,14},{6,10},... | collective-permute-start | bytes 196616 | tf_op jit(solution)/shard_map/ppermute | solution.py:408
  121.3 5.4 %collective-permute-start.36 = (bf16[32,1024]{1,0:T(8,128)(2,1)S(1)}, bf16[32,1024]{1,0:T(8,128)(2,1)S(1)}, u32[]{:S(2)}, u32[]{:S(2)}) collective-permute-start(bf16[32,1024]{1,0:T(8,128)(2,1)S(1)} %get-tuple-element.281.refs_0_.refs_4_), channel_id=1, source_target_pairs={{0,4},{4,0},{8,12},{12,8},{1,5},{5,1},{9,13},{13,9},{2,6},{6,2},{1... | collective-permute-start | bytes 196616 | tf_op jit(solution)/shard_map/ppermute | solution.py:408
  122.1 5.4 %collective-permute-start.35 = (bf16[32,1024]{1,0:T(8,128)(2,1)S(1)}, bf16[32,1024]{1,0:T(8,128)(2,1)S(1)}, u32[]{:S(2)}, u32[]{:S(2)}) collective-permute-start(bf16[32,1024]{1,0:T(8,128)(2,1)S(1)} %get-tuple-element.281.refs_0_.refs_4_), channel_id=1, source_target_pairs={{0,8},{4,12},{8,0},{12,4},{1,9},{5,13},{9,1},{13,5},{2,10},{6,14},... | collective-permute-start | bytes 196616 | tf_op jit(solution)/shard_map/ppermute | solution.py:408
  135.9 5.5 %collective-permute-start.40 = (f32[32,128]{1,0:T(8,128)S(1)}, f32[32,128]{1,0:T(8,128)S(1)}, u32[]{:S(2)}, u32[]{:S(2)}) collective-permute-start(f32[32,128]{1,0:T(8,128)S(1)} %get-tuple-element.294.refs_0_.scalars), channel_id=1, source_target_pairs={{0,12},{4,8},{8,4},{12,0},{1,13},{5,9},{9,5},{13,1},{2,14},{6,10},... | collective-permute-start | bytes 49160 | tf_op jit(solution)/shard_map/ppermute | solution.py:408
  (20 other events, 78.2 us)

commit v5 on v4

--- a/solution.py
+++ b/solution.py
@@ -13,7 +13,7 @@
 LANES = 128
 EDGE = 2 * GRID
 SLOTS = 8
-TAIL = 16
+TAIL = 8
 BF16 = jnp.bfloat16
 F32 = jnp.float32
 
@@ -26,6 +26,10 @@
 
 
 def send_order(count):
+    return [count - 1] + list(range(1, count - 1))
+
+
+def gather_order(count):
     return [count - 1] + list(range(1, count - 1))
 
 
@@ -164,10 +168,13 @@
     twice = None if first_sweep else refs.pop(0)
     image_in = refs.pop(0) if offset else None
     sets, width = shard.shape
-    pixels = green.shape[0]
+    pixels = green.shape[1] if n_shards > 1 else green.shape[0]
     at = own_columns(offset, width) if n_shards > 1 else slice(None)
     value = shard[...]
-    image = lax.dot_general(value, green[:, at], (((1,), (1,)), ((), ())), preferred_element_type=F32)
+    if n_shards > 1:
+        image = jnp.dot(value, green[...], preferred_element_type=F32)
+    else:
+        image = lax.dot_general(value, green[...], (((1,), (1,)), ((), ())), preferred_element_type=F32)
     if image_in is not None:
         image += image_in[...]
     rows = width // GRID
@@ -231,12 +238,13 @@
     below[...] = down
 
 
-def image_kernel(step, n_pix, first_sweep, has_block, *refs):
+def image_kernel(step, n_pix, first_sweep, has_block, keep_rounded, *refs):
     refs = list(refs)
     mine, got, above_in, below_in = (refs.pop(0) for _ in range(4))
     old_scalars, old_image = (None, None) if first_sweep else (refs.pop(0), refs.pop(0))
     green, lost = (refs.pop(0), refs.pop(0)) if has_block else (None, None)
-    scalars, image, rounded, above, below = (refs.pop(0) for _ in range(5))
+    scalars, image, above, below = (refs.pop(0) for _ in range(4))
+    rounded = refs.pop(0) if keep_rounded else None
     sets, pixels = image.shape
     value, sums, _, _, up, down = merge(
         mine, got, above_in[...], below_in[...], pixels, step, True, lax.axis_index("par")
@@ -252,7 +260,8 @@
         smooth_sq = smooth_sq + beta * (2.0 * sums[:, CROSS : CROSS + 1] + beta * old_smooth)
         value = value + beta * old_image[...]
     image[...] = value
-    rounded[...] = value.astype(BF16)
+    if keep_rounded:
+        rounded[...] = value.astype(BF16)
     image_sq = jnp.zeros((sets, LANES), F32)
     for at in range(0, pixels, LANES):
         part = value[:, at : at + LANES]
@@ -263,20 +272,21 @@
         {GRAD_SQ: grad_sq, SMOOTH_SQ: smooth_sq, IMAGE_SQ: image_sq, BETA: beta, GUESS: guess}, sets
     )
     if has_block:
-        send_block(send_order(n_pix)[0], value.astype(BF16), green, lost, guess, image_sq, *refs)
-
-
-def send_block(offset, image, green, lost, guess, image_sq, block, missed):
-    part = jnp.dot(image, green[:, own_columns(offset, missed.shape[1])], preferred_element_type=F32)
+        send_block(send_order(n_pix)[0], value.astype(BF16), green, lost.shape[1], lost, guess, image_sq, *refs)
+
+
+def send_block(offset, image, green, width, lost, guess, image_sq, block, missed=None):
+    part = jnp.dot(image, green[:, own_columns(offset, width)], preferred_element_type=F32)
     aimed = part if lost is None else part - guess * lost[...]
     sent = aimed.astype(BF16)
     store_block(block, sent, image_sq)
-    missed[...] = part - sent.astype(F32)
-
-
-def block_kernel(offset, rounded, scalars, green, lost, block, missed):
+    if missed is not None:
+        missed[...] = part - sent.astype(F32)
+
+
+def block_kernel(offset, rounded, scalars, green, lost, *refs):
     guess, image_sq = scalars[:, GUESS : GUESS + 1], scalars[:, IMAGE_SQ : IMAGE_SQ + 1]
-    send_block(offset, rounded[...], green, lost, guess, image_sq, block, missed)
+    send_block(offset, rounded[...], green, lost.shape[1], lost, guess, image_sq, *refs)
 
 
 def own_kernel(first_sweep, n_par, direct, has_product, *refs):
@@ -338,15 +348,18 @@
     for i, offset in enumerate(order):
         copies[i].wait()
         if offset:
-            send_block(offset, image, green, None, None, None, refs[i], refs[n_pix - 1 + i])
+            send_block(offset, image, green, width, None, None, None, refs[i], refs[n_pix - 1 + i])
         else:
             own[...] = jnp.dot(image, green[:, own_columns(0, width)], preferred_element_type=F32)
 
 
-def receive_start_kernel(own, *refs):
-    got, (grad, rounded) = refs[:-2], refs[-2:]
+def turn_kernel(offset, green, turned):
+    turned[...] = green[:, own_columns(offset, turned.shape[0])].T
+
+
+def receive_start_kernel(count, own, *refs):
+    got, (grad, rounded) = refs[: count - 1], refs[-2:]
     sets, width = own.shape
-    count = len(got) + 1
     value = tree_sum(by_offset(count, own[...], [load_block(ref, sets, width) for ref in got]))
     grad[...] = value
     rounded[...] = value.astype(BF16)
@@ -358,13 +371,15 @@
     return scalars[:, GRAD_SQ : GRAD_SQ + 1] / (image_sq + scalars[:, SMOOTH_SQ : SMOOTH_SQ + 1])
 
 
-def receive_kernel(own, scalars, old_grad, *refs):
-    got, (grad, rounded, length) = refs[:-3], refs[-3:]
+def receive_kernel(keep_grad, own, scalars, old_grad, *refs):
+    refs, grad = (refs[:-1], refs[-1]) if keep_grad else (refs, None)
+    got, (rounded, length) = refs[:-2], refs[-2:]
     sets, width = own.shape
     step_len = step_length(scalars, [load_scalar(ref, sets, width) for ref in got])
     change = tree_sum(by_offset(len(got) + 1, own[...], [load_block(ref, sets, width) for ref in got]))
     value = old_grad[...] - step_len * change
-    grad[...] = value
+    if keep_grad:
+        grad[...] = value
     rounded[...] = value.astype(BF16)
     length[...] = jnp.broadcast_to(step_len, length.shape)
 
@@ -405,7 +420,7 @@
 
 
 def exchange(blocks, axis, count):
-    return {k: lax.ppermute(blocks[k], axis, xor_pairs(count, k)) for k in send_order(count)}
+    return {k: lax.ppermute(block, axis, xor_pairs(count, k)) for k, block in blocks.items()}
 
 
 def by_offset(count, own, got):
@@ -431,6 +446,7 @@
     ring = ((sets, cells + 2 * EDGE), F32)
 
     order = send_order(n_pix) if direct else []
+    turn = gather_order(n_pix) if direct else []
     lost, got = {}, {}
     if direct:
         green, own, *rest = call(
@@ -443,18 +459,26 @@
             space=pltpu.HBM,
         )
         lost = dict(zip(order, rest[count:]))
+        turned_shape = ((width, pixels), BF16)
+        turned = {k: call(functools.partial(turn_kernel, k), [green], [turned_shape])[0] for k in [0] + turn}
         got = exchange(dict(zip(order, rest)), "pix", n_pix)
-    else:
+        ready = turned.values()
+    else:
+        turned, ready = {0: green}, []
         partial = jnp.dot(observed, green, preferred_element_type=F32)
         own = lax.psum_scatter(partial, "pix", scatter_dimension=1, tiled=True)
-    grad, rounded_grad = call(receive_start_kernel, [own, *got.values()], [shard, rounded_shard])
+    grad, rounded_grad = call(
+        functools.partial(receive_start_kernel, len(got) + 1),
+        [own, *got.values(), *ready],
+        [shard, rounded_shard],
+    )
     solution = jnp.zeros((sets, cells), F32)
     residual = observed.astype(F32)
     scalars = image = direction = twice = None
     for sweep in range(ITERS):
         first, final = sweep == 0, sweep + 1 == ITERS
         if direct:
-            shards = {0: rounded_grad, **exchange(dict.fromkeys(order, rounded_grad), "pix", n_pix)}
+            shards = {0: rounded_grad, **exchange(dict.fromkeys(turn, rounded_grad), "pix", n_pix)}
         else:
             shards = {0: lax.all_gather(rounded_grad, "pix", axis=1, tiled=True)}
         beside_them = [] if first else [twice]
@@ -463,15 +487,15 @@
             return ((sets, pixels + LANES + edge_columns(step, n_par)), F32 if step == 1 else BF16)
 
         partial, parts = [], {}
-        closing = ([0] + order)[-1]
-        for k in ([0] + order)[:-1]:
+        closing = ([0] + turn)[-1]
+        for k in ([0] + turn)[:-1]:
             kernel = functools.partial(shard_kernel, k, len(shards), first, False, n_par)
-            out, parts[k] = call(kernel, [shards[k], green, *beside_them, *partial], [line, scalar], flops=part_flops)
+            out, parts[k] = call(kernel, [shards[k], turned[k], *beside_them, *partial], [line, scalar], flops=part_flops)
             partial = [out]
         others = sorted(parts)
         whole, message = call(
             functools.partial(shard_kernel, closing, len(shards), first, True, n_par),
-            [shards[closing], green, *beside_them, *partial]
+            [shards[closing], turned[closing], *beside_them, *partial]
             + [shards[o] for o in others]
             + [parts[o] for o in others],
             [((sets, cells), BF16), message_of(1)],
@@ -491,13 +515,17 @@
         if above is None:
             above = below = jnp.zeros(edge[0], F32)
         has_block = direct and not final
+        again = sweep + 2 < ITERS
         blocks, missed = {}, {}
-        scalars, image, rounded, above, below, *rest = call(
-            functools.partial(image_kernel, step, n_pix, first, has_block),
+        sent = [block, shard] if again else [block]
+        scalars, image, above, below, *rest = call(
+            functools.partial(image_kernel, step, n_pix, first, has_block, not final),
             [message, got, above, below]
             + ([] if first else [scalars, image])
             + ([green, lost[order[0]]] if has_block else []),
-            [scalar, line, ((sets, pixels), BF16), edge, edge] + ([block, shard] if has_block else []),
+            [scalar, line, edge, edge]
+            + ([] if final else [((sets, pixels), BF16)])
+            + (sent if has_block else []),
             flops=part_flops if has_block else 0,
         )
         olds = [] if first else [direction]
@@ -513,13 +541,14 @@
                 got = {}
                 scalars = scalars.at[:, IMAGE_SQ].set(lax.psum(scalars[:, IMAGE_SQ], "pix"))
             return tuple(call(finish_kernel, [scalars, *got.values(), direction, image, solution, residual], [wide, line]))
+        rounded, *rest = rest
         if direct:
-            blocks[order[0]], missed[order[0]] = rest
+            blocks[order[0]], missed[order[0]] = rest[0], rest[1:]
             for k in order[1:]:
-                blocks[k], missed[k] = call(
+                blocks[k], *missed[k] = call(
                     functools.partial(block_kernel, k),
                     [rounded, scalars, green, lost[k]],
-                    [block, shard],
+                    sent,
                     flops=part_flops,
                 )
         direction, twice, own = call(
@@ -536,13 +565,17 @@
             own = lax.psum_scatter(own, "pix", scatter_dimension=1, tiled=True)
             own = own + lax.dynamic_slice_in_dim(twice, here * width, width, axis=1)
             scalars = scalars.at[:, IMAGE_SQ].set(lax.psum(scalars[:, IMAGE_SQ], "pix"))
-        grad, rounded_grad, length = call(
-            receive_kernel, [own, scalars, grad, *got.values()], [shard, rounded_shard, scalar]
+        rounded_grad, length, *rest = call(
+            functools.partial(receive_kernel, again),
+            [own, scalars, grad, *got.values()],
+            [rounded_shard, scalar] + ([shard] if again else []),
         )
+        (grad,) = rest or (None,)
         solution, residual, *rest = call(
-            functools.partial(update_kernel, count),
-            [length, direction, image, solution, residual, *lost.values(), *missed.values()],
-            [wide, line] + [shard] * count,
+            functools.partial(update_kernel, count if again else 0),
+            [length, direction, image, solution, residual]
+            + ([*lost.values(), *(one for (one,) in missed.values())] if again else []),
+            [wide, line] + ([shard] * count if again else []),
         )
         lost = dict(zip(order, rest))
 

time: 144 us -> 142 us (0.986)
  Pallas kernels: 37.2 us -> 32.2 us
  waiting for transfers between devices: 47.9 us -> 49.6 us
    pallas_call x54 -> x58, Pallas kernels: 37.2 us -> 32.2 us  [call(): pl.pallas_call(kernel, in_specs=[pl.BlockSpec(memory_space=space)] * len(...]
    ppermute x33, waiting for transfers between devices: 24.6 us -> 26.2 us  [exchange(): lax.ppermute(block, axis, xor_pairs(count, k))]
  transfers between devices with their start and end apart: 43 -> 43, of which waited for: 32 -> 37; matrix products, arithmetic and copies ran while one was open for 0% -> 0% of each run, Pallas kernels for 14% -> 13%
where the time goes in v5:
time: 142 us
  starting transfers between devices  58.6 us (41%)
  waiting for transfers between devices  49.6 us (35%)
  Pallas kernels  32.2 us (23%)
    ppermute x33, starting transfers between devices, exchange(): lax.ppermute(block, axis, xor_pairs(count, k))  50.7 us
    pallas_call x58, Pallas kernels, call(): pl.pallas_call(kernel, in_specs=[pl.BlockSpec(memory_space=space)] * len(...  32.2 us
    ppermute x33, waiting for transfers between devices, exchange(): lax.ppermute(block, axis, xor_pairs(count, k))  26.2 us
    ppermute x10, waiting for transfers between devices, on_device(): got = lax.ppermute(message, 'par', xor_pairs(n_par, step))  23.4 us
    ppermute x10, starting transfers between devices, on_device(): got = lax.ppermute(message, 'par', xor_pairs(n_par, step))  7.86 us
  transfers between devices with their start and end apart: 43, of which 37 were waited for; matrix products, arithmetic and copies ran while one was open for 0% of the time, Pallas kernels for 13%

profile of v5, /device:TPU:0, one launch (start us, length us, event | category | flops | bytes accessed | tf_op | source)
XLA Modules:
  0.0 141.5 jit_solution(13102689777014168697)
XLA Ops:
  0.6 4.4 %start_kernel.1 = (bf16[1152,4096]{1,0:T(8,128)(2,1)S(1)}, f32[32,1024]{1,0:T(8,128)S(1)}, bf16[256,128]{1,0:T(8,128)(2,1)S(1)}, bf16[256,128]{1,0:T(8,128)(2,1)...) custom-call(bf16[32,1152]{1,0:T(8,128)(2,1)} %observed_at.1, ...), custom_call_target="tpu_custom_call" | custom-call | flops 301989888 | bytes 19668992 | tf_op jit(solution)/shard_map/start_kernel/pallas_call | solution.py:410
  5.0 5.1 %collective-permute-start = (bf16[256,128]{1,0:T(8,128)(2,1)S(1)}, bf16[256,128]{1,0:T(8,128)(2,1)S(1)}, u32[]{:S(2)}, u32[]{:S(2)}) collective-permute-start(bf16[256,128]{1,0:T(8,128)(2,1)S(1)} %get-tuple-element.151), channel_id=1, source_target_pairs={{0,12},{4,8},{8,4},{12,0},{1,13},{5,9},{9,5},{13,1},{2,14},{6,10},... | collective-permute-start | bytes 196616 | tf_op jit(solution)/shard_map/ppermute | solution.py:423
  15.8 2.9 %collective-permute-start.5 = (bf16[32,1024]{1,0:T(8,128)(2,1)S(1)}, bf16[32,1024]{1,0:T(8,128)(2,1)S(1)}, u32[]{:S(2)}, u32[]{:S(2)}) collective-permute-start(bf16[32,1024]{1,0:T(8,128)(2,1)S(1)} %get-tuple-element.155.refs_0_.refs_3_), channel_id=1, source_target_pairs={{0,12},{4,8},{8,4},{12,0},{1,13},{5,9},{9,5},{13,1},{2,14},{6,10},... | collective-permute-start | bytes 196616 | tf_op jit(solution)/shard_map/ppermute | solution.py:423
  27.8 3.3 %collective-permute-done.7.refs_1_ = bf16[32,1536]{1,0:T(8,128)(2,1)S(1)} collective-permute-done((bf16[32,1536]{1,0:T(8,128)(2,1)S(1)}, bf16[32,1536]{1,0:T(8,128)(2,1)S(1)}, u32[]{:S(2)}, u32[]{:S(2)}) %collective-permute-start.7) | collective-permute-done | bytes 98336 | tf_op jit(solution)/shard_map/ppermute | solution.py:506
  31.7 2.7 %collective-permute-start.8 = (bf16[264,128]{1,0:T(8,128)(2,1)S(1)}, bf16[264,128]{1,0:T(8,128)(2,1)S(1)}, u32[]{:S(2)}, u32[]{:S(2)}) collective-permute-start(bf16[264,128]{1,0:T(8,128)(2,1)S(1)} %get-tuple-element.174), channel_id=1, source_target_pairs={{0,12},{4,8},{8,4},{12,0},{1,13},{5,9},{9,5},{13,1},{2,14},{6,10},... | collective-permute-start | bytes 202760 | tf_op jit(solution)/shard_map/ppermute | solution.py:423
  35.6 1.8 %collective-permute-start.10 = (bf16[264,128]{1,0:T(8,128)(2,1)S(1)}, bf16[264,128]{1,0:T(8,128)(2,1)S(1)}, u32[]{:S(2)}, u32[]{:S(2)}) collective-permute-start(bf16[264,128]{1,0:T(8,128)(2,1)S(1)} %get-tuple-element.178), channel_id=1, source_target_pairs={{0,8},{4,12},{8,0},{12,4},{1,9},{5,13},{9,1},{13,5},{2,10},{6,14},... | collective-permute-start | bytes 202760 | tf_op jit(solution)/shard_map/ppermute | solution.py:423
  41.2 2.9 %collective-permute-start.13 = (bf16[32,1024]{1,0:T(8,128)(2,1)S(1)}, bf16[32,1024]{1,0:T(8,128)(2,1)S(1)}, u32[]{:S(2)}, u32[]{:S(2)}) collective-permute-start(bf16[32,1024]{1,0:T(8,128)(2,1)S(1)} %get-tuple-element.179.refs_0_.refs_4_), channel_id=1, source_target_pairs={{0,12},{4,8},{8,4},{12,0},{1,13},{5,9},{9,5},{13,1},{2,14},{6,10},... | collective-permute-start | bytes 196616 | tf_op jit(solution)/shard_map/ppermute | solution.py:423
  46.2 1.9 %collective-permute-done.13.refs_0_.refs_6_ = bf16[32,1024]{1,0:T(8,128)(2,1)S(1)} collective-permute-done((bf16[32,1024]{1,0:T(8,128)(2,1)S(1)}, bf16[32,1024]{1,0:T(8,128)(2,1)S(1)}, u32[]{:S(2)}, u32[]{:S(2)}) %collective-permute-start.13) | collective-permute-done | bytes 65568 | tf_op jit(solution)/shard_map/ppermute | solution.py:423
  53.4 3.1 %collective-permute-done.15.refs_1_ = bf16[32,1536]{1,0:T(8,128)(2,1)S(1)} collective-permute-done((bf16[32,1536]{1,0:T(8,128)(2,1)S(1)}, bf16[32,1536]{1,0:T(8,128)(2,1)S(1)}, u32[]{:S(2)}, u32[]{:S(2)}) %collective-permute-start.15) | collective-permute-done | bytes 98336 | tf_op jit(solution)/shard_map/ppermute | solution.py:506
  57.2 2.7 %collective-permute-start.16 = (bf16[264,128]{1,0:T(8,128)(2,1)S(1)}, bf16[264,128]{1,0:T(8,128)(2,1)S(1)}, u32[]{:S(2)}, u32[]{:S(2)}) collective-permute-start(bf16[264,128]{1,0:T(8,128)(2,1)S(1)} %get-tuple-element.205), channel_id=1, source_target_pairs={{0,12},{4,8},{8,4},{12,0},{1,13},{5,9},{9,5},{13,1},{2,14},{6,10},... | collective-permute-start | bytes 202760 | tf_op jit(solution)/shard_map/ppermute | solution.py:423
  61.1 1.8 %collective-permute-start.18 = (bf16[264,128]{1,0:T(8,128)(2,1)S(1)}, bf16[264,128]{1,0:T(8,128)(2,1)S(1)}, u32[]{:S(2)}, u32[]{:S(2)}) collective-permute-start(bf16[264,128]{1,0:T(8,128)(2,1)S(1)} %get-tuple-element.209), channel_id=1, source_target_pairs={{0,8},{4,12},{8,0},{12,4},{1,9},{5,13},{9,1},{13,5},{2,10},{6,14},... | collective-permute-start | bytes 202760 | tf_op jit(solution)/shard_map/ppermute | solution.py:423
  66.8 2.9 %collective-permute-start.21 = (bf16[32,1024]{1,0:T(8,128)(2,1)S(1)}, bf16[32,1024]{1,0:T(8,128)(2,1)S(1)}, u32[]{:S(2)}, u32[]{:S(2)}) collective-permute-start(bf16[32,1024]{1,0:T(8,128)(2,1)S(1)} %get-tuple-element.210.refs_0_.refs_4_), channel_id=1, source_target_pairs={{0,12},{4,8},{8,4},{12,0},{1,13},{5,9},{9,5},{13,1},{2,14},{6,10},... | collective-permute-start | bytes 196616 | tf_op jit(solution)/shard_map/ppermute | solution.py:423
  78.9 3.1 %collective-permute-done.23.refs_1_ = bf16[32,1536]{1,0:T(8,128)(2,1)S(1)} collective-permute-done((bf16[32,1536]{1,0:T(8,128)(2,1)S(1)}, bf16[32,1536]{1,0:T(8,128)(2,1)S(1)}, u32[]{:S(2)}, u32[]{:S(2)}) %collective-permute-start.23) | collective-permute-done | bytes 98336 | tf_op jit(solution)/shard_map/ppermute | solution.py:506
  82.8 2.7 %collective-permute-start.24 = (bf16[264,128]{1,0:T(8,128)(2,1)S(1)}, bf16[264,128]{1,0:T(8,128)(2,1)S(1)}, u32[]{:S(2)}, u32[]{:S(2)}) collective-permute-start(bf16[264,128]{1,0:T(8,128)(2,1)S(1)} %get-tuple-element.238), channel_id=1, source_target_pairs={{0,12},{4,8},{8,4},{12,0},{1,13},{5,9},{9,5},{13,1},{2,14},{6,10},... | collective-permute-start | bytes 202760 | tf_op jit(solution)/shard_map/ppermute | solution.py:423
  86.6 1.8 %collective-permute-start.26 = (bf16[264,128]{1,0:T(8,128)(2,1)S(1)}, bf16[264,128]{1,0:T(8,128)(2,1)S(1)}, u32[]{:S(2)}, u32[]{:S(2)}) collective-permute-start(bf16[264,128]{1,0:T(8,128)(2,1)S(1)} %get-tuple-element.242), channel_id=1, source_target_pairs={{0,8},{4,12},{8,0},{12,4},{1,9},{5,13},{9,1},{13,5},{2,10},{6,14},... | collective-permute-start | bytes 202760 | tf_op jit(solution)/shard_map/ppermute | solution.py:423
  92.3 2.9 %collective-permute-start.29 = (bf16[32,1024]{1,0:T(8,128)(2,1)S(1)}, bf16[32,1024]{1,0:T(8,128)(2,1)S(1)}, u32[]{:S(2)}, u32[]{:S(2)}) collective-permute-start(bf16[32,1024]{1,0:T(8,128)(2,1)S(1)} %get-tuple-element.243.refs_0_.refs_4_), channel_id=1, source_target_pairs={{0,12},{4,8},{8,4},{12,0},{1,13},{5,9},{9,5},{13,1},{2,14},{6,10},... | collective-permute-start | bytes 196616 | tf_op jit(solution)/shard_map/ppermute | solution.py:423
  97.3 1.9 %collective-permute-done.29.refs_0_.refs_6_ = bf16[32,1024]{1,0:T(8,128)(2,1)S(1)} collective-permute-done((bf16[32,1024]{1,0:T(8,128)(2,1)S(1)}, bf16[32,1024]{1,0:T(8,128)(2,1)S(1)}, u32[]{:S(2)}, u32[]{:S(2)}) %collective-permute-start.29) | collective-permute-done | bytes 65568 | tf_op jit(solution)/shard_map/ppermute | solution.py:423
  104.5 3.1 %collective-permute-done.31.refs_1_ = bf16[32,1536]{1,0:T(8,128)(2,1)S(1)} collective-permute-done((bf16[32,1536]{1,0:T(8,128)(2,1)S(1)}, bf16[32,1536]{1,0:T(8,128)(2,1)S(1)}, u32[]{:S(2)}, u32[]{:S(2)}) %collective-permute-start.31) | collective-permute-done | bytes 98336 | tf_op jit(solution)/shard_map/ppermute | solution.py:506
  108.3 2.7 %collective-permute-start.32 = (bf16[264,128]{1,0:T(8,128)(2,1)S(1)}, bf16[264,128]{1,0:T(8,128)(2,1)S(1)}, u32[]{:S(2)}, u32[]{:S(2)}) collective-permute-start(bf16[264,128]{1,0:T(8,128)(2,1)S(1)} %get-tuple-element.271), channel_id=1, source_target_pairs={{0,12},{4,8},{8,4},{12,0},{1,13},{5,9},{9,5},{13,1},{2,14},{6,10},... | collective-permute-start | bytes 202760 | tf_op jit(solution)/shard_map/ppermute | solution.py:423
  112.1 1.8 %collective-permute-start.34 = (bf16[264,128]{1,0:T(8,128)(2,1)S(1)}, bf16[264,128]{1,0:T(8,128)(2,1)S(1)}, u32[]{:S(2)}, u32[]{:S(2)}) collective-permute-start(bf16[264,128]{1,0:T(8,128)(2,1)S(1)} %block_kernel.15), channel_id=1, source_target_pairs={{0,8},{4,12},{8,0},{12,4},{1,9},{5,13},{9,1},{13,5},{2,10},{6,14},... | collective-permute-start | bytes 202760 | tf_op jit(solution)/shard_map/ppermute | solution.py:423
  117.8 2.8 %collective-permute-start.37 = (bf16[32,1024]{1,0:T(8,128)(2,1)S(1)}, bf16[32,1024]{1,0:T(8,128)(2,1)S(1)}, u32[]{:S(2)}, u32[]{:S(2)}) collective-permute-start(bf16[32,1024]{1,0:T(8,128)(2,1)S(1)} %get-tuple-element.274.refs_0_.refs_4_), channel_id=1, source_target_pairs={{0,12},{4,8},{8,4},{12,0},{1,13},{5,9},{9,5},{13,1},{2,14},{6,10},... | collective-permute-start | bytes 196616 | tf_op jit(solution)/shard_map/ppermute | solution.py:423
  122.8 1.9 %collective-permute-done.37.refs_0_.refs_6_ = bf16[32,1024]{1,0:T(8,128)(2,1)S(1)} collective-permute-done((bf16[32,1024]{1,0:T(8,128)(2,1)S(1)}, bf16[32,1024]{1,0:T(8,128)(2,1)S(1)}, u32[]{:S(2)}, u32[]{:S(2)}) %collective-permute-start.37) | collective-permute-done | bytes 65568 | tf_op jit(solution)/shard_map/ppermute | solution.py:423
  130.2 3.3 %collective-permute-done.39.refs_1_ = bf16[32,1536]{1,0:T(8,128)(2,1)S(1)} collective-permute-done((bf16[32,1536]{1,0:T(8,128)(2,1)S(1)}, bf16[32,1536]{1,0:T(8,128)(2,1)S(1)}, u32[]{:S(2)}, u32[]{:S(2)}) %collective-permute-start.39) | collective-permute-done | bytes 98336 | tf_op jit(solution)/shard_map/ppermute | solution.py:506
  135.8 2.7 %collective-permute-start.42 = (f32[32,128]{1,0:T(8,128)S(1)}, f32[32,128]{1,0:T(8,128)S(1)}, u32[]{:S(2)}, u32[]{:S(2)}) collective-permute-start(f32[32,128]{1,0:T(8,128)S(1)} %get-tuple-element.287.refs_0_.scalars), channel_id=1, source_target_pairs={{0,8},{4,12},{8,0},{12,4},{1,9},{5,13},{9,1},{13,5},{2,10},{6,14},... | collective-permute-start | bytes 49160 | tf_op jit(solution)/shard_map/ppermute | solution.py:423
  (124 shorter events, 74.3 us)
Async XLA Ops:
  5.0 8.5 %collective-permute-start = (bf16[256,128]{1,0:T(8,128)(2,1)S(1)}, bf16[256,128]{1,0:T(8,128)(2,1)S(1)}, u32[]{:S(2)}, u32[]{:S(2)}) collective-permute-start(bf16[256,128]{1,0:T(8,128)(2,1)S(1)} %get-tuple-element.151), channel_id=1, source_target_pairs={{0,12},{4,8},{8,4},{12,0},{1,13},{5,9},{9,5},{13,1},{2,14},{6,10},... | collective-permute-start | bytes 196616 | tf_op jit(solution)/shard_map/ppermute | solution.py:423
  10.2 5.6 %collective-permute-start.2 = (bf16[256,128]{1,0:T(8,128)(2,1)S(1)}, bf16[256,128]{1,0:T(8,128)(2,1)S(1)}, u32[]{:S(2)}, u32[]{:S(2)}) collective-permute-start(bf16[256,128]{1,0:T(8,128)(2,1)S(1)} %get-tuple-element.153), channel_id=1, source_target_pairs={{0,8},{4,12},{8,0},{12,4},{1,9},{5,13},{9,1},{13,5},{2,10},{6,14},... | collective-permute-start | bytes 196616 | tf_op jit(solution)/shard_map/ppermute | solution.py:423
  15.8 6.5 %collective-permute-start.5 = (bf16[32,1024]{1,0:T(8,128)(2,1)S(1)}, bf16[32,1024]{1,0:T(8,128)(2,1)S(1)}, u32[]{:S(2)}, u32[]{:S(2)}) collective-permute-start(bf16[32,1024]{1,0:T(8,128)(2,1)S(1)} %get-tuple-element.155.refs_0_.refs_3_), channel_id=1, source_target_pairs={{0,12},{4,8},{8,4},{12,0},{1,13},{5,9},{9,5},{13,1},{2,14},{6,10},... | collective-permute-start | bytes 196616 | tf_op jit(solution)/shard_map/ppermute | solution.py:423
  18.8 5.3 %collective-permute-start.3 = (bf16[32,1024]{1,0:T(8,128)(2,1)S(1)}, bf16[32,1024]{1,0:T(8,128)(2,1)S(1)}, u32[]{:S(2)}, u32[]{:S(2)}) collective-permute-start(bf16[32,1024]{1,0:T(8,128)(2,1)S(1)} %get-tuple-element.155.refs_0_.refs_3_), channel_id=1, source_target_pairs={{0,8},{4,12},{8,0},{12,4},{1,9},{5,13},{9,1},{13,5},{2,10},{6,14},... | collective-permute-start | bytes 196616 | tf_op jit(solution)/shard_map/ppermute | solution.py:423
  26.3 4.8 %collective-permute-start.7 = (bf16[32,1536]{1,0:T(8,128)(2,1)S(1)}, bf16[32,1536]{1,0:T(8,128)(2,1)S(1)}, u32[]{:S(2)}, u32[]{:S(2)}) collective-permute-start(bf16[32,1536]{1,0:T(8,128)(2,1)S(1)} %get-tuple-element.163.refs_0_), channel_id=1, source_target_pairs={{0,2},{1,3},{2,0},{3,1},{4,6},{5,7},{6,4},{7,5},{8,10},{9,11},{10,... | collective-permute-start | bytes 294920 | tf_op jit(solution)/shard_map/ppermute | solution.py:506
  31.7 6.5 %collective-permute-start.8 = (bf16[264,128]{1,0:T(8,128)(2,1)S(1)}, bf16[264,128]{1,0:T(8,128)(2,1)S(1)}, u32[]{:S(2)}, u32[]{:S(2)}) collective-permute-start(bf16[264,128]{1,0:T(8,128)(2,1)S(1)} %get-tuple-element.174), channel_id=1, source_target_pairs={{0,12},{4,8},{8,4},{12,0},{1,13},{5,9},{9,5},{13,1},{2,14},{6,10},... | collective-permute-start | bytes 202760 | tf_op jit(solution)/shard_map/ppermute | solution.py:423
  35.6 5.4 %collective-permute-start.10 = (bf16[264,128]{1,0:T(8,128)(2,1)S(1)}, bf16[264,128]{1,0:T(8,128)(2,1)S(1)}, u32[]{:S(2)}, u32[]{:S(2)}) collective-permute-start(bf16[264,128]{1,0:T(8,128)(2,1)S(1)} %get-tuple-element.178), channel_id=1, source_target_pairs={{0,8},{4,12},{8,0},{12,4},{1,9},{5,13},{9,1},{13,5},{2,10},{6,14},... | collective-permute-start | bytes 202760 | tf_op jit(solution)/shard_map/ppermute | solution.py:423
  41.2 6.9 %collective-permute-start.13 = (bf16[32,1024]{1,0:T(8,128)(2,1)S(1)}, bf16[32,1024]{1,0:T(8,128)(2,1)S(1)}, u32[]{:S(2)}, u32[]{:S(2)}) collective-permute-start(bf16[32,1024]{1,0:T(8,128)(2,1)S(1)} %get-tuple-element.179.refs_0_.refs_4_), channel_id=1, source_target_pairs={{0,12},{4,8},{8,4},{12,0},{1,13},{5,9},{9,5},{13,1},{2,14},{6,10},... | collective-permute-start | bytes 196616 | tf_op jit(solution)/shard_map/ppermute | solution.py:423
  44.1 5.2 %collective-permute-start.11 = (bf16[32,1024]{1,0:T(8,128)(2,1)S(1)}, bf16[32,1024]{1,0:T(8,128)(2,1)S(1)}, u32[]{:S(2)}, u32[]{:S(2)}) collective-permute-start(bf16[32,1024]{1,0:T(8,128)(2,1)S(1)} %get-tuple-element.179.refs_0_.refs_4_), channel_id=1, source_target_pairs={{0,8},{4,12},{8,0},{12,4},{1,9},{5,13},{9,1},{13,5},{2,10},{6,14},... | collective-permute-start | bytes 196616 | tf_op jit(solution)/shard_map/ppermute | solution.py:423
  57.2 6.6 %collective-permute-start.16 = (bf16[264,128]{1,0:T(8,128)(2,1)S(1)}, bf16[264,128]{1,0:T(8,128)(2,1)S(1)}, u32[]{:S(2)}, u32[]{:S(2)}) collective-permute-start(bf16[264,128]{1,0:T(8,128)(2,1)S(1)} %get-tuple-element.205), channel_id=1, source_target_pairs={{0,12},{4,8},{8,4},{12,0},{1,13},{5,9},{9,5},{13,1},{2,14},{6,10},... | collective-permute-start | bytes 202760 | tf_op jit(solution)/shard_map/ppermute | solution.py:423
  61.1 5.4 %collective-permute-start.18 = (bf16[264,128]{1,0:T(8,128)(2,1)S(1)}, bf16[264,128]{1,0:T(8,128)(2,1)S(1)}, u32[]{:S(2)}, u32[]{:S(2)}) collective-permute-start(bf16[264,128]{1,0:T(8,128)(2,1)S(1)} %get-tuple-element.209), channel_id=1, source_target_pairs={{0,8},{4,12},{8,0},{12,4},{1,9},{5,13},{9,1},{13,5},{2,10},{6,14},... | collective-permute-start | bytes 202760 | tf_op jit(solution)/shard_map/ppermute | solution.py:423
  66.8 6.8 %collective-permute-start.21 = (bf16[32,1024]{1,0:T(8,128)(2,1)S(1)}, bf16[32,1024]{1,0:T(8,128)(2,1)S(1)}, u32[]{:S(2)}, u32[]{:S(2)}) collective-permute-start(bf16[32,1024]{1,0:T(8,128)(2,1)S(1)} %get-tuple-element.210.refs_0_.refs_4_), channel_id=1, source_target_pairs={{0,12},{4,8},{8,4},{12,0},{1,13},{5,9},{9,5},{13,1},{2,14},{6,10},... | collective-permute-start | bytes 196616 | tf_op jit(solution)/shard_map/ppermute | solution.py:423
  69.7 5.2 %collective-permute-start.19 = (bf16[32,1024]{1,0:T(8,128)(2,1)S(1)}, bf16[32,1024]{1,0:T(8,128)(2,1)S(1)}, u32[]{:S(2)}, u32[]{:S(2)}) collective-permute-start(bf16[32,1024]{1,0:T(8,128)(2,1)S(1)} %get-tuple-element.210.refs_0_.refs_4_), channel_id=1, source_target_pairs={{0,8},{4,12},{8,0},{12,4},{1,9},{5,13},{9,1},{13,5},{2,10},{6,14},... | collective-permute-start | bytes 196616 | tf_op jit(solution)/shard_map/ppermute | solution.py:423
  77.2 4.8 %collective-permute-start.23 = (bf16[32,1536]{1,0:T(8,128)(2,1)S(1)}, bf16[32,1536]{1,0:T(8,128)(2,1)S(1)}, u32[]{:S(2)}, u32[]{:S(2)}) collective-permute-start(bf16[32,1536]{1,0:T(8,128)(2,1)S(1)} %get-tuple-element.219.refs_0_), channel_id=1, source_target_pairs={{0,2},{1,3},{2,0},{3,1},{4,6},{5,7},{6,4},{7,5},{8,10},{9,11},{10,... | collective-permute-start | bytes 294920 | tf_op jit(solution)/shard_map/ppermute | solution.py:506
  82.8 6.6 %collective-permute-start.24 = (bf16[264,128]{1,0:T(8,128)(2,1)S(1)}, bf16[264,128]{1,0:T(8,128)(2,1)S(1)}, u32[]{:S(2)}, u32[]{:S(2)}) collective-permute-start(bf16[264,128]{1,0:T(8,128)(2,1)S(1)} %get-tuple-element.238), channel_id=1, source_target_pairs={{0,12},{4,8},{8,4},{12,0},{1,13},{5,9},{9,5},{13,1},{2,14},{6,10},... | collective-permute-start | bytes 202760 | tf_op jit(solution)/shard_map/ppermute | solution.py:423
  86.6 5.4 %collective-permute-start.26 = (bf16[264,128]{1,0:T(8,128)(2,1)S(1)}, bf16[264,128]{1,0:T(8,128)(2,1)S(1)}, u32[]{:S(2)}, u32[]{:S(2)}) collective-permute-start(bf16[264,128]{1,0:T(8,128)(2,1)S(1)} %get-tuple-element.242), channel_id=1, source_target_pairs={{0,8},{4,12},{8,0},{12,4},{1,9},{5,13},{9,1},{13,5},{2,10},{6,14},... | collective-permute-start | bytes 202760 | tf_op jit(solution)/shard_map/ppermute | solution.py:423
  92.3 6.8 %collective-permute-start.29 = (bf16[32,1024]{1,0:T(8,128)(2,1)S(1)}, bf16[32,1024]{1,0:T(8,128)(2,1)S(1)}, u32[]{:S(2)}, u32[]{:S(2)}) collective-permute-start(bf16[32,1024]{1,0:T(8,128)(2,1)S(1)} %get-tuple-element.243.refs_0_.refs_4_), channel_id=1, source_target_pairs={{0,12},{4,8},{8,4},{12,0},{1,13},{5,9},{9,5},{13,1},{2,14},{6,10},... | collective-permute-start | bytes 196616 | tf_op jit(solution)/shard_map/ppermute | solution.py:423
  95.2 5.2 %collective-permute-start.27 = (bf16[32,1024]{1,0:T(8,128)(2,1)S(1)}, bf16[32,1024]{1,0:T(8,128)(2,1)S(1)}, u32[]{:S(2)}, u32[]{:S(2)}) collective-permute-start(bf16[32,1024]{1,0:T(8,128)(2,1)S(1)} %get-tuple-element.243.refs_0_.refs_4_), channel_id=1, source_target_pairs={{0,8},{4,12},{8,0},{12,4},{1,9},{5,13},{9,1},{13,5},{2,10},{6,14},... | collective-permute-start | bytes 196616 | tf_op jit(solution)/shard_map/ppermute | solution.py:423
  108.3 6.6 %collective-permute-start.32 = (bf16[264,128]{1,0:T(8,128)(2,1)S(1)}, bf16[264,128]{1,0:T(8,128)(2,1)S(1)}, u32[]{:S(2)}, u32[]{:S(2)}) collective-permute-start(bf16[264,128]{1,0:T(8,128)(2,1)S(1)} %get-tuple-element.271), channel_id=1, source_target_pairs={{0,12},{4,8},{8,4},{12,0},{1,13},{5,9},{9,5},{13,1},{2,14},{6,10},... | collective-permute-start | bytes 202760 | tf_op jit(solution)/shard_map/ppermute | solution.py:423
  112.1 5.5 %collective-permute-start.34 = (bf16[264,128]{1,0:T(8,128)(2,1)S(1)}, bf16[264,128]{1,0:T(8,128)(2,1)S(1)}, u32[]{:S(2)}, u32[]{:S(2)}) collective-permute-start(bf16[264,128]{1,0:T(8,128)(2,1)S(1)} %block_kernel.15), channel_id=1, source_target_pairs={{0,8},{4,12},{8,0},{12,4},{1,9},{5,13},{9,1},{13,5},{2,10},{6,14},... | collective-permute-start | bytes 202760 | tf_op jit(solution)/shard_map/ppermute | solution.py:423
  117.8 6.8 %collective-permute-start.37 = (bf16[32,1024]{1,0:T(8,128)(2,1)S(1)}, bf16[32,1024]{1,0:T(8,128)(2,1)S(1)}, u32[]{:S(2)}, u32[]{:S(2)}) collective-permute-start(bf16[32,1024]{1,0:T(8,128)(2,1)S(1)} %get-tuple-element.274.refs_0_.refs_4_), channel_id=1, source_target_pairs={{0,12},{4,8},{8,4},{12,0},{1,13},{5,9},{9,5},{13,1},{2,14},{6,10},... | collective-permute-start | bytes 196616 | tf_op jit(solution)/shard_map/ppermute | solution.py:423
  120.6 5.2 %collective-permute-start.36 = (bf16[32,1024]{1,0:T(8,128)(2,1)S(1)}, bf16[32,1024]{1,0:T(8,128)(2,1)S(1)}, u32[]{:S(2)}, u32[]{:S(2)}) collective-permute-start(bf16[32,1024]{1,0:T(8,128)(2,1)S(1)} %get-tuple-element.274.refs_0_.refs_4_), channel_id=1, source_target_pairs={{0,4},{4,0},{8,12},{12,8},{1,5},{5,1},{9,13},{13,9},{2,6},{6,2},{1... | collective-permute-start | bytes 196616 | tf_op jit(solution)/shard_map/ppermute | solution.py:423
  120.6 5.8 %collective-permute-start.35 = (bf16[32,1024]{1,0:T(8,128)(2,1)S(1)}, bf16[32,1024]{1,0:T(8,128)(2,1)S(1)}, u32[]{:S(2)}, u32[]{:S(2)}) collective-permute-start(bf16[32,1024]{1,0:T(8,128)(2,1)S(1)} %get-tuple-element.274.refs_0_.refs_4_), channel_id=1, source_target_pairs={{0,8},{4,12},{8,0},{12,4},{1,9},{5,13},{9,1},{13,5},{2,10},{6,14},... | collective-permute-start | bytes 196616 | tf_op jit(solution)/shard_map/ppermute | solution.py:423
  134.1 5.6 %collective-permute-start.40 = (f32[32,128]{1,0:T(8,128)S(1)}, f32[32,128]{1,0:T(8,128)S(1)}, u32[]{:S(2)}, u32[]{:S(2)}) collective-permute-start(f32[32,128]{1,0:T(8,128)S(1)} %get-tuple-element.287.refs_0_.scalars), channel_id=1, source_target_pairs={{0,12},{4,8},{8,4},{12,0},{1,13},{5,9},{9,5},{13,1},{2,14},{6,10},... | collective-permute-start | bytes 49160 | tf_op jit(solution)/shard_map/ppermute | solution.py:423
  (20 other events, 77.0 us)

commit v6 on v5

--- a/solution.py
+++ b/solution.py
@@ -26,11 +26,13 @@
 
 
 def send_order(count):
-    return [count - 1] + list(range(1, count - 1))
+    half = count // 2
+    return [half] + [k for k in range(count - 1, 0, -1) if k != half]
 
 
 def gather_order(count):
-    return [count - 1] + list(range(1, count - 1))
+    half = count // 2
+    return [half] + [k for k in range(1, count) if k != half]
 
 
 def tree_sum(parts):
@@ -93,14 +95,18 @@
     return jnp.sum(0.0625 * (up0 * up0 + low1 * low1) - 0.5 * cross, axis=1, keepdims=True)
 
 
-def merge(mine_ref, got_ref, above, below, pixels, step, final, tile):
+def merge_sums(mine_ref, got_ref, pixels):
+    scalar_at = pl.ds(pixels, LANES)
+    if mine_ref.dtype == F32:
+        scalars = mine_ref[:, scalar_at] + got_ref[:, scalar_at]
+    else:
+        scalars = unpack(mine_ref[:, scalar_at]) + unpack(got_ref[:, scalar_at])
+    return mine_ref[:, :pixels].astype(F32) + got_ref[:, :pixels].astype(F32), scalars
+
+
+def merge_edges(mine_ref, got_ref, above, below, pixels, step, final, tile):
     upper_side = (tile // step) % 2 == 1
     inside = tile % step
-    scalar_at = pl.ds(pixels, LANES)
-    if mine_ref.dtype == F32:
-        mine, got = mine_ref[:, scalar_at], got_ref[:, scalar_at]
-    else:
-        mine, got = unpack(mine_ref[:, scalar_at]), unpack(got_ref[:, scalar_at])
     edges, got_edges = mine_ref[:, pixels + LANES :].astype(F32), got_ref[:, pixels + LANES :].astype(F32)
     if final:
         first = last = None
@@ -111,12 +117,9 @@
         last = jnp.where(upper_side, edges[:, EDGE:], got_edges[:, EDGE:])
         lower_last = jnp.where(upper_side, got_edges[:, EDGE:], edges[:, EDGE:])
         upper_first = jnp.where(upper_side, edges[:, :EDGE], got_edges[:, :EDGE])
-    sets = mine.shape[0]
-    scalars = mine + got + lanes_of({SMOOTH_SQ: seam(lower_last, upper_first)}, sets)
     above = jnp.where(upper_side & (inside == 0), lower_last, above)
     below = jnp.where(jnp.logical_not(upper_side) & (inside == step - 1), upper_first, below)
-    value = mine_ref[:, :pixels].astype(F32) + got_ref[:, :pixels].astype(F32)
-    return value, scalars, first, last, above, below
+    return seam(lower_last, upper_first), first, last, above, below
 
 
 def edge_columns(step, n_par):
@@ -230,7 +233,9 @@
         old_above, old_below = above_in[...], below_in[...]
     pixels = mine.shape[1] - LANES - 2 * EDGE
     tile = lax.axis_index("par")
-    value, scalars, first, last, up, down = merge(mine, got, old_above, old_below, pixels, step, False, tile)
+    value, scalars = merge_sums(mine, got, pixels)
+    added, first, last, up, down = merge_edges(mine, got, old_above, old_below, pixels, step, False, tile)
+    scalars += lanes_of({SMOOTH_SQ: added}, value.shape[0])
     message[:, :pixels] = value.astype(BF16)
     message[:, pixels : pixels + LANES] = pack(scalars)
     store_edges(message, pixels + LANES, first, last, 2 * step, n_par, tile)
@@ -238,19 +243,16 @@
     below[...] = down
 
 
-def image_kernel(step, n_pix, first_sweep, has_block, keep_rounded, *refs):
+def image_kernel(n_pix, first_sweep, early, keep_rounded, *refs):
     refs = list(refs)
-    mine, got, above_in, below_in = (refs.pop(0) for _ in range(4))
+    mine, got = refs.pop(0), refs.pop(0)
     old_scalars, old_image = (None, None) if first_sweep else (refs.pop(0), refs.pop(0))
-    green, lost = (refs.pop(0), refs.pop(0)) if has_block else (None, None)
-    scalars, image, above, below = (refs.pop(0) for _ in range(4))
+    green = refs.pop(0) if early else None
+    lost = [refs.pop(0) for _ in early]
+    scalars, image = refs.pop(0), refs.pop(0)
     rounded = refs.pop(0) if keep_rounded else None
     sets, pixels = image.shape
-    value, sums, _, _, up, down = merge(
-        mine, got, above_in[...], below_in[...], pixels, step, True, lax.axis_index("par")
-    )
-    above[...] = up
-    below[...] = down
+    value, sums = merge_sums(mine, got, pixels)
     grad_sq = sums[:, GRAD_SQ : GRAD_SQ + 1]
     smooth_sq = sums[:, SMOOTH_SQ : SMOOTH_SQ + 1]
     beta = jnp.zeros((sets, 1), F32)
@@ -267,12 +269,14 @@
         part = value[:, at : at + LANES]
         image_sq += part * part
     image_sq = jnp.sum(image_sq, axis=1, keepdims=True)
-    guess = (n_pix * image_sq + smooth_sq) / grad_sq
+    guess = (n_pix * image_sq + jnp.maximum(smooth_sq, 0.0)) / grad_sq
     scalars[...] = lanes_of(
         {GRAD_SQ: grad_sq, SMOOTH_SQ: smooth_sq, IMAGE_SQ: image_sq, BETA: beta, GUESS: guess}, sets
     )
-    if has_block:
-        send_block(send_order(n_pix)[0], value.astype(BF16), green, lost.shape[1], lost, guess, image_sq, *refs)
+    each = len(refs) // len(early) if early else 0
+    for i, offset in enumerate(early):
+        outs = refs[i * each : (i + 1) * each]
+        send_block(offset, value.astype(BF16), green, lost[i].shape[1], lost[i], guess, image_sq, *outs)
 
 
 def send_block(offset, image, green, width, lost, guess, image_sq, block, missed=None):
@@ -289,27 +293,30 @@
     send_block(offset, rounded[...], green, lost.shape[1], lost, guess, image_sq, *refs)
 
 
-def own_kernel(first_sweep, n_par, direct, has_product, *refs):
+def own_kernel(step, first_sweep, n_par, direct, has_product, *refs):
     refs = list(refs)
-    scalars, above, below, whole = (refs.pop(0) for _ in range(4))
+    sums, mine, got, above_in, below_in, whole = (refs.pop(0) for _ in range(6))
     old_direction = None if first_sweep else refs.pop(0)
     rounded, green = (refs.pop(0), refs.pop(0)) if has_product else (None, None)
-    direction = refs.pop(0)
-    cells = whole.shape[1]
+    scalars, direction = refs.pop(0), refs.pop(0)
+    sets, cells = whole.shape
     rows = cells // GRID
+    tile = lax.axis_index("par")
+    pixels = mine.shape[1] - LANES - EDGE
+    added, _, _, above, below = merge_edges(mine, got, above_in[...], below_in[...], pixels, step, True, tile)
+    scalars[...] = sums[...] + lanes_of({SMOOTH_SQ: added}, sets)
     if first_sweep:
-        direction[:, :EDGE] = above[...]
+        direction[:, :EDGE] = above
         direction[:, EDGE : EDGE + cells] = whole[...].astype(F32)
-        direction[:, EDGE + cells :] = below[...]
-    else:
-        beta = scalars[:, BETA : BETA + 1]
-        direction[:, :EDGE] = above[...] + beta * old_direction[:, :EDGE]
+        direction[:, EDGE + cells :] = below
+    else:
+        beta = sums[:, BETA : BETA + 1]
+        direction[:, :EDGE] = above + beta * old_direction[:, :EDGE]
         direction[:, EDGE : EDGE + cells] = whole[...].astype(F32) + beta * old_direction[:, EDGE : EDGE + cells]
-        direction[:, EDGE + cells :] = below[...] + beta * old_direction[:, EDGE + cells :]
+        direction[:, EDGE + cells :] = below + beta * old_direction[:, EDGE + cells :]
     if not has_product:
         return
     twice, own, once = refs
-    tile = lax.axis_index("par")
 
     def from_ref(ref, r):
         return ref[:, r * GRID : (r + 1) * GRID]
@@ -514,47 +521,45 @@
             step *= 2
         if above is None:
             above = below = jnp.zeros(edge[0], F32)
-        has_block = direct and not final
         again = sweep + 2 < ITERS
+        early = [] if final else order[:1]
         blocks, missed = {}, {}
         sent = [block, shard] if again else [block]
-        scalars, image, above, below, *rest = call(
-            functools.partial(image_kernel, step, n_pix, first, has_block, not final),
-            [message, got, above, below]
+        sums, image, *rest = call(
+            functools.partial(image_kernel, n_pix, first, early, not final),
+            [message, got]
             + ([] if first else [scalars, image])
-            + ([green, lost[order[0]]] if has_block else []),
-            [scalar, line, edge, edge]
-            + ([] if final else [((sets, pixels), BF16)])
-            + (sent if has_block else []),
-            flops=part_flops if has_block else 0,
+            + ([green] if early else [])
+            + [lost[k] for k in early],
+            [scalar, line] + ([] if final else [((sets, pixels), BF16)]) + sent * len(early),
+            flops=part_flops * len(early),
         )
-        olds = [] if first else [direction]
+        ends = [sums, message, got, above, below, whole, *([] if first else [direction])]
         if final:
-            (direction,) = call(
-                functools.partial(own_kernel, first, n_par, direct, False),
-                [scalars, above, below, whole, *olds],
-                [ring],
+            scalars, direction = call(
+                functools.partial(own_kernel, step, first, n_par, direct, False), ends, [scalar, ring]
             )
             if direct:
-                got = exchange(dict.fromkeys(order, scalars), "pix", n_pix)
+                got = exchange(dict.fromkeys(order, sums), "pix", n_pix)
             else:
                 got = {}
                 scalars = scalars.at[:, IMAGE_SQ].set(lax.psum(scalars[:, IMAGE_SQ], "pix"))
             return tuple(call(finish_kernel, [scalars, *got.values(), direction, image, solution, residual], [wide, line]))
         rounded, *rest = rest
         if direct:
-            blocks[order[0]], missed[order[0]] = rest[0], rest[1:]
-            for k in order[1:]:
+            for i, k in enumerate(early):
+                blocks[k], *missed[k] = rest[i * len(sent) : (i + 1) * len(sent)]
+            for k in order[len(early) :]:
                 blocks[k], *missed[k] = call(
                     functools.partial(block_kernel, k),
-                    [rounded, scalars, green, lost[k]],
+                    [rounded, sums, green, lost[k]],
                     sent,
                     flops=part_flops,
                 )
-        direction, twice, own = call(
-            functools.partial(own_kernel, first, n_par, direct, True),
-            [scalars, above, below, whole, *olds, rounded, green],
-            [ring, wide, shard if direct else wide],
+        scalars, direction, twice, own = call(
+            functools.partial(own_kernel, step, first, n_par, direct, True),
+            [*ends, rounded, green],
+            [scalar, ring, wide, shard if direct else wide],
             [pltpu.VMEM((sets, cells + EDGE), F32)],
             part_flops if direct else flops,
         )

time: 142 us -> 139 us (0.979)
  starting transfers between devices: 58.6 us -> 54.1 us
  waiting for transfers between devices: 49.6 us -> 51.9 us
    ppermute x33, starting transfers between devices: 50.7 us -> 46.2 us  [exchange(): lax.ppermute(block, axis, xor_pairs(count, k))]
    ppermute x33, waiting for transfers between devices: 26.2 us -> 28.5 us  [exchange(): lax.ppermute(block, axis, xor_pairs(count, k))]
  transfers between devices with their start and end apart: 43 -> 43, of which waited for: 37 -> 38; matrix products, arithmetic and copies ran while one was open for 0% -> 0% of each run, Pallas kernels for 13% -> 14%
where the time goes in v6:
time: 139 us
  starting transfers between devices  54.1 us (39%)
  waiting for transfers between devices  51.9 us (37%)
  Pallas kernels  32.2 us (23%)
    ppermute x33, starting transfers between devices, exchange(): lax.ppermute(block, axis, xor_pairs(count, k))  46.2 us
    pallas_call x58, Pallas kernels, call(): pl.pallas_call(kernel, in_specs=[pl.BlockSpec(memory_space=space)] * len(...  32.2 us
    ppermute x33, waiting for transfers between devices, exchange(): lax.ppermute(block, axis, xor_pairs(count, k))  28.5 us
    ppermute x10, waiting for transfers between devices, on_device(): got = lax.ppermute(message, 'par', xor_pairs(n_par, step))  23.4 us
    ppermute x10, starting transfers between devices, on_device(): got = lax.ppermute(message, 'par', xor_pairs(n_par, step))  7.87 us
  transfers between devices with their start and end apart: 43, of which 38 were waited for; matrix products, arithmetic and copies ran while one was open for 0% of the time, Pallas kernels for 14%

profile of v6, /device:TPU:0, one launch (start us, length us, event | category | flops | bytes accessed | tf_op | source)
XLA Modules:
  0.0 139.3 jit_solution(17907936325520195756)
XLA Ops:
  0.6 4.4 %start_kernel.1 = (bf16[1152,4096]{1,0:T(8,128)(2,1)S(1)}, f32[32,1024]{1,0:T(8,128)S(1)}, bf16[256,128]{1,0:T(8,128)(2,1)S(1)}, bf16[256,128]{1,0:T(8,128)(2,1)...) custom-call(bf16[32,1152]{1,0:T(8,128)(2,1)} %observed_at.1, ...), custom_call_target="tpu_custom_call" | custom-call | flops 301989888 | bytes 19668992 | tf_op jit(solution)/shard_map/start_kernel/pallas_call | solution.py:417
  5.0 4.1 %collective-permute-start = (bf16[256,128]{1,0:T(8,128)(2,1)S(1)}, bf16[256,128]{1,0:T(8,128)(2,1)S(1)}, u32[]{:S(2)}, u32[]{:S(2)}) collective-permute-start(bf16[256,128]{1,0:T(8,128)(2,1)S(1)} %get-tuple-element.147), channel_id=1, source_target_pairs={{0,8},{4,12},{8,0},{12,4},{1,9},{5,13},{9,1},{13,5},{2,10},{6,14},... | collective-permute-start | bytes 196616 | tf_op jit(solution)/shard_map/ppermute | solution.py:430
  13.4 1.9 %collective-permute-done.1.refs_1_ = bf16[256,128]{1,0:T(8,128)(2,1)S(1)} collective-permute-done((bf16[256,128]{1,0:T(8,128)(2,1)S(1)}, bf16[256,128]{1,0:T(8,128)(2,1)S(1)}, u32[]{:S(2)}, u32[]{:S(2)}) %collective-permute-start.1) | collective-permute-done | bytes 65568 | tf_op jit(solution)/shard_map/ppermute | solution.py:430
  15.5 2.7 %collective-permute-start.5 = (bf16[32,1024]{1,0:T(8,128)(2,1)S(1)}, bf16[32,1024]{1,0:T(8,128)(2,1)S(1)}, u32[]{:S(2)}, u32[]{:S(2)}) collective-permute-start(bf16[32,1024]{1,0:T(8,128)(2,1)S(1)} %get-tuple-element.151.refs_0_.refs_3_), channel_id=1, source_target_pairs={{0,8},{4,12},{8,0},{12,4},{1,9},{5,13},{9,1},{13,5},{2,10},{6,14},... | collective-permute-start | bytes 196616 | tf_op jit(solution)/shard_map/ppermute | solution.py:430
  29.0 3.3 %collective-permute-done.7.refs_1_.refs_2_ = bf16[32,1536]{1,0:T(8,128)(2,1)S(1)} collective-permute-done((bf16[32,1536]{1,0:T(8,128)(2,1)S(1)}, bf16[32,1536]{1,0:T(8,128)(2,1)S(1)}, u32[]{:S(2)}, u32[]{:S(2)}) %collective-permute-start.7) | collective-permute-done | bytes 98336 | tf_op jit(solution)/shard_map/ppermute | solution.py:513
  35.9 1.7 %collective-permute-start.10 = (bf16[264,128]{1,0:T(8,128)(2,1)S(1)}, bf16[264,128]{1,0:T(8,128)(2,1)S(1)}, u32[]{:S(2)}, u32[]{:S(2)}) collective-permute-start(bf16[264,128]{1,0:T(8,128)(2,1)S(1)} %get-tuple-element.173), channel_id=1, source_target_pairs={{0,4},{4,0},{8,12},{12,8},{1,5},{5,1},{9,13},{13,9},{2,6},{6,2},{1... | collective-permute-start | bytes 202760 | tf_op jit(solution)/shard_map/ppermute | solution.py:430
  39.4 1.6 %collective-permute-done.9.refs_1_ = bf16[264,128]{1,0:T(8,128)(2,1)S(1)} collective-permute-done((bf16[264,128]{1,0:T(8,128)(2,1)S(1)}, bf16[264,128]{1,0:T(8,128)(2,1)S(1)}, u32[]{:S(2)}, u32[]{:S(2)}) %collective-permute-start.9) | collective-permute-done | bytes 67616 | tf_op jit(solution)/shard_map/ppermute | solution.py:430
  42.8 1.6 %collective-permute-start.12 = (bf16[32,1024]{1,0:T(8,128)(2,1)S(1)}, bf16[32,1024]{1,0:T(8,128)(2,1)S(1)}, u32[]{:S(2)}, u32[]{:S(2)}) collective-permute-start(bf16[32,1024]{1,0:T(8,128)(2,1)S(1)} %get-tuple-element.174.refs_0_.refs_4_), channel_id=1, source_target_pairs={{0,4},{4,0},{8,12},{12,8},{1,5},{5,1},{9,13},{13,9},{2,6},{6,2},{1... | collective-permute-start | bytes 196616 | tf_op jit(solution)/shard_map/ppermute | solution.py:430
  46.4 1.7 %collective-permute-done.13.refs_0_.refs_6_ = bf16[32,1024]{1,0:T(8,128)(2,1)S(1)} collective-permute-done((bf16[32,1024]{1,0:T(8,128)(2,1)S(1)}, bf16[32,1024]{1,0:T(8,128)(2,1)S(1)}, u32[]{:S(2)}, u32[]{:S(2)}) %collective-permute-start.13) | collective-permute-done | bytes 65568 | tf_op jit(solution)/shard_map/ppermute | solution.py:430
  54.6 3.1 %collective-permute-done.15.refs_1_.refs_2_ = bf16[32,1536]{1,0:T(8,128)(2,1)S(1)} collective-permute-done((bf16[32,1536]{1,0:T(8,128)(2,1)S(1)}, bf16[32,1536]{1,0:T(8,128)(2,1)S(1)}, u32[]{:S(2)}, u32[]{:S(2)}) %collective-permute-start.15) | collective-permute-done | bytes 98336 | tf_op jit(solution)/shard_map/ppermute | solution.py:513
  61.1 1.9 %collective-permute-start.18 = (bf16[264,128]{1,0:T(8,128)(2,1)S(1)}, bf16[264,128]{1,0:T(8,128)(2,1)S(1)}, u32[]{:S(2)}, u32[]{:S(2)}) collective-permute-start(bf16[264,128]{1,0:T(8,128)(2,1)S(1)} %get-tuple-element.203), channel_id=1, source_target_pairs={{0,4},{4,0},{8,12},{12,8},{1,5},{5,1},{9,13},{13,9},{2,6},{6,2},{1... | collective-permute-start | bytes 202760 | tf_op jit(solution)/shard_map/ppermute | solution.py:430
  69.4 1.7 %collective-permute-start.19 = (bf16[32,1024]{1,0:T(8,128)(2,1)S(1)}, bf16[32,1024]{1,0:T(8,128)(2,1)S(1)}, u32[]{:S(2)}, u32[]{:S(2)}) collective-permute-start(bf16[32,1024]{1,0:T(8,128)(2,1)S(1)} %get-tuple-element.204.refs_0_.refs_4_), channel_id=1, source_target_pairs={{0,12},{4,8},{8,4},{12,0},{1,13},{5,9},{9,5},{13,1},{2,14},{6,10},... | collective-permute-start | bytes 196616 | tf_op jit(solution)/shard_map/ppermute | solution.py:430
  71.8 1.9 %collective-permute-done.21.refs_0_.refs_6_ = bf16[32,1024]{1,0:T(8,128)(2,1)S(1)} collective-permute-done((bf16[32,1024]{1,0:T(8,128)(2,1)S(1)}, bf16[32,1024]{1,0:T(8,128)(2,1)S(1)}, u32[]{:S(2)}, u32[]{:S(2)}) %collective-permute-start.21) | collective-permute-done | bytes 65568 | tf_op jit(solution)/shard_map/ppermute | solution.py:430
  79.5 3.1 %collective-permute-done.23.refs_1_.refs_2_ = bf16[32,1536]{1,0:T(8,128)(2,1)S(1)} collective-permute-done((bf16[32,1536]{1,0:T(8,128)(2,1)S(1)}, bf16[32,1536]{1,0:T(8,128)(2,1)S(1)}, u32[]{:S(2)}, u32[]{:S(2)}) %collective-permute-start.23) | collective-permute-done | bytes 98336 | tf_op jit(solution)/shard_map/ppermute | solution.py:513
  83.9 1.9 %collective-permute-start.25 = (bf16[264,128]{1,0:T(8,128)(2,1)S(1)}, bf16[264,128]{1,0:T(8,128)(2,1)S(1)}, u32[]{:S(2)}, u32[]{:S(2)}) collective-permute-start(bf16[264,128]{1,0:T(8,128)(2,1)S(1)} %get-tuple-element.233), channel_id=1, source_target_pairs={{0,12},{4,8},{8,4},{12,0},{1,13},{5,9},{9,5},{13,1},{2,14},{6,10},... | collective-permute-start | bytes 202760 | tf_op jit(solution)/shard_map/ppermute | solution.py:430
  86.3 1.7 %collective-permute-start.26 = (bf16[264,128]{1,0:T(8,128)(2,1)S(1)}, bf16[264,128]{1,0:T(8,128)(2,1)S(1)}, u32[]{:S(2)}, u32[]{:S(2)}) collective-permute-start(bf16[264,128]{1,0:T(8,128)(2,1)S(1)} %get-tuple-element.235), channel_id=1, source_target_pairs={{0,4},{4,0},{8,12},{12,8},{1,5},{5,1},{9,13},{13,9},{2,6},{6,2},{1... | collective-permute-start | bytes 202760 | tf_op jit(solution)/shard_map/ppermute | solution.py:430
  94.1 2.0 %collective-permute-start.27 = (bf16[32,1024]{1,0:T(8,128)(2,1)S(1)}, bf16[32,1024]{1,0:T(8,128)(2,1)S(1)}, u32[]{:S(2)}, u32[]{:S(2)}) collective-permute-start(bf16[32,1024]{1,0:T(8,128)(2,1)S(1)} %get-tuple-element.236.refs_0_.refs_4_), channel_id=1, source_target_pairs={{0,12},{4,8},{8,4},{12,0},{1,13},{5,9},{9,5},{13,1},{2,14},{6,10},... | collective-permute-start | bytes 196616 | tf_op jit(solution)/shard_map/ppermute | solution.py:430
  96.5 1.8 %collective-permute-done.29.refs_0_.refs_6_ = bf16[32,1024]{1,0:T(8,128)(2,1)S(1)} collective-permute-done((bf16[32,1024]{1,0:T(8,128)(2,1)S(1)}, bf16[32,1024]{1,0:T(8,128)(2,1)S(1)}, u32[]{:S(2)}, u32[]{:S(2)}) %collective-permute-start.29) | collective-permute-done | bytes 65568 | tf_op jit(solution)/shard_map/ppermute | solution.py:430
  104.2 3.1 %collective-permute-done.31.refs_1_.refs_2_ = bf16[32,1536]{1,0:T(8,128)(2,1)S(1)} collective-permute-done((bf16[32,1536]{1,0:T(8,128)(2,1)S(1)}, bf16[32,1536]{1,0:T(8,128)(2,1)S(1)}, u32[]{:S(2)}, u32[]{:S(2)}) %collective-permute-start.31) | collective-permute-done | bytes 98336 | tf_op jit(solution)/shard_map/ppermute | solution.py:513
  108.5 2.0 %collective-permute-start.33 = (bf16[264,128]{1,0:T(8,128)(2,1)S(1)}, bf16[264,128]{1,0:T(8,128)(2,1)S(1)}, u32[]{:S(2)}, u32[]{:S(2)}) collective-permute-start(bf16[264,128]{1,0:T(8,128)(2,1)S(1)} %block_kernel.14), channel_id=1, source_target_pairs={{0,12},{4,8},{8,4},{12,0},{1,13},{5,9},{9,5},{13,1},{2,14},{6,10},... | collective-permute-start | bytes 202760 | tf_op jit(solution)/shard_map/ppermute | solution.py:430
  118.8 1.9 %collective-permute-start.35 = (bf16[32,1024]{1,0:T(8,128)(2,1)S(1)}, bf16[32,1024]{1,0:T(8,128)(2,1)S(1)}, u32[]{:S(2)}, u32[]{:S(2)}) collective-permute-start(bf16[32,1024]{1,0:T(8,128)(2,1)S(1)} %get-tuple-element.266.refs_0_.refs_4_), channel_id=1, source_target_pairs={{0,12},{4,8},{8,4},{12,0},{1,13},{5,9},{9,5},{13,1},{2,14},{6,10},... | collective-permute-start | bytes 196616 | tf_op jit(solution)/shard_map/ppermute | solution.py:430
  121.2 1.6 %collective-permute-done.37.refs_0_.refs_6_ = bf16[32,1024]{1,0:T(8,128)(2,1)S(1)} collective-permute-done((bf16[32,1024]{1,0:T(8,128)(2,1)S(1)}, bf16[32,1024]{1,0:T(8,128)(2,1)S(1)}, u32[]{:S(2)}, u32[]{:S(2)}) %collective-permute-start.37) | collective-permute-done | bytes 65568 | tf_op jit(solution)/shard_map/ppermute | solution.py:430
  128.7 3.3 %collective-permute-done.39.refs_1_.refs_2_ = bf16[32,1536]{1,0:T(8,128)(2,1)S(1)} collective-permute-done((bf16[32,1536]{1,0:T(8,128)(2,1)S(1)}, bf16[32,1536]{1,0:T(8,128)(2,1)S(1)}, u32[]{:S(2)}, u32[]{:S(2)}) %collective-permute-start.39) | collective-permute-done | bytes 98336 | tf_op jit(solution)/shard_map/ppermute | solution.py:513
  132.4 2.0 %collective-permute-start.41 = (f32[32,128]{1,0:T(8,128)S(1)}, f32[32,128]{1,0:T(8,128)S(1)}, u32[]{:S(2)}, u32[]{:S(2)}) collective-permute-start(f32[32,128]{1,0:T(8,128)S(1)} %get-tuple-element.277.refs_0_), channel_id=1, source_target_pairs={{0,12},{4,8},{8,4},{12,0},{1,13},{5,9},{9,5},{13,1},{2,14},{6,10},... | collective-permute-start | bytes 49160 | tf_op jit(solution)/shard_map/ppermute | solution.py:430
  (124 shorter events, 82.2 us)
Async XLA Ops:
  5.0 8.4 %collective-permute-start = (bf16[256,128]{1,0:T(8,128)(2,1)S(1)}, bf16[256,128]{1,0:T(8,128)(2,1)S(1)}, u32[]{:S(2)}, u32[]{:S(2)}) collective-permute-start(bf16[256,128]{1,0:T(8,128)(2,1)S(1)} %get-tuple-element.147), channel_id=1, source_target_pairs={{0,8},{4,12},{8,0},{12,4},{1,9},{5,13},{9,1},{13,5},{2,10},{6,14},... | collective-permute-start | bytes 196616 | tf_op jit(solution)/shard_map/ppermute | solution.py:430
  9.2 6.2 %collective-permute-start.1 = (bf16[256,128]{1,0:T(8,128)(2,1)S(1)}, bf16[256,128]{1,0:T(8,128)(2,1)S(1)}, u32[]{:S(2)}, u32[]{:S(2)}) collective-permute-start(bf16[256,128]{1,0:T(8,128)(2,1)S(1)} %get-tuple-element.148), channel_id=1, source_target_pairs={{0,12},{4,8},{8,4},{12,0},{1,13},{5,9},{9,5},{13,1},{2,14},{6,10},... | collective-permute-start | bytes 196616 | tf_op jit(solution)/shard_map/ppermute | solution.py:430
  15.5 6.2 %collective-permute-start.5 = (bf16[32,1024]{1,0:T(8,128)(2,1)S(1)}, bf16[32,1024]{1,0:T(8,128)(2,1)S(1)}, u32[]{:S(2)}, u32[]{:S(2)}) collective-permute-start(bf16[32,1024]{1,0:T(8,128)(2,1)S(1)} %get-tuple-element.151.refs_0_.refs_3_), channel_id=1, source_target_pairs={{0,8},{4,12},{8,0},{12,4},{1,9},{5,13},{9,1},{13,5},{2,10},{6,14},... | collective-permute-start | bytes 196616 | tf_op jit(solution)/shard_map/ppermute | solution.py:430
  19.1 6.1 %collective-permute-start.3 = (bf16[32,1024]{1,0:T(8,128)(2,1)S(1)}, bf16[32,1024]{1,0:T(8,128)(2,1)S(1)}, u32[]{:S(2)}, u32[]{:S(2)}) collective-permute-start(bf16[32,1024]{1,0:T(8,128)(2,1)S(1)} %get-tuple-element.151.refs_0_.refs_3_), channel_id=1, source_target_pairs={{0,12},{4,8},{8,4},{12,0},{1,13},{5,9},{9,5},{13,1},{2,14},{6,10},... | collective-permute-start | bytes 196616 | tf_op jit(solution)/shard_map/ppermute | solution.py:430
  32.9 6.5 %collective-permute-start.8 = (bf16[264,128]{1,0:T(8,128)(2,1)S(1)}, bf16[264,128]{1,0:T(8,128)(2,1)S(1)}, u32[]{:S(2)}, u32[]{:S(2)}) collective-permute-start(bf16[264,128]{1,0:T(8,128)(2,1)S(1)} %get-tuple-element.169), channel_id=1, source_target_pairs={{0,8},{4,12},{8,0},{12,4},{1,9},{5,13},{9,1},{13,5},{2,10},{6,14},... | collective-permute-start | bytes 202760 | tf_op jit(solution)/shard_map/ppermute | solution.py:430
  34.7 6.2 %collective-permute-start.9 = (bf16[264,128]{1,0:T(8,128)(2,1)S(1)}, bf16[264,128]{1,0:T(8,128)(2,1)S(1)}, u32[]{:S(2)}, u32[]{:S(2)}) collective-permute-start(bf16[264,128]{1,0:T(8,128)(2,1)S(1)} %get-tuple-element.171), channel_id=1, source_target_pairs={{0,12},{4,8},{8,4},{12,0},{1,13},{5,9},{9,5},{13,1},{2,14},{6,10},... | collective-permute-start | bytes 202760 | tf_op jit(solution)/shard_map/ppermute | solution.py:430
  41.4 6.6 %collective-permute-start.13 = (bf16[32,1024]{1,0:T(8,128)(2,1)S(1)}, bf16[32,1024]{1,0:T(8,128)(2,1)S(1)}, u32[]{:S(2)}, u32[]{:S(2)}) collective-permute-start(bf16[32,1024]{1,0:T(8,128)(2,1)S(1)} %get-tuple-element.174.refs_0_.refs_4_), channel_id=1, source_target_pairs={{0,8},{4,12},{8,0},{12,4},{1,9},{5,13},{9,1},{13,5},{2,10},{6,14},... | collective-permute-start | bytes 196616 | tf_op jit(solution)/shard_map/ppermute | solution.py:430
  42.8 5.8 %collective-permute-start.12 = (bf16[32,1024]{1,0:T(8,128)(2,1)S(1)}, bf16[32,1024]{1,0:T(8,128)(2,1)S(1)}, u32[]{:S(2)}, u32[]{:S(2)}) collective-permute-start(bf16[32,1024]{1,0:T(8,128)(2,1)S(1)} %get-tuple-element.174.refs_0_.refs_4_), channel_id=1, source_target_pairs={{0,4},{4,0},{8,12},{12,8},{1,5},{5,1},{9,13},{13,9},{2,6},{6,2},{1... | collective-permute-start | bytes 196616 | tf_op jit(solution)/shard_map/ppermute | solution.py:430
  44.4 6.1 %collective-permute-start.11 = (bf16[32,1024]{1,0:T(8,128)(2,1)S(1)}, bf16[32,1024]{1,0:T(8,128)(2,1)S(1)}, u32[]{:S(2)}, u32[]{:S(2)}) collective-permute-start(bf16[32,1024]{1,0:T(8,128)(2,1)S(1)} %get-tuple-element.174.refs_0_.refs_4_), channel_id=1, source_target_pairs={{0,12},{4,8},{8,4},{12,0},{1,13},{5,9},{9,5},{13,1},{2,14},{6,10},... | collective-permute-start | bytes 196616 | tf_op jit(solution)/shard_map/ppermute | solution.py:430
  58.3 6.5 %collective-permute-start.16 = (bf16[264,128]{1,0:T(8,128)(2,1)S(1)}, bf16[264,128]{1,0:T(8,128)(2,1)S(1)}, u32[]{:S(2)}, u32[]{:S(2)}) collective-permute-start(bf16[264,128]{1,0:T(8,128)(2,1)S(1)} %get-tuple-element.199), channel_id=1, source_target_pairs={{0,8},{4,12},{8,0},{12,4},{1,9},{5,13},{9,1},{13,5},{2,10},{6,14},... | collective-permute-start | bytes 202760 | tf_op jit(solution)/shard_map/ppermute | solution.py:430
  59.7 6.3 %collective-permute-start.17 = (bf16[264,128]{1,0:T(8,128)(2,1)S(1)}, bf16[264,128]{1,0:T(8,128)(2,1)S(1)}, u32[]{:S(2)}, u32[]{:S(2)}) collective-permute-start(bf16[264,128]{1,0:T(8,128)(2,1)S(1)} %get-tuple-element.201), channel_id=1, source_target_pairs={{0,12},{4,8},{8,4},{12,0},{1,13},{5,9},{9,5},{13,1},{2,14},{6,10},... | collective-permute-start | bytes 202760 | tf_op jit(solution)/shard_map/ppermute | solution.py:430
  66.6 7.1 %collective-permute-start.21 = (bf16[32,1024]{1,0:T(8,128)(2,1)S(1)}, bf16[32,1024]{1,0:T(8,128)(2,1)S(1)}, u32[]{:S(2)}, u32[]{:S(2)}) collective-permute-start(bf16[32,1024]{1,0:T(8,128)(2,1)S(1)} %get-tuple-element.204.refs_0_.refs_4_), channel_id=1, source_target_pairs={{0,8},{4,12},{8,0},{12,4},{1,9},{5,13},{9,1},{13,5},{2,10},{6,14},... | collective-permute-start | bytes 196616 | tf_op jit(solution)/shard_map/ppermute | solution.py:430
  68.0 6.2 %collective-permute-start.20 = (bf16[32,1024]{1,0:T(8,128)(2,1)S(1)}, bf16[32,1024]{1,0:T(8,128)(2,1)S(1)}, u32[]{:S(2)}, u32[]{:S(2)}) collective-permute-start(bf16[32,1024]{1,0:T(8,128)(2,1)S(1)} %get-tuple-element.204.refs_0_.refs_4_), channel_id=1, source_target_pairs={{0,4},{4,0},{8,12},{12,8},{1,5},{5,1},{9,13},{13,9},{2,6},{6,2},{1... | collective-permute-start | bytes 196616 | tf_op jit(solution)/shard_map/ppermute | solution.py:430
  69.4 6.1 %collective-permute-start.19 = (bf16[32,1024]{1,0:T(8,128)(2,1)S(1)}, bf16[32,1024]{1,0:T(8,128)(2,1)S(1)}, u32[]{:S(2)}, u32[]{:S(2)}) collective-permute-start(bf16[32,1024]{1,0:T(8,128)(2,1)S(1)} %get-tuple-element.204.refs_0_.refs_4_), channel_id=1, source_target_pairs={{0,12},{4,8},{8,4},{12,0},{1,13},{5,9},{9,5},{13,1},{2,14},{6,10},... | collective-permute-start | bytes 196616 | tf_op jit(solution)/shard_map/ppermute | solution.py:430
  83.3 6.8 %collective-permute-start.24 = (bf16[264,128]{1,0:T(8,128)(2,1)S(1)}, bf16[264,128]{1,0:T(8,128)(2,1)S(1)}, u32[]{:S(2)}, u32[]{:S(2)}) collective-permute-start(bf16[264,128]{1,0:T(8,128)(2,1)S(1)} %get-tuple-element.231), channel_id=1, source_target_pairs={{0,8},{4,12},{8,0},{12,4},{1,9},{5,13},{9,1},{13,5},{2,10},{6,14},... | collective-permute-start | bytes 202760 | tf_op jit(solution)/shard_map/ppermute | solution.py:430
  83.9 6.6 %collective-permute-start.25 = (bf16[264,128]{1,0:T(8,128)(2,1)S(1)}, bf16[264,128]{1,0:T(8,128)(2,1)S(1)}, u32[]{:S(2)}, u32[]{:S(2)}) collective-permute-start(bf16[264,128]{1,0:T(8,128)(2,1)S(1)} %get-tuple-element.233), channel_id=1, source_target_pairs={{0,12},{4,8},{8,4},{12,0},{1,13},{5,9},{9,5},{13,1},{2,14},{6,10},... | collective-permute-start | bytes 202760 | tf_op jit(solution)/shard_map/ppermute | solution.py:430
  91.6 6.8 %collective-permute-start.29 = (bf16[32,1024]{1,0:T(8,128)(2,1)S(1)}, bf16[32,1024]{1,0:T(8,128)(2,1)S(1)}, u32[]{:S(2)}, u32[]{:S(2)}) collective-permute-start(bf16[32,1024]{1,0:T(8,128)(2,1)S(1)} %get-tuple-element.236.refs_0_.refs_4_), channel_id=1, source_target_pairs={{0,8},{4,12},{8,0},{12,4},{1,9},{5,13},{9,1},{13,5},{2,10},{6,14},... | collective-permute-start | bytes 196616 | tf_op jit(solution)/shard_map/ppermute | solution.py:430
  92.9 6.0 %collective-permute-start.28 = (bf16[32,1024]{1,0:T(8,128)(2,1)S(1)}, bf16[32,1024]{1,0:T(8,128)(2,1)S(1)}, u32[]{:S(2)}, u32[]{:S(2)}) collective-permute-start(bf16[32,1024]{1,0:T(8,128)(2,1)S(1)} %get-tuple-element.236.refs_0_.refs_4_), channel_id=1, source_target_pairs={{0,4},{4,0},{8,12},{12,8},{1,5},{5,1},{9,13},{13,9},{2,6},{6,2},{1... | collective-permute-start | bytes 196616 | tf_op jit(solution)/shard_map/ppermute | solution.py:430
  94.1 6.1 %collective-permute-start.27 = (bf16[32,1024]{1,0:T(8,128)(2,1)S(1)}, bf16[32,1024]{1,0:T(8,128)(2,1)S(1)}, u32[]{:S(2)}, u32[]{:S(2)}) collective-permute-start(bf16[32,1024]{1,0:T(8,128)(2,1)S(1)} %get-tuple-element.236.refs_0_.refs_4_), channel_id=1, source_target_pairs={{0,12},{4,8},{8,4},{12,0},{1,13},{5,9},{9,5},{13,1},{2,14},{6,10},... | collective-permute-start | bytes 196616 | tf_op jit(solution)/shard_map/ppermute | solution.py:430
  107.9 7.0 %collective-permute-start.32 = (bf16[264,128]{1,0:T(8,128)(2,1)S(1)}, bf16[264,128]{1,0:T(8,128)(2,1)S(1)}, u32[]{:S(2)}, u32[]{:S(2)}) collective-permute-start(bf16[264,128]{1,0:T(8,128)(2,1)S(1)} %get-tuple-element.263), channel_id=1, source_target_pairs={{0,8},{4,12},{8,0},{12,4},{1,9},{5,13},{9,1},{13,5},{2,10},{6,14},... | collective-permute-start | bytes 202760 | tf_op jit(solution)/shard_map/ppermute | solution.py:430
  108.5 6.9 %collective-permute-start.33 = (bf16[264,128]{1,0:T(8,128)(2,1)S(1)}, bf16[264,128]{1,0:T(8,128)(2,1)S(1)}, u32[]{:S(2)}, u32[]{:S(2)}) collective-permute-start(bf16[264,128]{1,0:T(8,128)(2,1)S(1)} %block_kernel.14), channel_id=1, source_target_pairs={{0,12},{4,8},{8,4},{12,0},{1,13},{5,9},{9,5},{13,1},{2,14},{6,10},... | collective-permute-start | bytes 202760 | tf_op jit(solution)/shard_map/ppermute | solution.py:430
  116.2 6.6 %collective-permute-start.37 = (bf16[32,1024]{1,0:T(8,128)(2,1)S(1)}, bf16[32,1024]{1,0:T(8,128)(2,1)S(1)}, u32[]{:S(2)}, u32[]{:S(2)}) collective-permute-start(bf16[32,1024]{1,0:T(8,128)(2,1)S(1)} %get-tuple-element.266.refs_0_.refs_4_), channel_id=1, source_target_pairs={{0,8},{4,12},{8,0},{12,4},{1,9},{5,13},{9,1},{13,5},{2,10},{6,14},... | collective-permute-start | bytes 196616 | tf_op jit(solution)/shard_map/ppermute | solution.py:430
  118.8 6.1 %collective-permute-start.35 = (bf16[32,1024]{1,0:T(8,128)(2,1)S(1)}, bf16[32,1024]{1,0:T(8,128)(2,1)S(1)}, u32[]{:S(2)}, u32[]{:S(2)}) collective-permute-start(bf16[32,1024]{1,0:T(8,128)(2,1)S(1)} %get-tuple-element.266.refs_0_.refs_4_), channel_id=1, source_target_pairs={{0,12},{4,8},{8,4},{12,0},{1,13},{5,9},{9,5},{13,1},{2,14},{6,10},... | collective-permute-start | bytes 196616 | tf_op jit(solution)/shard_map/ppermute | solution.py:430
  132.4 5.6 %collective-permute-start.41 = (f32[32,128]{1,0:T(8,128)S(1)}, f32[32,128]{1,0:T(8,128)S(1)}, u32[]{:S(2)}, u32[]{:S(2)}) collective-permute-start(f32[32,128]{1,0:T(8,128)S(1)} %get-tuple-element.277.refs_0_), channel_id=1, source_target_pairs={{0,12},{4,8},{8,4},{12,0},{1,13},{5,9},{9,5},{13,1},{2,14},{6,10},... | collective-permute-start | bytes 49160 | tf_op jit(solution)/shard_map/ppermute | solution.py:430
  (20 other events, 81.4 us)

commit v7 on v6

--- a/solution.py
+++ b/solution.py
@@ -97,10 +97,7 @@
 
 def merge_sums(mine_ref, got_ref, pixels):
     scalar_at = pl.ds(pixels, LANES)
-    if mine_ref.dtype == F32:
-        scalars = mine_ref[:, scalar_at] + got_ref[:, scalar_at]
-    else:
-        scalars = unpack(mine_ref[:, scalar_at]) + unpack(got_ref[:, scalar_at])
+    scalars = unpack(mine_ref[:, scalar_at]) + unpack(got_ref[:, scalar_at])
     return mine_ref[:, :pixels].astype(F32) + got_ref[:, :pixels].astype(F32), scalars
 
 
@@ -218,8 +215,8 @@
     for k in range(1, n_shards):
         edge = k * width
         seams += seam(whole[:, edge - EDGE : edge].astype(F32), whole[:, edge : edge + EDGE].astype(F32))
-    message[:, :pixels] = image
-    message[:, pixels : pixels + LANES] = total + lanes_of({SMOOTH_SQ: seams}, sets)
+    message[:, :pixels] = image.astype(BF16)
+    message[:, pixels : pixels + LANES] = pack(total + lanes_of({SMOOTH_SQ: seams}, sets))
     first, last = whole[:, :EDGE].astype(F32), whole[:, cells - EDGE :].astype(F32)
     store_edges(message, pixels + LANES, first, last, 1, n_par, lax.axis_index("par"))
 
@@ -491,7 +488,7 @@
         beside_them = [] if first else [twice]
 
         def message_of(step):
-            return ((sets, pixels + LANES + edge_columns(step, n_par)), F32 if step == 1 else BF16)
+            return ((sets, pixels + LANES + edge_columns(step, n_par)), BF16)
 
         partial, parts = [], {}
         closing = ([0] + turn)[-1]

time: 139 us -> 139 us (level)
  no operation moved by 1% of the time
where the time goes in v7:
time: 139 us
  starting transfers between devices  54.1 us (39%)
  waiting for transfers between devices  51.2 us (37%)
  Pallas kernels  32.4 us (23%)
    ppermute x33, starting transfers between devices, exchange(): lax.ppermute(block, axis, xor_pairs(count, k))  46.2 us
    pallas_call x58, Pallas kernels, call(): pl.pallas_call(kernel, in_specs=[pl.BlockSpec(memory_space=space)] * len(...  32.4 us
    ppermute x33, waiting for transfers between devices, exchange(): lax.ppermute(block, axis, xor_pairs(count, k))  28.5 us
    ppermute x10, waiting for transfers between devices, on_device(): got = lax.ppermute(message, 'par', xor_pairs(n_par, step))  22.6 us
    ppermute x10, starting transfers between devices, on_device(): got = lax.ppermute(message, 'par', xor_pairs(n_par, step))  7.87 us
  transfers between devices with their start and end apart: 43, of which 38 were waited for; matrix products, arithmetic and copies ran while one was open for 0% of the time, Pallas kernels for 14%

profile of v7, /device:TPU:0, one launch (start us, length us, event | category | flops | bytes accessed | tf_op | source)
XLA Modules:
  0.0 138.7 jit_solution(5835867064580679537)
XLA Ops:
  0.6 4.4 %start_kernel.1 = (bf16[1152,4096]{1,0:T(8,128)(2,1)S(1)}, f32[32,1024]{1,0:T(8,128)S(1)}, bf16[256,128]{1,0:T(8,128)(2,1)S(1)}, bf16[256,128]{1,0:T(8,128)(2,1)...) custom-call(bf16[32,1152]{1,0:T(8,128)(2,1)} %observed_at.1, ...), custom_call_target="tpu_custom_call" | custom-call | flops 301989888 | bytes 19668992 | tf_op jit(solution)/shard_map/start_kernel/pallas_call | solution.py:414
  5.0 4.1 %collective-permute-start = (bf16[256,128]{1,0:T(8,128)(2,1)S(1)}, bf16[256,128]{1,0:T(8,128)(2,1)S(1)}, u32[]{:S(2)}, u32[]{:S(2)}) collective-permute-start(bf16[256,128]{1,0:T(8,128)(2,1)S(1)} %get-tuple-element.147), channel_id=1, source_target_pairs={{0,8},{4,12},{8,0},{12,4},{1,9},{5,13},{9,1},{13,5},{2,10},{6,14},... | collective-permute-start | bytes 196616 | tf_op jit(solution)/shard_map/ppermute | solution.py:427
  13.4 1.9 %collective-permute-done.1.refs_1_ = bf16[256,128]{1,0:T(8,128)(2,1)S(1)} collective-permute-done((bf16[256,128]{1,0:T(8,128)(2,1)S(1)}, bf16[256,128]{1,0:T(8,128)(2,1)S(1)}, u32[]{:S(2)}, u32[]{:S(2)}) %collective-permute-start.1) | collective-permute-done | bytes 65568 | tf_op jit(solution)/shard_map/ppermute | solution.py:427
  15.5 2.7 %collective-permute-start.5 = (bf16[32,1024]{1,0:T(8,128)(2,1)S(1)}, bf16[32,1024]{1,0:T(8,128)(2,1)S(1)}, u32[]{:S(2)}, u32[]{:S(2)}) collective-permute-start(bf16[32,1024]{1,0:T(8,128)(2,1)S(1)} %get-tuple-element.151.refs_0_.refs_3_), channel_id=1, source_target_pairs={{0,8},{4,12},{8,0},{12,4},{1,9},{5,13},{9,1},{13,5},{2,10},{6,14},... | collective-permute-start | bytes 196616 | tf_op jit(solution)/shard_map/ppermute | solution.py:427
  28.9 3.4 %collective-permute-done.7.refs_1_.refs_2_ = bf16[32,1536]{1,0:T(8,128)(2,1)S(1)} collective-permute-done((bf16[32,1536]{1,0:T(8,128)(2,1)S(1)}, bf16[32,1536]{1,0:T(8,128)(2,1)S(1)}, u32[]{:S(2)}, u32[]{:S(2)}) %collective-permute-start.7) | collective-permute-done | bytes 98336 | tf_op jit(solution)/shard_map/ppermute | solution.py:510
  35.8 1.7 %collective-permute-start.10 = (bf16[264,128]{1,0:T(8,128)(2,1)S(1)}, bf16[264,128]{1,0:T(8,128)(2,1)S(1)}, u32[]{:S(2)}, u32[]{:S(2)}) collective-permute-start(bf16[264,128]{1,0:T(8,128)(2,1)S(1)} %get-tuple-element.173), channel_id=1, source_target_pairs={{0,4},{4,0},{8,12},{12,8},{1,5},{5,1},{9,13},{13,9},{2,6},{6,2},{1... | collective-permute-start | bytes 202760 | tf_op jit(solution)/shard_map/ppermute | solution.py:427
  39.3 1.6 %collective-permute-done.9.refs_1_ = bf16[264,128]{1,0:T(8,128)(2,1)S(1)} collective-permute-done((bf16[264,128]{1,0:T(8,128)(2,1)S(1)}, bf16[264,128]{1,0:T(8,128)(2,1)S(1)}, u32[]{:S(2)}, u32[]{:S(2)}) %collective-permute-start.9) | collective-permute-done | bytes 67616 | tf_op jit(solution)/shard_map/ppermute | solution.py:427
  42.7 1.6 %collective-permute-start.12 = (bf16[32,1024]{1,0:T(8,128)(2,1)S(1)}, bf16[32,1024]{1,0:T(8,128)(2,1)S(1)}, u32[]{:S(2)}, u32[]{:S(2)}) collective-permute-start(bf16[32,1024]{1,0:T(8,128)(2,1)S(1)} %get-tuple-element.174.refs_0_.refs_4_), channel_id=1, source_target_pairs={{0,4},{4,0},{8,12},{12,8},{1,5},{5,1},{9,13},{13,9},{2,6},{6,2},{1... | collective-permute-start | bytes 196616 | tf_op jit(solution)/shard_map/ppermute | solution.py:427
  46.2 1.7 %collective-permute-done.13.refs_0_.refs_6_ = bf16[32,1024]{1,0:T(8,128)(2,1)S(1)} collective-permute-done((bf16[32,1024]{1,0:T(8,128)(2,1)S(1)}, bf16[32,1024]{1,0:T(8,128)(2,1)S(1)}, u32[]{:S(2)}, u32[]{:S(2)}) %collective-permute-start.13) | collective-permute-done | bytes 65568 | tf_op jit(solution)/shard_map/ppermute | solution.py:427
  54.3 3.1 %collective-permute-done.15.refs_1_.refs_2_ = bf16[32,1536]{1,0:T(8,128)(2,1)S(1)} collective-permute-done((bf16[32,1536]{1,0:T(8,128)(2,1)S(1)}, bf16[32,1536]{1,0:T(8,128)(2,1)S(1)}, u32[]{:S(2)}, u32[]{:S(2)}) %collective-permute-start.15) | collective-permute-done | bytes 98336 | tf_op jit(solution)/shard_map/ppermute | solution.py:510
  60.9 1.9 %collective-permute-start.18 = (bf16[264,128]{1,0:T(8,128)(2,1)S(1)}, bf16[264,128]{1,0:T(8,128)(2,1)S(1)}, u32[]{:S(2)}, u32[]{:S(2)}) collective-permute-start(bf16[264,128]{1,0:T(8,128)(2,1)S(1)} %get-tuple-element.203), channel_id=1, source_target_pairs={{0,4},{4,0},{8,12},{12,8},{1,5},{5,1},{9,13},{13,9},{2,6},{6,2},{1... | collective-permute-start | bytes 202760 | tf_op jit(solution)/shard_map/ppermute | solution.py:427
  69.2 1.7 %collective-permute-start.19 = (bf16[32,1024]{1,0:T(8,128)(2,1)S(1)}, bf16[32,1024]{1,0:T(8,128)(2,1)S(1)}, u32[]{:S(2)}, u32[]{:S(2)}) collective-permute-start(bf16[32,1024]{1,0:T(8,128)(2,1)S(1)} %get-tuple-element.204.refs_0_.refs_4_), channel_id=1, source_target_pairs={{0,12},{4,8},{8,4},{12,0},{1,13},{5,9},{9,5},{13,1},{2,14},{6,10},... | collective-permute-start | bytes 196616 | tf_op jit(solution)/shard_map/ppermute | solution.py:427
  71.5 1.9 %collective-permute-done.21.refs_0_.refs_6_ = bf16[32,1024]{1,0:T(8,128)(2,1)S(1)} collective-permute-done((bf16[32,1024]{1,0:T(8,128)(2,1)S(1)}, bf16[32,1024]{1,0:T(8,128)(2,1)S(1)}, u32[]{:S(2)}, u32[]{:S(2)}) %collective-permute-start.21) | collective-permute-done | bytes 65568 | tf_op jit(solution)/shard_map/ppermute | solution.py:427
  79.1 3.1 %collective-permute-done.23.refs_1_.refs_2_ = bf16[32,1536]{1,0:T(8,128)(2,1)S(1)} collective-permute-done((bf16[32,1536]{1,0:T(8,128)(2,1)S(1)}, bf16[32,1536]{1,0:T(8,128)(2,1)S(1)}, u32[]{:S(2)}, u32[]{:S(2)}) %collective-permute-start.23) | collective-permute-done | bytes 98336 | tf_op jit(solution)/shard_map/ppermute | solution.py:510
  83.6 1.9 %collective-permute-start.25 = (bf16[264,128]{1,0:T(8,128)(2,1)S(1)}, bf16[264,128]{1,0:T(8,128)(2,1)S(1)}, u32[]{:S(2)}, u32[]{:S(2)}) collective-permute-start(bf16[264,128]{1,0:T(8,128)(2,1)S(1)} %get-tuple-element.233), channel_id=1, source_target_pairs={{0,12},{4,8},{8,4},{12,0},{1,13},{5,9},{9,5},{13,1},{2,14},{6,10},... | collective-permute-start | bytes 202760 | tf_op jit(solution)/shard_map/ppermute | solution.py:427
  86.0 1.7 %collective-permute-start.26 = (bf16[264,128]{1,0:T(8,128)(2,1)S(1)}, bf16[264,128]{1,0:T(8,128)(2,1)S(1)}, u32[]{:S(2)}, u32[]{:S(2)}) collective-permute-start(bf16[264,128]{1,0:T(8,128)(2,1)S(1)} %get-tuple-element.235), channel_id=1, source_target_pairs={{0,4},{4,0},{8,12},{12,8},{1,5},{5,1},{9,13},{13,9},{2,6},{6,2},{1... | collective-permute-start | bytes 202760 | tf_op jit(solution)/shard_map/ppermute | solution.py:427
  93.7 2.0 %collective-permute-start.27 = (bf16[32,1024]{1,0:T(8,128)(2,1)S(1)}, bf16[32,1024]{1,0:T(8,128)(2,1)S(1)}, u32[]{:S(2)}, u32[]{:S(2)}) collective-permute-start(bf16[32,1024]{1,0:T(8,128)(2,1)S(1)} %get-tuple-element.236.refs_0_.refs_4_), channel_id=1, source_target_pairs={{0,12},{4,8},{8,4},{12,0},{1,13},{5,9},{9,5},{13,1},{2,14},{6,10},... | collective-permute-start | bytes 196616 | tf_op jit(solution)/shard_map/ppermute | solution.py:427
  96.2 1.8 %collective-permute-done.29.refs_0_.refs_6_ = bf16[32,1024]{1,0:T(8,128)(2,1)S(1)} collective-permute-done((bf16[32,1024]{1,0:T(8,128)(2,1)S(1)}, bf16[32,1024]{1,0:T(8,128)(2,1)S(1)}, u32[]{:S(2)}, u32[]{:S(2)}) %collective-permute-start.29) | collective-permute-done | bytes 65568 | tf_op jit(solution)/shard_map/ppermute | solution.py:427
  103.7 3.1 %collective-permute-done.31.refs_1_.refs_2_ = bf16[32,1536]{1,0:T(8,128)(2,1)S(1)} collective-permute-done((bf16[32,1536]{1,0:T(8,128)(2,1)S(1)}, bf16[32,1536]{1,0:T(8,128)(2,1)S(1)}, u32[]{:S(2)}, u32[]{:S(2)}) %collective-permute-start.31) | collective-permute-done | bytes 98336 | tf_op jit(solution)/shard_map/ppermute | solution.py:510
  108.1 2.0 %collective-permute-start.33 = (bf16[264,128]{1,0:T(8,128)(2,1)S(1)}, bf16[264,128]{1,0:T(8,128)(2,1)S(1)}, u32[]{:S(2)}, u32[]{:S(2)}) collective-permute-start(bf16[264,128]{1,0:T(8,128)(2,1)S(1)} %block_kernel.14), channel_id=1, source_target_pairs={{0,12},{4,8},{8,4},{12,0},{1,13},{5,9},{9,5},{13,1},{2,14},{6,10},... | collective-permute-start | bytes 202760 | tf_op jit(solution)/shard_map/ppermute | solution.py:427
  118.3 1.9 %collective-permute-start.35 = (bf16[32,1024]{1,0:T(8,128)(2,1)S(1)}, bf16[32,1024]{1,0:T(8,128)(2,1)S(1)}, u32[]{:S(2)}, u32[]{:S(2)}) collective-permute-start(bf16[32,1024]{1,0:T(8,128)(2,1)S(1)} %get-tuple-element.266.refs_0_.refs_4_), channel_id=1, source_target_pairs={{0,12},{4,8},{8,4},{12,0},{1,13},{5,9},{9,5},{13,1},{2,14},{6,10},... | collective-permute-start | bytes 196616 | tf_op jit(solution)/shard_map/ppermute | solution.py:427
  120.7 1.6 %collective-permute-done.37.refs_0_.refs_6_ = bf16[32,1024]{1,0:T(8,128)(2,1)S(1)} collective-permute-done((bf16[32,1024]{1,0:T(8,128)(2,1)S(1)}, bf16[32,1024]{1,0:T(8,128)(2,1)S(1)}, u32[]{:S(2)}, u32[]{:S(2)}) %collective-permute-start.37) | collective-permute-done | bytes 65568 | tf_op jit(solution)/shard_map/ppermute | solution.py:427
  128.0 3.4 %collective-permute-done.39.refs_1_.refs_2_ = bf16[32,1536]{1,0:T(8,128)(2,1)S(1)} collective-permute-done((bf16[32,1536]{1,0:T(8,128)(2,1)S(1)}, bf16[32,1536]{1,0:T(8,128)(2,1)S(1)}, u32[]{:S(2)}, u32[]{:S(2)}) %collective-permute-start.39) | collective-permute-done | bytes 98336 | tf_op jit(solution)/shard_map/ppermute | solution.py:510
  131.8 2.0 %collective-permute-start.41 = (f32[32,128]{1,0:T(8,128)S(1)}, f32[32,128]{1,0:T(8,128)S(1)}, u32[]{:S(2)}, u32[]{:S(2)}) collective-permute-start(f32[32,128]{1,0:T(8,128)S(1)} %get-tuple-element.277.refs_0_), channel_id=1, source_target_pairs={{0,12},{4,8},{8,4},{12,0},{1,13},{5,9},{9,5},{13,1},{2,14},{6,10},... | collective-permute-start | bytes 49160 | tf_op jit(solution)/shard_map/ppermute | solution.py:427
  (124 shorter events, 81.5 us)
Async XLA Ops:
  5.0 8.4 %collective-permute-start = (bf16[256,128]{1,0:T(8,128)(2,1)S(1)}, bf16[256,128]{1,0:T(8,128)(2,1)S(1)}, u32[]{:S(2)}, u32[]{:S(2)}) collective-permute-start(bf16[256,128]{1,0:T(8,128)(2,1)S(1)} %get-tuple-element.147), channel_id=1, source_target_pairs={{0,8},{4,12},{8,0},{12,4},{1,9},{5,13},{9,1},{13,5},{2,10},{6,14},... | collective-permute-start | bytes 196616 | tf_op jit(solution)/shard_map/ppermute | solution.py:427
  9.2 6.2 %collective-permute-start.1 = (bf16[256,128]{1,0:T(8,128)(2,1)S(1)}, bf16[256,128]{1,0:T(8,128)(2,1)S(1)}, u32[]{:S(2)}, u32[]{:S(2)}) collective-permute-start(bf16[256,128]{1,0:T(8,128)(2,1)S(1)} %get-tuple-element.148), channel_id=1, source_target_pairs={{0,12},{4,8},{8,4},{12,0},{1,13},{5,9},{9,5},{13,1},{2,14},{6,10},... | collective-permute-start | bytes 196616 | tf_op jit(solution)/shard_map/ppermute | solution.py:427
  15.5 6.2 %collective-permute-start.5 = (bf16[32,1024]{1,0:T(8,128)(2,1)S(1)}, bf16[32,1024]{1,0:T(8,128)(2,1)S(1)}, u32[]{:S(2)}, u32[]{:S(2)}) collective-permute-start(bf16[32,1024]{1,0:T(8,128)(2,1)S(1)} %get-tuple-element.151.refs_0_.refs_3_), channel_id=1, source_target_pairs={{0,8},{4,12},{8,0},{12,4},{1,9},{5,13},{9,1},{13,5},{2,10},{6,14},... | collective-permute-start | bytes 196616 | tf_op jit(solution)/shard_map/ppermute | solution.py:427
  19.1 6.1 %collective-permute-start.3 = (bf16[32,1024]{1,0:T(8,128)(2,1)S(1)}, bf16[32,1024]{1,0:T(8,128)(2,1)S(1)}, u32[]{:S(2)}, u32[]{:S(2)}) collective-permute-start(bf16[32,1024]{1,0:T(8,128)(2,1)S(1)} %get-tuple-element.151.refs_0_.refs_3_), channel_id=1, source_target_pairs={{0,12},{4,8},{8,4},{12,0},{1,13},{5,9},{9,5},{13,1},{2,14},{6,10},... | collective-permute-start | bytes 196616 | tf_op jit(solution)/shard_map/ppermute | solution.py:427
  32.8 6.5 %collective-permute-start.8 = (bf16[264,128]{1,0:T(8,128)(2,1)S(1)}, bf16[264,128]{1,0:T(8,128)(2,1)S(1)}, u32[]{:S(2)}, u32[]{:S(2)}) collective-permute-start(bf16[264,128]{1,0:T(8,128)(2,1)S(1)} %get-tuple-element.169), channel_id=1, source_target_pairs={{0,8},{4,12},{8,0},{12,4},{1,9},{5,13},{9,1},{13,5},{2,10},{6,14},... | collective-permute-start | bytes 202760 | tf_op jit(solution)/shard_map/ppermute | solution.py:427
  34.6 6.3 %collective-permute-start.9 = (bf16[264,128]{1,0:T(8,128)(2,1)S(1)}, bf16[264,128]{1,0:T(8,128)(2,1)S(1)}, u32[]{:S(2)}, u32[]{:S(2)}) collective-permute-start(bf16[264,128]{1,0:T(8,128)(2,1)S(1)} %get-tuple-element.171), channel_id=1, source_target_pairs={{0,12},{4,8},{8,4},{12,0},{1,13},{5,9},{9,5},{13,1},{2,14},{6,10},... | collective-permute-start | bytes 202760 | tf_op jit(solution)/shard_map/ppermute | solution.py:427
  41.3 6.6 %collective-permute-start.13 = (bf16[32,1024]{1,0:T(8,128)(2,1)S(1)}, bf16[32,1024]{1,0:T(8,128)(2,1)S(1)}, u32[]{:S(2)}, u32[]{:S(2)}) collective-permute-start(bf16[32,1024]{1,0:T(8,128)(2,1)S(1)} %get-tuple-element.174.refs_0_.refs_4_), channel_id=1, source_target_pairs={{0,8},{4,12},{8,0},{12,4},{1,9},{5,13},{9,1},{13,5},{2,10},{6,14},... | collective-permute-start | bytes 196616 | tf_op jit(solution)/shard_map/ppermute | solution.py:427
  42.7 5.8 %collective-permute-start.12 = (bf16[32,1024]{1,0:T(8,128)(2,1)S(1)}, bf16[32,1024]{1,0:T(8,128)(2,1)S(1)}, u32[]{:S(2)}, u32[]{:S(2)}) collective-permute-start(bf16[32,1024]{1,0:T(8,128)(2,1)S(1)} %get-tuple-element.174.refs_0_.refs_4_), channel_id=1, source_target_pairs={{0,4},{4,0},{8,12},{12,8},{1,5},{5,1},{9,13},{13,9},{2,6},{6,2},{1... | collective-permute-start | bytes 196616 | tf_op jit(solution)/shard_map/ppermute | solution.py:427
  44.3 6.1 %collective-permute-start.11 = (bf16[32,1024]{1,0:T(8,128)(2,1)S(1)}, bf16[32,1024]{1,0:T(8,128)(2,1)S(1)}, u32[]{:S(2)}, u32[]{:S(2)}) collective-permute-start(bf16[32,1024]{1,0:T(8,128)(2,1)S(1)} %get-tuple-element.174.refs_0_.refs_4_), channel_id=1, source_target_pairs={{0,12},{4,8},{8,4},{12,0},{1,13},{5,9},{9,5},{13,1},{2,14},{6,10},... | collective-permute-start | bytes 196616 | tf_op jit(solution)/shard_map/ppermute | solution.py:427
  58.0 6.5 %collective-permute-start.16 = (bf16[264,128]{1,0:T(8,128)(2,1)S(1)}, bf16[264,128]{1,0:T(8,128)(2,1)S(1)}, u32[]{:S(2)}, u32[]{:S(2)}) collective-permute-start(bf16[264,128]{1,0:T(8,128)(2,1)S(1)} %get-tuple-element.199), channel_id=1, source_target_pairs={{0,8},{4,12},{8,0},{12,4},{1,9},{5,13},{9,1},{13,5},{2,10},{6,14},... | collective-permute-start | bytes 202760 | tf_op jit(solution)/shard_map/ppermute | solution.py:427
  59.5 6.3 %collective-permute-start.17 = (bf16[264,128]{1,0:T(8,128)(2,1)S(1)}, bf16[264,128]{1,0:T(8,128)(2,1)S(1)}, u32[]{:S(2)}, u32[]{:S(2)}) collective-permute-start(bf16[264,128]{1,0:T(8,128)(2,1)S(1)} %get-tuple-element.201), channel_id=1, source_target_pairs={{0,12},{4,8},{8,4},{12,0},{1,13},{5,9},{9,5},{13,1},{2,14},{6,10},... | collective-permute-start | bytes 202760 | tf_op jit(solution)/shard_map/ppermute | solution.py:427
  66.4 7.1 %collective-permute-start.21 = (bf16[32,1024]{1,0:T(8,128)(2,1)S(1)}, bf16[32,1024]{1,0:T(8,128)(2,1)S(1)}, u32[]{:S(2)}, u32[]{:S(2)}) collective-permute-start(bf16[32,1024]{1,0:T(8,128)(2,1)S(1)} %get-tuple-element.204.refs_0_.refs_4_), channel_id=1, source_target_pairs={{0,8},{4,12},{8,0},{12,4},{1,9},{5,13},{9,1},{13,5},{2,10},{6,14},... | collective-permute-start | bytes 196616 | tf_op jit(solution)/shard_map/ppermute | solution.py:427
  67.8 6.2 %collective-permute-start.20 = (bf16[32,1024]{1,0:T(8,128)(2,1)S(1)}, bf16[32,1024]{1,0:T(8,128)(2,1)S(1)}, u32[]{:S(2)}, u32[]{:S(2)}) collective-permute-start(bf16[32,1024]{1,0:T(8,128)(2,1)S(1)} %get-tuple-element.204.refs_0_.refs_4_), channel_id=1, source_target_pairs={{0,4},{4,0},{8,12},{12,8},{1,5},{5,1},{9,13},{13,9},{2,6},{6,2},{1... | collective-permute-start | bytes 196616 | tf_op jit(solution)/shard_map/ppermute | solution.py:427
  69.2 6.1 %collective-permute-start.19 = (bf16[32,1024]{1,0:T(8,128)(2,1)S(1)}, bf16[32,1024]{1,0:T(8,128)(2,1)S(1)}, u32[]{:S(2)}, u32[]{:S(2)}) collective-permute-start(bf16[32,1024]{1,0:T(8,128)(2,1)S(1)} %get-tuple-element.204.refs_0_.refs_4_), channel_id=1, source_target_pairs={{0,12},{4,8},{8,4},{12,0},{1,13},{5,9},{9,5},{13,1},{2,14},{6,10},... | collective-permute-start | bytes 196616 | tf_op jit(solution)/shard_map/ppermute | solution.py:427
  82.9 6.9 %collective-permute-start.24 = (bf16[264,128]{1,0:T(8,128)(2,1)S(1)}, bf16[264,128]{1,0:T(8,128)(2,1)S(1)}, u32[]{:S(2)}, u32[]{:S(2)}) collective-permute-start(bf16[264,128]{1,0:T(8,128)(2,1)S(1)} %get-tuple-element.231), channel_id=1, source_target_pairs={{0,8},{4,12},{8,0},{12,4},{1,9},{5,13},{9,1},{13,5},{2,10},{6,14},... | collective-permute-start | bytes 202760 | tf_op jit(solution)/shard_map/ppermute | solution.py:427
  83.6 6.6 %collective-permute-start.25 = (bf16[264,128]{1,0:T(8,128)(2,1)S(1)}, bf16[264,128]{1,0:T(8,128)(2,1)S(1)}, u32[]{:S(2)}, u32[]{:S(2)}) collective-permute-start(bf16[264,128]{1,0:T(8,128)(2,1)S(1)} %get-tuple-element.233), channel_id=1, source_target_pairs={{0,12},{4,8},{8,4},{12,0},{1,13},{5,9},{9,5},{13,1},{2,14},{6,10},... | collective-permute-start | bytes 202760 | tf_op jit(solution)/shard_map/ppermute | solution.py:427
  91.2 6.8 %collective-permute-start.29 = (bf16[32,1024]{1,0:T(8,128)(2,1)S(1)}, bf16[32,1024]{1,0:T(8,128)(2,1)S(1)}, u32[]{:S(2)}, u32[]{:S(2)}) collective-permute-start(bf16[32,1024]{1,0:T(8,128)(2,1)S(1)} %get-tuple-element.236.refs_0_.refs_4_), channel_id=1, source_target_pairs={{0,8},{4,12},{8,0},{12,4},{1,9},{5,13},{9,1},{13,5},{2,10},{6,14},... | collective-permute-start | bytes 196616 | tf_op jit(solution)/shard_map/ppermute | solution.py:427
  92.5 6.0 %collective-permute-start.28 = (bf16[32,1024]{1,0:T(8,128)(2,1)S(1)}, bf16[32,1024]{1,0:T(8,128)(2,1)S(1)}, u32[]{:S(2)}, u32[]{:S(2)}) collective-permute-start(bf16[32,1024]{1,0:T(8,128)(2,1)S(1)} %get-tuple-element.236.refs_0_.refs_4_), channel_id=1, source_target_pairs={{0,4},{4,0},{8,12},{12,8},{1,5},{5,1},{9,13},{13,9},{2,6},{6,2},{1... | collective-permute-start | bytes 196616 | tf_op jit(solution)/shard_map/ppermute | solution.py:427
  93.7 6.1 %collective-permute-start.27 = (bf16[32,1024]{1,0:T(8,128)(2,1)S(1)}, bf16[32,1024]{1,0:T(8,128)(2,1)S(1)}, u32[]{:S(2)}, u32[]{:S(2)}) collective-permute-start(bf16[32,1024]{1,0:T(8,128)(2,1)S(1)} %get-tuple-element.236.refs_0_.refs_4_), channel_id=1, source_target_pairs={{0,12},{4,8},{8,4},{12,0},{1,13},{5,9},{9,5},{13,1},{2,14},{6,10},... | collective-permute-start | bytes 196616 | tf_op jit(solution)/shard_map/ppermute | solution.py:427
  107.5 7.0 %collective-permute-start.32 = (bf16[264,128]{1,0:T(8,128)(2,1)S(1)}, bf16[264,128]{1,0:T(8,128)(2,1)S(1)}, u32[]{:S(2)}, u32[]{:S(2)}) collective-permute-start(bf16[264,128]{1,0:T(8,128)(2,1)S(1)} %get-tuple-element.263), channel_id=1, source_target_pairs={{0,8},{4,12},{8,0},{12,4},{1,9},{5,13},{9,1},{13,5},{2,10},{6,14},... | collective-permute-start | bytes 202760 | tf_op jit(solution)/shard_map/ppermute | solution.py:427
  108.1 6.9 %collective-permute-start.33 = (bf16[264,128]{1,0:T(8,128)(2,1)S(1)}, bf16[264,128]{1,0:T(8,128)(2,1)S(1)}, u32[]{:S(2)}, u32[]{:S(2)}) collective-permute-start(bf16[264,128]{1,0:T(8,128)(2,1)S(1)} %block_kernel.14), channel_id=1, source_target_pairs={{0,12},{4,8},{8,4},{12,0},{1,13},{5,9},{9,5},{13,1},{2,14},{6,10},... | collective-permute-start | bytes 202760 | tf_op jit(solution)/shard_map/ppermute | solution.py:427
  115.7 6.6 %collective-permute-start.37 = (bf16[32,1024]{1,0:T(8,128)(2,1)S(1)}, bf16[32,1024]{1,0:T(8,128)(2,1)S(1)}, u32[]{:S(2)}, u32[]{:S(2)}) collective-permute-start(bf16[32,1024]{1,0:T(8,128)(2,1)S(1)} %get-tuple-element.266.refs_0_.refs_4_), channel_id=1, source_target_pairs={{0,8},{4,12},{8,0},{12,4},{1,9},{5,13},{9,1},{13,5},{2,10},{6,14},... | collective-permute-start | bytes 196616 | tf_op jit(solution)/shard_map/ppermute | solution.py:427
  118.3 6.1 %collective-permute-start.35 = (bf16[32,1024]{1,0:T(8,128)(2,1)S(1)}, bf16[32,1024]{1,0:T(8,128)(2,1)S(1)}, u32[]{:S(2)}, u32[]{:S(2)}) collective-permute-start(bf16[32,1024]{1,0:T(8,128)(2,1)S(1)} %get-tuple-element.266.refs_0_.refs_4_), channel_id=1, source_target_pairs={{0,12},{4,8},{8,4},{12,0},{1,13},{5,9},{9,5},{13,1},{2,14},{6,10},... | collective-permute-start | bytes 196616 | tf_op jit(solution)/shard_map/ppermute | solution.py:427
  131.8 5.6 %collective-permute-start.41 = (f32[32,128]{1,0:T(8,128)S(1)}, f32[32,128]{1,0:T(8,128)S(1)}, u32[]{:S(2)}, u32[]{:S(2)}) collective-permute-start(f32[32,128]{1,0:T(8,128)S(1)} %get-tuple-element.277.refs_0_), channel_id=1, source_target_pairs={{0,12},{4,8},{8,4},{12,0},{1,13},{5,9},{9,5},{13,1},{2,14},{6,10},... | collective-permute-start | bytes 49160 | tf_op jit(solution)/shard_map/ppermute | solution.py:427
  (20 other events, 80.6 us)
